TPU v7x, 32 devices: a whole 2x2x4 slice. The times are simulated.
32 devices in a mesh: lon: 8 (over y, x, core), lev: 4 (over z).
Axes of the slice: x: 2, y: 2, z: 4, core: 2. Of those that a mesh axis runs over, the one named last changes fastest.
Arguments:
- field: float32 [72, 128, 128], P('lev', 'lon'), may hold values from -6 to 6
- ens: bfloat16 [80, 72, 128, 128], P(None, 'lev', 'lon'), may hold values from -2 to 2
- sdev: float32 [72, 128, 128], P('lev', 'lon'), may hold values from 0.5 to 2
- lon_taper: bfloat16 [17], replicated, may hold values from 0 to 0.079589844
- static_taper: bfloat16 [17], replicated, may hold values from 0 to 0.079589844
- loc_vert: bfloat16 [72, 72], P('lev'), may hold values from -0.75 to 0.75
- static_vert: bfloat16 [72, 72], P('lev'), may hold values from -0.75 to 0.75
- obs_block: int32 [8192], P('lon'), may hold values from -1 to 127, as said below
- obs_value: float32 [8192], P('lon'), may hold values from -6 to 6
- obs_rinv: float32 [8192], P('lon'), may hold values from 0.25 to 4
- obs_horiz: float32 [8192, 128], P('lon'), may hold values from -0.5 to 0.5
- obs_vert: float32 [8192, 72], P('lon', 'lev'), may hold values from -0.75 to 0.75
Outputs:
- increment: float32 [72, 128, 128], P('lev', 'lon')
- adjoint_field: float32 [72, 128, 128], P('lev', 'lon')
- obs_cost: float32 [], replicated
Inputs may be any that keep to these rules, and one draw needn't show every extreme that they name: `obs_block`: each longitude sector's 1024 slots name only blocks within that sector's longitudes; live slots come first, in non-falling block order; at least half of a sector's slots are live, and some sector has all its slots live.
All inputs are finite; a program needn't handle non-finite values.
Results may differ from a plain program's by a relative error of at most 0.0041.
Values may be sent and summed in bfloat16 or wider, within the bound.
No kernel may reach another device: no remote copies, remote signals or barrier semaphores. Data moves between devices by JAX's collectives and lax.ppermute only.
A program may use at most 128 MiB of HBM per device.

v0:
```python
import jax
import jax.numpy as jnp
from jax import lax
from jax.sharding import PartitionSpec as P

ens_weight = 0.8
static_weight = 0.5


def padded(block, sides, width):
    for axis, dim in sides:
        count = lax.axis_size(axis)
        forward = [(i, i + 1) for i in range(count - 1)]
        forward.append((count - 1, 0))
        backward = [(target, source) for source, target in forward]
        low = lax.ppermute(
            lax.slice_in_dim(block, block.shape[dim] - width, None, axis=dim), axis, forward
        )
        high = lax.ppermute(lax.slice_in_dim(block, 0, width, axis=dim), axis, backward)
        block = jnp.concatenate([low, block, high], axis=dim)
    return block


def band_matrix(taper, columns):
    width = taper.shape[0]
    extended = columns + width - 1
    offsets = jnp.arange(extended)[:, None] - jnp.arange(columns)[None, :]
    onehot = (offsets[:, :, None] == jnp.arange(width)[None, None, :]).astype(jnp.float32)
    return jnp.einsum("eid,d->ei", onehot, taper.astype(jnp.float32)).astype(jnp.bfloat16)


def body(
    field,
    ens,
    sdev,
    lon_taper,
    static_taper,
    loc_vert,
    static_vert,
    obs_block,
    obs_value,
    obs_rinv,
    obs_horiz,
    obs_vert,
):
    members, lev_rows, lon_cols, lat_rows = ens.shape
    half = lon_taper.shape[0] // 2
    zpert = (ens.astype(jnp.float32) * field[None]).astype(jnp.bfloat16)
    spart = (sdev * field).astype(jnp.bfloat16)[None]
    zwide, swide = (padded(zpert, (("lon", 2),), half), padded(spart, (("lon", 2),), half))
    zsmooth = jnp.einsum(
        "klea,ei->klia", zwide, band_matrix(lon_taper, lon_cols), preferred_element_type=jnp.float32
    ).astype(jnp.bfloat16)
    ssmooth = jnp.einsum(
        "klea,ei->klia",
        swide,
        band_matrix(static_taper, lon_cols),
        preferred_element_type=jnp.float32,
    ).astype(jnp.bfloat16)
    full_loc, full_static = (
        lax.all_gather(loc_vert, "lev", axis=0, tiled=True),
        lax.all_gather(static_vert, "lev", axis=0, tiled=True),
    )
    zcols, scols, ecols = (
        lax.all_to_all(zsmooth, "lev", split_axis=2, concat_axis=1, tiled=True),
        lax.all_to_all(ssmooth, "lev", split_axis=2, concat_axis=1, tiled=True),
        lax.all_to_all(ens, "lev", split_axis=2, concat_axis=1, tiled=True),
    )
    zvert = jnp.einsum("lm,kmia->klia", full_loc, zcols, preferred_element_type=jnp.float32)
    ens_cols = jnp.sum(ecols.astype(jnp.float32) * zvert, axis=0)[None]
    static_cols = jnp.einsum(
        "lm,kmia->klia", full_static, scols, preferred_element_type=jnp.float32
    )
    ens_back, static_back = (
        lax.all_to_all(ens_cols, "lev", split_axis=1, concat_axis=2, tiled=True),
        lax.all_to_all(static_cols, "lev", split_axis=1, concat_axis=2, tiled=True),
    )
    ens_sum = ens_back[0]
    static_sum = static_back[0]
    increment = ens_weight * ens_sum + static_weight * sdev * static_sum
    block_lon = lon_cols // 8
    block_lat = lat_rows // 16
    nblk = block_lon * block_lat
    slots = obs_block.shape[0]
    blocks = (
        increment.reshape(lev_rows, block_lon, 8, block_lat, 16)
        .transpose(0, 1, 3, 2, 4)
        .reshape(lev_rows * nblk, 128)
    )
    live = obs_block >= 0
    local_ids = obs_block - lax.axis_index("lon") * nblk
    safe = jnp.where(live, local_ids, 0)
    selector = ((jnp.arange(nblk)[:, None] == safe[None, :]) & live[None, :]).astype(jnp.float32)
    vert_rows = obs_vert.T
    projected = jnp.dot(blocks, obs_horiz.T, precision=lax.Precision.HIGHEST).reshape(
        lev_rows, nblk, slots
    )
    picked = jnp.sum(projected * selector[None], axis=1)
    partial_value = jnp.sum(picked * vert_rows, axis=0)
    hx = lax.psum(partial_value, "lev")
    miss = hx - obs_value
    dep = jnp.where(live, obs_rinv * miss, 0.0)
    obs_cost = lax.psum(0.5 * jnp.sum(dep * miss), "lon")
    weights = vert_rows * dep[None, :]
    spread = (weights[:, None, :] * selector[None]).reshape(lev_rows * nblk, slots)
    adj_blocks = jnp.dot(spread, obs_horiz, precision=lax.Precision.HIGHEST)
    adjoint_field = (
        adj_blocks.reshape(lev_rows, block_lon, block_lat, 8, 16)
        .transpose(0, 1, 3, 2, 4)
        .reshape(lev_rows, lon_cols, lat_rows)
    )
    return (increment, adjoint_field, obs_cost)


def solution(mesh):
    return jax.shard_map(
        body,
        mesh=mesh,
        in_specs=(
            P("lev", "lon", None),
            P(None, "lev", "lon", None),
            P("lev", "lon", None),
            P(),
            P(),
            P("lev", None),
            P("lev", None),
            P("lon"),
            P("lon"),
            P("lon"),
            P("lon", None),
            P("lon", "lev"),
        ),
        out_specs=(P("lev", "lon", None), P("lev", "lon", None), P()),
        check_vma=False,
    )
```

profile of v0, /device:TPU:0, one launch (start us, length us, event | category | flops | bytes accessed | tf_op | source)
XLA Modules:
  0.0 396.7 jit_solution(12835550179646047944)
XLA Ops:
  2.2 2.9 collective-permute-start.3
  7.6 5.6 %all-to-all-start.3 = ((bf16[1,18,16,128]{3,1,0,2:T(8,128)(2,1)}), bf16[1,18,16,128]{3,1,0,2:T(8,128)(2,1)S(1)}, u32[]{:S(2)}, u32[]{:S(2)}) async-start(bf16[1,18,16,128]{3,1,0,2:T(8,128)(2,1)} %copy.83), calls=%async_computation.3 | async-start | bytes 196608 | tf_op jit(solution)/shard_map/all_to_all | solution.py:66
  13.2 7.5 %copy.73 = bf16[80,18,16,128]{3,0,1,2:T(8,128)(2,1)} copy(bf16[80,18,16,128]{3,2,1,0:T(8,128)(2,1)} %param.13) | data formatting | bytes 11796480 | tf_op args[1]
  20.7 5.3 %all-to-all-start = ((bf16[80,18,16,128]{3,0,1,2:T(8,128)(2,1)}), bf16[80,18,16,128]{3,0,1,2:T(8,128)(2,1)}, u32[]{:S(2)}, u32[]{:S(2)}) async-start(bf16[80,18,16,128]{3,0,1,2:T(8,128)(2,1)} %copy.73), calls=%async_computation | async-start | bytes 11796480 | tf_op jit(solution)/shard_map/all_to_all | solution.py:67
  26.0 3.8 multiply_convert_fusion
  29.8 3.1 fusion.42
  36.4 63.5 %collective-permute-done = bf16[80,18,8,128]{3,2,1,0:T(8,128)(2,1)} collective-permute-done((bf16[80,18,8,128]{3,2,1,0:T(8,128)(2,1)}, bf16[80,18,8,128]{3,2,1,0:T(8,128)(2,1)}, u32[]{:S(2)}, u32[]{:S(2)}) %collective-permute-start) | collective-permute-done | bytes 2949152 | tf_op jit(solution)/shard_map/ppermute | solution.py:16
  99.8 5.4 %convert_bitcast_fusion.1 = bf16[80,18,16,128]{3,2,1,0:T(8,128)(2,1)S(1)} fusion(bf16[80,18,8,128]{3,2,1,0:T(8,128)(2,1)} %collective-permute-done.1, bf16[80,18,16,128]{3,2,1,0:T(8,128)(2,1)} %copy-done.3, bf16[80,18,8,128]{3,2,1,0:T(8,128)(2,1)} %collective-permute-done, bf16[1,32,16]{1,2,0:T(8,128)(2,1)S(1)} %copy.90), kind=kOutput, calls=%fused_computation.12 | convolution fusion | flops 227082240 | bytes 17695744 | tf_op jit(solution)/shard_map/klea,ei->klia/dot_general | solution.py:51
  105.3 4.8 %copy.76 = bf16[80,18,16,128]{3,0,1,2:T(8,128)(2,1)} copy(bf16[80,18,16,128]{3,2,1,0:T(8,128)(2,1)S(1)} %convert_bitcast_fusion.1) | data formatting | bytes 11796480 | tf_op jit(solution)/shard_map/convert_element_type | solution.py:53
  110.1 46.5 %all-to-all-done = bf16[80,18,16,128]{3,0,1,2:T(8,128)(2,1)} async-done(((bf16[80,18,16,128]{3,0,1,2:T(8,128)(2,1)}), bf16[80,18,16,128]{3,0,1,2:T(8,128)(2,1)}, u32[]{:S(2)}, u32[]{:S(2)}) %all-to-all-start) | async-done | bytes 5898272 | tf_op jit(solution)/shard_map/all_to_all | solution.py:67
  156.6 5.2 %all-to-all-start.1 = ((bf16[80,18,16,128]{3,0,1,2:T(8,128)(2,1)}), bf16[80,18,16,128]{3,0,1,2:T(8,128)(2,1)}, u32[]{:S(2)}, u32[]{:S(2)}) async-start(bf16[80,18,16,128]{3,0,1,2:T(8,128)(2,1)} %copy.76), calls=%async_computation.1 | async-start | bytes 11796480 | tf_op jit(solution)/shard_map/all_to_all | solution.py:65
  161.8 135.0 %all-gather = bf16[4,18,72]{2,1,0:T(8,128)(2,1)S(1)} all-gather(bf16[1,18,72]{2,1,0:T(8,128)(2,1)S(1)} %bitcast.112), channel_id=1, replica_groups=mesh['lon'=8,'lev'=4] {'lev'}, dimensions={0}, use_global_device_ids=true | all-gather | bytes 12960 | tf_op jit(solution)/shard_map/all_gather | solution.py:61
  296.9 13.3 %all-gather.1 = bf16[4,18,72]{2,1,0:T(8,128)(2,1)S(1)} all-gather(bf16[1,18,72]{2,1,0:T(8,128)(2,1)S(1)} %bitcast.113), channel_id=1, replica_groups=mesh['lon'=8,'lev'=4] {'lev'}, dimensions={0}, use_global_device_ids=true | all-gather | bytes 12960 | tf_op jit(solution)/shard_map/all_gather | solution.py:62
  312.2 4.3 %copy.74 = bf16[80,18,16,128]{3,0,2,1:T(8,128)(2,1)S(1)} copy(bf16[80,18,16,128]{3,0,1,2:T(8,128)(2,1)} %all-to-all-done) | data formatting | bytes 11796480 | tf_op jit(solution)/shard_map/all_to_all | solution.py:67
  316.5 6.0 %convert_bitcast_fusion = f32[80,4,18,4,128]{4,0,3,1,2:T(8,128)} fusion(bf16[80,18,4,4,128]{4,0,3,2,1:T(8,128)(2,1)S(1)} %bitcast.102), kind=kLoop, calls=%fused_computation.6 | loop fusion | flops 2949120 | bytes 17694720 | tf_op jit(solution)/shard_map/convert_element_type | solution.py:70
  322.5 10.2 %copy.75 = f32[80,4,18,4,128]{4,0,3,2,1:T(8,128)} copy(f32[80,4,18,4,128]{4,0,3,1,2:T(8,128)} %convert_bitcast_fusion) | data formatting | bytes 23592960 | tf_op jit(solution)/shard_map/convert_element_type | solution.py:70
  332.7 3.9 all-to-all-start.4
  336.5 4.5 %copy.78 = bf16[80,4,18,4,128]{4,0,3,2,1:T(8,128)(2,1)S(1)} copy(bf16[80,4,18,4,128]{4,0,2,3,1:T(8,128)(2,1)} %bitcast.10) | data formatting | bytes 11796480 | tf_op jit(solution)/shard_map/all_to_all | solution.py:65
  342.6 10.5 %fusion.6 = f32[72,4,128]{2,0,1:T(8,128)S(1)} fusion(f32[80,72,4,128]{3,0,2,1:T(8,128)S(1)} %bitcast.100, bf16[80,72,4,128]{3,0,2,1:T(8,128)(2,1)S(1)} %bitcast.101, bf16[72,72,1,1]{1,0,2,3:T(8,128)(2,1)S(1)} %reshape.131), kind=kOutput, calls=%fused_computation.8 | convolution fusion | flops 430534656 | bytes 17852544 | tf_op jit(solution)/shard_map/lm,kmia->klia/dot_general | solution.py:69
  353.8 5.1 %all-to-all-start.2 = ((f32[1,72,4,128]{3,2,0,1:T(4,128)}), f32[1,72,4,128]{3,2,0,1:T(4,128)S(1)}, u32[]{:S(2)}, u32[]{:S(2)}) async-start(f32[1,72,4,128]{3,2,0,1:T(4,128)} %copy.81), calls=%async_computation.2 | async-start | bytes 294912 | tf_op jit(solution)/shard_map/all_to_all | solution.py:75
  359.0 5.9 %all-to-all-done.2 = f32[1,72,4,128]{3,2,0,1:T(4,128)S(1)} async-done(((f32[1,72,4,128]{3,2,0,1:T(4,128)}), f32[1,72,4,128]{3,2,0,1:T(4,128)S(1)}, u32[]{:S(2)}, u32[]{:S(2)}) %all-to-all-start.2) | async-done | bytes 147488 | tf_op jit(solution)/shard_map/all_to_all | solution.py:75
  367.2 10.0 %psum.14 = f32[1024]{0:T(1024)S(1)} all-reduce(f32[1024]{0:T(1024)S(1)} %fusion.28), channel_id=1, replica_groups=mesh['lon'=8,'lev'=4] {'lev'}, use_global_device_ids=true, to_apply=%region_3.4 | all-reduce | flops 1024 | bytes 8192 | tf_op jit(solution)/shard_map/psum | solution.py:100
  378.5 4.9 %convolution_bitcast_fusion = f32[18,2,8,8,16]{4,3,2,1,0:T(8,128)S(1)} fusion(f32[8,16,1024,1,1]{2,1,0,4,3:T(8,128)} %bitcast.109, f32[2,8,1024]{2,1,0:T(8,128)S(1)} %and_convert_fusion, f32[18,1024]{1,0:T(8,128)S(1)} %bitcast_multiply_fusion.1), kind=kOutput, calls=%fused_computation.13 | convolution fusion | flops 453279744 | bytes 811008 | tf_op jit(solution)/shard_map/dot_general | solution.py:106
  384.4 12.3 %psum.15 = f32[]{:T(128)} all-reduce(f32[]{:T(128)S(6)} %mul.109), channel_id=1, replica_groups=mesh['lon'=8,'lev'=4] {'lon'}, use_global_device_ids=true, to_apply=%region_5.6 | all-reduce | flops 1 | bytes 8 | tf_op jit(solution)/shard_map/psum | solution.py:103
  (71 shorter events, 15.8 us)
Async XLA Ops:
  0.6 4.5 %copy-start = (bf16[17]{0:T(256)(128)(2,1)S(1)}, bf16[17]{0:T(256)(128)(2,1)}, u32[]{:S(2)}) copy-start(bf16[17]{0:T(256)(128)(2,1)} %param.16) | copy-start | bytes 106
  1.7 5.1 %collective-permute-start.2 = (bf16[1,18,8,128]{3,2,1,0:T(8,128)(2,1)S(1)}, bf16[1,18,8,128]{3,2,1,0:T(8,128)(2,1)S(1)}, u32[]{:S(2)}, u32[]{:S(2)}) collective-permute-start(bf16[1,18,8,128]{3,2,1,0:T(8,128)(2,1)S(1)} %get-tuple-element.9), channel_id=1, source_target_pairs={{0,4},{4,8},{8,12},{12,16},{16,20},{20,24},{24,28},{28,0},{1,5},{5... | collective-permute-start | bytes 110600 | tf_op jit(solution)/shard_map/ppermute | solution.py:16
  2.2 4.6 %collective-permute-start.3 = (bf16[1,18,8,128]{3,2,1,0:T(8,128)(2,1)S(1)}, bf16[1,18,8,128]{3,2,1,0:T(8,128)(2,1)S(1)}, u32[]{:S(2)}, u32[]{:S(2)}) collective-permute-start(bf16[1,18,8,128]{3,2,1,0:T(8,128)(2,1)S(1)} %get-tuple-element.10), channel_id=1, source_target_pairs={{4,0},{8,4},{12,8},{16,12},{20,16},{24,20},{28,24},{0,28},{5,1},{9... | collective-permute-start | bytes 110600 | tf_op jit(solution)/shard_map/ppermute | solution.py:19
  7.6 13.1 %all-to-all-start.3 = ((bf16[1,18,16,128]{3,1,0,2:T(8,128)(2,1)}), bf16[1,18,16,128]{3,1,0,2:T(8,128)(2,1)S(1)}, u32[]{:S(2)}, u32[]{:S(2)}) async-start(bf16[1,18,16,128]{3,1,0,2:T(8,128)(2,1)} %copy.83), calls=%async_computation.3 | async-start | bytes 196608 | tf_op jit(solution)/shard_map/all_to_all | solution.py:66
  20.7 5.3 %copy-start.7 = (f32[18,16,128]{2,1,0:T(8,128)S(1)}, f32[18,16,128]{2,1,0:T(8,128)}, u32[]{:S(2)}) copy-start(f32[18,16,128]{2,1,0:T(8,128)} %param.12) | copy-start | bytes 442372
  20.7 135.9 %all-to-all-start = ((bf16[80,18,16,128]{3,0,1,2:T(8,128)(2,1)}), bf16[80,18,16,128]{3,0,1,2:T(8,128)(2,1)}, u32[]{:S(2)}, u32[]{:S(2)}) async-start(bf16[80,18,16,128]{3,0,1,2:T(8,128)(2,1)} %copy.73), calls=%async_computation | async-start | bytes 11796480 | tf_op jit(solution)/shard_map/all_to_all | solution.py:67
  29.8 3.4 copy-start.3
  29.8 6.0 %copy-start.14 = (bf16[17]{0:T(256)(128)(2,1)S(1)}, bf16[17]{0:T(256)(128)(2,1)}, u32[]{:S(2)}) copy-start(bf16[17]{0:T(256)(128)(2,1)} %param.15) | copy-start | bytes 106
  33.2 66.7 %collective-permute-start = (bf16[80,18,8,128]{3,2,1,0:T(8,128)(2,1)}, bf16[80,18,8,128]{3,2,1,0:T(8,128)(2,1)}, u32[]{:S(2)}, u32[]{:S(2)}) collective-permute-start(bf16[80,18,8,128]{3,2,1,0:T(8,128)(2,1)} %get-tuple-element.7), channel_id=1, source_target_pairs={{0,4},{4,8},{8,12},{12,16},{16,20},{20,24},{24,28},{28,0},{1,5},{5... | collective-permute-start | bytes 8847368 | tf_op jit(solution)/shard_map/ppermute | solution.py:16
  33.6 66.2 %collective-permute-start.1 = (bf16[80,18,8,128]{3,2,1,0:T(8,128)(2,1)S(1)}, bf16[80,18,8,128]{3,2,1,0:T(8,128)(2,1)}, u32[]{:S(2)}, u32[]{:S(2)}) collective-permute-start(bf16[80,18,8,128]{3,2,1,0:T(8,128)(2,1)S(1)} %get-tuple-element.8), channel_id=1, source_target_pairs={{4,0},{8,4},{12,8},{16,12},{20,16},{24,20},{28,24},{0,28},{5,1},{9... | collective-permute-start | bytes 8847368 | tf_op jit(solution)/shard_map/ppermute | solution.py:19
  110.1 51.7 %copy-start.9 = (bf16[18,72]{1,0:T(8,128)(2,1)S(1)}, bf16[18,72]{1,0:T(8,128)(2,1)}, u32[]{:S(2)}) copy-start(bf16[18,72]{1,0:T(8,128)(2,1)} %param.17) | copy-start | bytes 7780
  110.1 186.8 %copy-start.10 = (bf16[18,72]{1,0:T(8,128)(2,1)S(1)}, bf16[18,72]{1,0:T(8,128)(2,1)}, u32[]{:S(2)}) copy-start(bf16[18,72]{1,0:T(8,128)(2,1)} %param.18) | copy-start | bytes 7780
  110.1 200.2 %copy-start.4 = (f32[1024,128]{1,0:T(8,128)S(1)}, f32[1024,128]{1,0:T(8,128)}, u32[]{:S(2)}) copy-start(f32[1024,128]{1,0:T(8,128)} %param.22) | copy-start | bytes 1572868
  110.1 201.2 %copy-start.11 = (s32[1024]{0:T(1024)S(1)}, s32[1024]{0:T(1024)}, u32[]{:S(2)}) copy-start(s32[1024]{0:T(1024)} %param.19) | copy-start | bytes 12292
  156.6 176.1 %all-to-all-start.1 = ((bf16[80,18,16,128]{3,0,1,2:T(8,128)(2,1)}), bf16[80,18,16,128]{3,0,1,2:T(8,128)(2,1)}, u32[]{:S(2)}, u32[]{:S(2)}) async-start(bf16[80,18,16,128]{3,0,1,2:T(8,128)(2,1)} %copy.76), calls=%async_computation.1 | async-start | bytes 11796480 | tf_op jit(solution)/shard_map/all_to_all | solution.py:65
  332.7 21.2 %all-to-all-start.4 = ((f32[1,72,4,128]{3,2,0,1:T(4,128)}), f32[1,72,4,128]{3,2,0,1:T(4,128)S(1)}, u32[]{:S(2)}, u32[]{:S(2)}) async-start(f32[1,72,4,128]{3,2,0,1:T(4,128)} %copy.86), calls=%async_computation.4 | async-start | bytes 294912 | tf_op jit(solution)/shard_map/all_to_all | solution.py:76
  336.5 6.1 %copy-start.2 = (f32[80,4,18,4,128]{4,0,3,2,1:T(8,128)S(1)}, f32[80,4,18,4,128]{4,0,3,2,1:T(8,128)}, u32[]{:S(2)}) copy-start(f32[80,4,18,4,128]{4,0,3,2,1:T(8,128)} %copy.75) | copy-start | bytes 35389444
  342.6 22.4 %copy-start.5 = (f32[18,16,128]{2,1,0:T(8,128)S(1)}, f32[18,16,128]{2,1,0:T(8,128)}, u32[]{:S(2)}) copy-start(f32[18,16,128]{2,1,0:T(8,128)} %param.14) | copy-start | bytes 442372
  353.1 14.1 %copy-start.8 = (f32[1024,18]{0,1:T(8,128)S(1)}, f32[1024,18]{0,1:T(8,128)}, u32[]{:S(2)}) copy-start(f32[1024,18]{0,1:T(8,128)} %param.23) | copy-start | bytes 221188
  353.1 24.1 %copy-start.12 = (f32[1024]{0:T(1024)S(1)}, f32[1024]{0:T(1024)}, u32[]{:S(2)}) copy-start(f32[1024]{0:T(1024)} %param.21) | copy-start | bytes 12292
  353.1 24.1 %copy-start.13 = (f32[1024]{0:T(1024)S(1)}, f32[1024]{0:T(1024)}, u32[]{:S(2)}) copy-start(f32[1024]{0:T(1024)} %param.20) | copy-start | bytes 12292
  353.8 11.1 %all-to-all-start.2 = ((f32[1,72,4,128]{3,2,0,1:T(4,128)}), f32[1,72,4,128]{3,2,0,1:T(4,128)S(1)}, u32[]{:S(2)}, u32[]{:S(2)}) async-start(f32[1,72,4,128]{3,2,0,1:T(4,128)} %copy.81), calls=%async_computation.2 | async-start | bytes 294912 | tf_op jit(solution)/shard_map/all_to_all | solution.py:75
  365.0 31.7 %copy-start.1 = (bf16[17]{0:T(256)(128)(2,1)S(1)}, bf16[17]{0:T(256)(128)(2,1)}, u32[]{:S(2)}) copy-start(bf16[17]{0:T(256)(128)(2,1)} %param.16) | copy-start | bytes 106
  365.0 31.7 %copy-start.6 = (f32[18,16,128]{2,1,0:T(8,128)}, f32[18,16,128]{2,1,0:T(8,128)S(1)}, u32[]{:S(2)}) copy-start(f32[18,16,128]{2,1,0:T(8,128)S(1)} %multiply_add_fusion) | copy-start | bytes 442372
where the time goes:
time: 398 us; the launch traced here: 397 us
  blocking collectives  171 us (43%)
  waiting for transfers between devices  117 us (29%)
  local copies, waits for them, and re-layouts  41.5 us (10%)
  starting transfers between devices  31.1 us (8%)
  matrix products  23.3 us (6%)
  other arithmetic  11.6 us (3%)
    all_gather x1, blocking collectives, body(): lax.all_gather(loc_vert, 'lev', axis=0, tiled=True)  135 us
    ppermute x2, waiting for transfers between devices, padded(): lax.ppermute(lax.slice_in_dim(block, block.shape[dim] - width, None, axis...  64.5 us
    all_to_all x1, waiting for transfers between devices, body(): lax.all_to_all(ens, 'lev', split_axis=2, concat_axis=1, tiled=True)  46.5 us
    all_gather x1, blocking collectives, body(): lax.all_gather(static_vert, 'lev', axis=0, tiled=True)  13.3 us
    psum x1, blocking collectives, body(): obs_cost = lax.psum(0.5 * jnp.sum(dep * miss), 'lon')  12.3 us
    unnamed x34, local copies, waits for them, and re-layouts  10.5 us
    dot_general x1, matrix products, body(): jnp.einsum('lm,kmia->klia', full_loc, zcols, preferred_element_type=jnp.f...  10.5 us
    convert_element_type x1, local copies, waits for them, and re-layouts, body(): ens_cols = jnp.sum(ecols.astype(jnp.float32) * zvert, axis=0)[None]  10.2 us
  transfers between devices with their start and end apart: 9, of which 5 were waited for; matrix products, arithmetic and copies ran while one was open for 16% of the time, Pallas kernels for 0%

commit v1 on v0

v1 whole, which is shorter than its diff:
```python
import functools

import jax
import jax.numpy as jnp
from jax import lax
from jax.experimental import pallas as pl
from jax.experimental.pallas import tpu as pltpu
from jax.sharding import PartitionSpec as P


ens_weight = 0.8
static_weight = 0.5
block_lon = 8
block_lat = 16
f32 = jnp.float32
bf16 = jnp.bfloat16


def shift_by(axis, amount):
    count = lax.axis_size(axis)
    return [(i, (i + amount) % count) for i in range(count)]


def vmem():
    return pl.BlockSpec(memory_space=pltpu.VMEM)


def anywhere():
    return pl.BlockSpec(memory_space=pl.ANY)


def params(count=0):
    return pltpu.CompilerParams(vmem_limit_bytes=(24 if count <= 2 else 58) * 2**20)


def smem():
    return pl.BlockSpec(memory_space=pltpu.SMEM)


def cost(flops, nbytes):
    return pl.CostEstimate(flops=int(flops), bytes_accessed=int(nbytes), transcendentals=0)


def lane_groups(shape, width):
    return lax.broadcasted_iota(jnp.int32, shape, len(shape) - 1) // width


def regroup(sources, quarter, parts, width):
    group = lane_groups(sources[0].shape, width)
    out = None
    for p, source in enumerate(sources):
        turn = lax.rem(p - quarter + parts, parts) * width
        moved = pltpu.roll(source, turn, source.ndim - 1)
        out = moved if out is None else jnp.where(group == p, moved, out)
    return out


def pack_kernel(parts, halves, me_ref, ens_ref, after, *outs):
    levels, columns, lanes = ens_ref.shape[1:]
    width = lanes // parts
    rows = columns // halves
    me = me_ref[0]
    sources = [ens_ref[p].astype(f32).reshape(levels * columns, lanes) for p in range(parts)]
    for s, out in enumerate(outs):
        packed = regroup(sources, lax.rem(me + s, parts), parts, width)
        packed = packed.reshape(levels, halves, rows, lanes)
        for h in range(halves):
            out[0, h] = packed[:, h].reshape(levels * rows, lanes).astype(bf16)


def pack(me, ens, start, count, parts, halves, after):
    _, levels, columns, lanes = ens.shape
    rows = levels * columns // halves
    shape = jax.ShapeDtypeStruct((count, halves, rows, lanes), bf16)
    return pl.pallas_call(
        functools.partial(pack_kernel, parts, halves),
        grid=(count,),
        in_specs=[
            smem(),
            pl.BlockSpec((parts, levels, columns, lanes), lambda i: (start + i, 0, 0, 0)),
            anywhere(),
        ],
        out_specs=[pl.BlockSpec((1, halves, rows, lanes), lambda i: (i, 0, 0, 0))] * parts,
        out_shape=[shape] * parts,
        cost_estimate=cost(count * 4e6, count * parts * halves * rows * lanes * 4),
        compiler_params=params(8),
        name="pack",
    )(me, ens, after)


def ceil_to(x, unit):
    return -(-x // unit) * unit


def message_rows(levels, half_rows, slots, lanes):
    vert = 2 * half_rows
    loc = vert + ceil_to(levels * slots // lanes, 16)
    stat = loc + ceil_to(levels, 16)
    return 0, half_rows, vert, loc, stat, stat + ceil_to(levels, 16)


def pack_small_kernel(
    parts, halves, first, me_ref, field_ref, sdev_ref, vert_ref, loc_ref, stat_ref, after, *outs
):
    levels, columns, lanes = field_ref.shape
    width = lanes // parts
    rows = columns // halves
    slots = vert_ref.shape[0]
    me = me_ref[0]
    sources = []
    for h in range(halves):
        for ref in (field_ref, sdev_ref):
            sources.append(ref[:, h * rows : (h + 1) * rows, :].reshape(levels * rows, lanes))
    flat = vert_ref[...].T
    flat = jnp.concatenate(
        [flat[:, t : t + lanes] for t in range(0, slots, lanes)], axis=0
    ).astype(bf16)
    for s, out in enumerate(outs):
        high, low = split(regroup(sources, lax.rem(me + s, parts), parts, width))
        out[first[0] : first[1], :] = high
        out[first[1] : first[2], :] = low
        out[first[2] : first[2] + flat.shape[0], :] = flat
        for begin, ref in ((first[3], loc_ref), (first[4], stat_ref)):
            out[begin : begin + ceil_to(levels, 16), :] = jnp.zeros(
                (ceil_to(levels, 16), lanes), bf16
            )
            out[begin : begin + levels, : ref.shape[1]] = ref[...]


def pack_small(me, field, sdev, vert, loc, stat, parts, halves, after):
    levels, columns, lanes = field.shape
    first = message_rows(levels, levels * columns // halves, vert.shape[0], lanes)
    return pl.pallas_call(
        functools.partial(pack_small_kernel, parts, halves, first),
        in_specs=[smem()] + [vmem()] * 5 + [anywhere()],
        out_specs=[vmem()] * parts,
        out_shape=[jax.ShapeDtypeStruct((first[-1], lanes), bf16)] * parts,
        compiler_params=params(),
        name="pack_small",
    )(me, field, sdev, vert, loc, stat, after)


def spread_kernel(parts, halves, levels, first, after, *refs):
    messages, (wide_field, wide_sdev, left_end, right_end, vert, loc, stat) = (
        refs[:parts],
        refs[parts:],
    )
    rows = wide_field.shape[1] // parts
    lanes = messages[0].shape[1]
    width = lanes // parts
    group = lane_groups((rows, lanes), width)
    ends = (left_end, right_end)
    for s, message in enumerate(messages):
        x = message[:rows, :].astype(f32) + message[rows : 2 * rows, :].astype(f32)
        for h in range(halves):
            wide = []
            for t in range(2):
                one = jnp.where(group == 2 * h + t, x, 0.0)
                both = one
                for k in range(1, parts):
                    both = both + pltpu.roll(one, k * width, 1)
                wide.append(both)
            wide_field[h, s * rows : (s + 1) * rows, :] = wide[0]
            wide_sdev[h, s * rows : (s + 1) * rows, :] = wide[1]
            ends[h][0, s * rows : (s + 1) * rows, :] = (wide[0] * wide[1]).astype(bf16)
        here = slice(s * levels, (s + 1) * levels)
        count = vert.shape[1] // lanes
        x = message[first[2] : first[2] + count * levels, :].astype(f32)
        for t in range(count):
            vert[here, t * lanes : (t + 1) * lanes] = x[t * levels : (t + 1) * levels]
    for begin, out in ((first[3], loc), (first[4], stat)):
        out[...] = jnp.concatenate(
            [m[begin : begin + ceil_to(levels, 16), :].astype(f32)[:levels] for m in messages],
            axis=0,
        ).astype(bf16)


def spread(messages, levels, rows, slots, parts, halves, after):
    lanes = messages[0].shape[1]
    first = message_rows(levels, rows, slots, lanes)
    wide = jax.ShapeDtypeStruct((halves, parts * rows, lanes), f32)
    end = jax.ShapeDtypeStruct((1, parts * rows, lanes), bf16)
    matrix = jax.ShapeDtypeStruct((parts * levels, lanes), bf16)
    vert = jax.ShapeDtypeStruct((parts * levels, slots), f32)
    return pl.pallas_call(
        functools.partial(spread_kernel, parts, halves, levels, first),
        in_specs=[anywhere()] + [vmem()] * parts,
        out_specs=[vmem()] * 7,
        out_shape=[wide, wide, end, end, vert, matrix, matrix],
        compiler_params=params(),
        name="spread",
    )(after, *messages)


def product_kernel(parts, field_ref, after, *refs):
    xs, ends = refs[:parts], refs[parts:]
    count, _, rows, _ = xs[0].shape
    for s, x in enumerate(xs):
        here = slice(s * rows, (s + 1) * rows)
        for h, end in enumerate(ends):
            scale = field_ref[h, here, :]
            for k in range(count):
                end[k, here, :] = (x[k, h].astype(f32) * scale).astype(bf16)


def product(wide_field, xs, after):
    parts = len(xs)
    count, halves, rows, lanes = xs[0].shape
    step = 2 if count % 2 == 0 else 1
    end = jax.ShapeDtypeStruct((count, parts * rows, lanes), bf16)
    return pl.pallas_call(
        functools.partial(product_kernel, parts),
        grid=(count // step,),
        in_specs=[pl.BlockSpec(wide_field.shape, lambda i: (0, 0, 0)), anywhere()]
        + [pl.BlockSpec((step, halves, rows, lanes), lambda i: (i, 0, 0, 0))] * parts,
        out_specs=[pl.BlockSpec((step, parts * rows, lanes), lambda i: (i, 0, 0))] * halves,
        out_shape=[end] * halves,
        cost_estimate=cost(count * 1e6, count * halves * parts * rows * lanes * 4),
        compiler_params=params(count),
        name="product",
    )(wide_field, after, *xs)


def filter_kernel(pair, has_total, matrix_ref, left, first, last, right, *refs):
    refs = list(refs)
    stack = refs.pop()
    total_out = refs.pop()
    total_in = refs.pop() if has_total else None
    xs = refs
    rows, lanes = first.shape[1:]

    @pl.when(pl.program_id(0) == 0)
    def _():
        if has_total:
            total_out[...] = total_in[...]
        else:
            total_out[...] = jnp.zeros_like(total_out)

    for n, ref in enumerate((left, first, last, right)):
        for k in range(pair):
            stack[n * rows : (n + 1) * rows, k * lanes : (k + 1) * lanes] = ref[k]
    for h in range(total_out.shape[0]):
        y = jnp.dot(
            matrix_ref[...], stack[h * rows : (h + 3) * rows, :], preferred_element_type=f32
        )
        piece = rows // len(xs)
        for s, x in enumerate(xs):
            here = slice(s * piece, (s + 1) * piece)
            add = total_out[h, here, :]
            for k in range(pair):
                add = add + x[k, h].astype(f32) * y[here, k * lanes : (k + 1) * lanes]
            total_out[h, here, :] = add


def filtered(matrix, left, first, last, right, xs, total):
    count, rows, lanes = first.shape
    pair = 2 if count % 2 == 0 else 1
    halves = 2
    piece = rows // len(xs)
    edge = pl.BlockSpec((pair, rows, lanes), lambda i: (i, 0, 0))
    whole = pl.BlockSpec((halves, rows, lanes), lambda i: (0, 0, 0))
    return pl.pallas_call(
        functools.partial(filter_kernel, pair, total is not None),
        grid=(count // pair,),
        in_specs=[pl.BlockSpec(matrix.shape, lambda i: (0, 0))]
        + [edge] * 4
        + [pl.BlockSpec((pair, halves, piece, lanes), lambda i: (i, 0, 0, 0))] * len(xs)
        + ([whole] if total is not None else []),
        out_specs=whole,
        out_shape=jax.ShapeDtypeStruct((halves, rows, lanes), f32),
        scratch_shapes=[pltpu.VMEM((4 * rows, pair * lanes), bf16)],
        cost_estimate=cost(
            2 * halves * matrix.shape[0] * matrix.shape[1] * lanes * count,
            count * rows * lanes * 12,
        ),
        compiler_params=params(count),
        name="filtered",
    )(matrix, left, first, last, right, *xs, *([total] if total is not None else []))


def fold_kernel(parts, block_rows, total_ref, static_ref, blocks_ref, mixed):
    halves, rows, lanes = total_ref.shape
    width = lanes // parts
    levels = rows // block_lon
    for h in range(halves):
        x = ens_weight * total_ref[h] + (static_weight / parts) * static_ref[h]
        folded = x
        for k in range(1, parts):
            folded = folded + pltpu.roll(x, k * width, 1)
        mixed[h * rows : (h + 1) * rows, :] = folded
    group = lane_groups((levels, lanes), block_lat)
    for h in range(halves):
        strips = [mixed[pl.ds(h * rows + i, levels, stride=block_lon), :] for i in range(block_lon)]
        for b in range(block_rows):
            out = None
            for i, strip in enumerate(strips):
                moved = pltpu.roll(strip, ((i - b) * block_lat) % lanes, 1)
                out = moved if out is None else jnp.where(group == i, moved, out)
            blocks_ref[b, h * levels : (h + 1) * levels, :] = out


def fold(total, static, parts):
    halves, rows, lanes = total.shape
    levels = rows // block_lon
    block_rows = lanes // parts // block_lat
    return pl.pallas_call(
        functools.partial(fold_kernel, parts, block_rows),
        in_specs=[vmem()] * 2,
        out_specs=vmem(),
        out_shape=jax.ShapeDtypeStruct((block_rows, halves * levels, lanes), f32),
        scratch_shapes=[pltpu.VMEM((halves * rows, lanes), f32)],
        cost_estimate=cost(2e6, 2e6),
        compiler_params=params(),
        name="fold",
    )(total, static)


def split(x):
    high = x.astype(bf16)
    return high, (x - high.astype(f32)).astype(bf16)


def horiz_kernel(horiz_ref, high, low, high_t, low_t):
    hi, lo = split(horiz_ref[...])
    high[...] = hi
    low[...] = lo
    flipped_hi, flipped_lo = split(horiz_ref[...].T)
    high_t[...] = flipped_hi
    low_t[...] = flipped_lo


def horiz_parts(horiz):
    slots, cells = horiz.shape
    return pl.pallas_call(
        horiz_kernel,
        in_specs=[vmem()],
        out_specs=[vmem()] * 4,
        out_shape=[jax.ShapeDtypeStruct((slots, cells), bf16)] * 2
        + [jax.ShapeDtypeStruct((cells, slots), bf16)] * 2,
        cost_estimate=cost(1e6, 2e6),
        compiler_params=params(),
        name="horiz_parts",
    )(horiz)


def product3(a, high, low):
    a_high, a_low = split(a)
    dot = functools.partial(jnp.dot, preferred_element_type=f32)
    return dot(a_high, high) + (dot(a_low, high) + dot(a_high, low))


def observe_kernel(
    parts, halves, lat_blocks, me_ref, blocks_ref, vert_ref, high, low, high_t, low_t,
    ids_ref, value_ref, rinv_ref, *outs
):
    block_rows, stacked, cells = blocks_ref.shape
    levels = stacked // halves
    piece = levels // parts
    base = me_ref[0] * block_rows
    ids = ids_ref[...]
    vert = vert_ref[...]
    picks = [
        [ids == h * lat_blocks + base + b for b in range(block_rows)] for h in range(halves)
    ]
    mine = None
    hx = jnp.zeros(ids.shape, f32)
    for b in range(block_rows):
        projected = product3(blocks_ref[b], high_t[...], low_t[...])
        for h in range(halves):
            one = jnp.sum(projected[h * levels : (h + 1) * levels] * vert, axis=0, keepdims=True)
            hx = jnp.where(picks[h][b], one, hx)
            mine = picks[h][b] if mine is None else mine | picks[h][b]
    miss = hx - value_ref[...]
    dep = jnp.where(mine, rinv_ref[...] * miss, 0.0)
    total = 0.5 * jnp.sum(dep * miss, axis=1, keepdims=True)
    tile = (8, cells)
    spot = lax.broadcasted_iota(jnp.int32, tile, 0) * cells
    spot = spot + lax.broadcasted_iota(jnp.int32, tile, 1)
    share = jnp.where(spot == me_ref[1], jnp.broadcast_to(total, tile), 0.0)
    for ref in outs:
        ref[ref.shape[0] - 8 :, :] = share
    for b in range(block_rows):
        weights = jnp.concatenate(
            [vert * jnp.where(picks[h][b], dep, 0.0) for h in range(halves)], axis=0
        )
        adjoint = product3(weights, high[...], low[...])
        for h in range(halves):
            block = h * block_rows + b
            for s, ref in enumerate(outs):
                first = h * levels + s * piece
                count = piece * halves * block_rows
                where = pl.ds(block, piece, stride=halves * block_rows)
                ref[where, :] = blocks_ref[b, first : first + piece, :]
                where = pl.ds(count + block, piece, stride=halves * block_rows)
                ref[where, :] = adjoint[first : first + piece]


def observe(me, blocks, vert, horiz, ids, value, rinv, parts, halves, lat_blocks):
    block_rows, stacked, cells = blocks.shape
    back = jax.ShapeDtypeStruct((2 * block_rows * stacked // parts + 8, cells), f32)
    return pl.pallas_call(
        functools.partial(observe_kernel, parts, halves, lat_blocks),
        in_specs=[smem()] + [vmem()] * 9,
        out_specs=[vmem()] * parts,
        out_shape=[back] * parts,
        cost_estimate=cost(1e9, 4e6),
        compiler_params=params(),
        name="observe",
    )(me, blocks, vert, *horiz, ids, value, rinv)


def unpack(index, backs, levels, columns, lanes):
    parts = len(backs)
    halves = columns // block_lon
    block_rows = lanes // parts // block_lat
    used = 2 * levels * halves * block_rows
    twice = jnp.concatenate([x[None, :used] for x in backs + backs], axis=0)
    ordered = lax.dynamic_slice_in_dim(twice, (parts - index) % parts, parts, axis=0)
    ordered = ordered.reshape(parts, 2, levels, halves, block_rows, block_lon, block_lat)
    both = ordered.transpose(1, 2, 3, 5, 0, 4, 6).reshape(2, levels, columns, lanes)
    return both[0], both[1]


def exchange(blocks, axis, sign):
    return [blocks[0]] + [
        lax.ppermute(blocks[s], axis, shift_by(axis, sign * s)) for s in range(1, len(blocks))
    ]


def bands_kernel(rows, span, lon_ref, static_ref, *outs):
    for taper_ref, out in zip((lon_ref, static_ref), outs):
        column = lax.broadcasted_iota(jnp.int32, out.shape, 1)
        offset = column // span * rows + column % rows
        offset = offset - lax.broadcasted_iota(jnp.int32, out.shape, 0)
        band = jnp.zeros(out.shape, f32)
        for d in range(2 * rows + 1):
            band = jnp.where(offset == d, taper_ref[d], band)
        out[...] = band


def bands(lon_taper, static_taper, rows, span):
    shape = jax.ShapeDtypeStruct((rows, 3 * span), f32)
    return pl.pallas_call(
        functools.partial(bands_kernel, rows, span),
        in_specs=[smem()] * 2,
        out_specs=[vmem()] * 2,
        out_shape=[shape] * 2,
        compiler_params=params(),
        name="bands",
    )(lon_taper.astype(f32), static_taper.astype(f32))


def operator(vert_rows, band, me, parts, levels, rows):
    total = parts * levels
    span = total * rows
    column = jnp.arange(3 * span)
    source = column % span // rows
    owner = (me - source // levels) % parts
    pick = (jnp.arange(vert_rows.shape[1])[:, None] == (owner * levels + source % levels)[None, :])
    wide = jnp.dot(vert_rows, pick.astype(bf16), preferred_element_type=f32).astype(bf16)
    grow = (jnp.arange(span)[:, None] // rows == jnp.arange(total)[None, :]).astype(bf16)
    tall = jnp.dot(grow, wide, preferred_element_type=f32)
    return (tall.reshape(total, rows, 3 * span) * band[None]).astype(bf16).reshape(span, 3 * span)


def sent(packed):
    return exchange(packed, "lev", 1)


def chunk_sizes(groups):
    sizes = [2, 4, 4, 4, 4, 2]
    if sum(sizes) == groups:
        return sizes
    return [groups - groups // 2, groups // 2] if groups > 1 else [groups]


def body(
    field,
    ens,
    sdev,
    lon_taper,
    static_taper,
    loc_vert,
    static_vert,
    obs_block,
    obs_value,
    obs_rinv,
    obs_horiz,
    obs_vert,
):
    members, levels, columns, lanes = ens.shape
    parts = lax.axis_size("lev")
    rows = lon_taper.shape[0] // 2
    halves = columns // rows
    lat_blocks = lanes // block_lat
    slots = obs_block.shape[0]
    index = lax.axis_index("lev")
    me = jnp.stack([index, lax.axis_index("lon") * parts + index]).astype(jnp.int32)

    sizes = chunk_sizes(members // parts)
    starts = [sum(sizes[:n]) for n in range(len(sizes))]
    first_pack = pack(me, ens, starts[0], sizes[0], parts, halves, me)
    messages = pack_small(
        me, field, sdev, obs_vert, loc_vert, static_vert, parts, halves, first_pack[0]
    )
    half_rows = levels * rows
    received = [sent(first_pack)]
    after = messages[0]
    messages = exchange(messages, "lev", 1)
    for n in range(1, len(sizes)):
        packed = pack(me, ens, starts[n], sizes[n], parts, halves, after)
        after = packed[0]
        received.append(sent(packed))

    wide_field, wide_sdev, static_first, static_last, vert_all, loc_all, stat_all = spread(
        messages, levels, half_rows, slots, parts, halves, after
    )
    lon_band, static_band = bands(lon_taper, static_taper, rows, parts * half_rows)
    loc_matrix = operator(loc_all, lon_band, index, parts, levels, rows)
    stat_matrix = operator(stat_all, static_band, index, parts, levels, rows)
    horiz = horiz_parts(obs_horiz)

    def halo(first, last):
        left = lax.ppermute(last, "lon", shift_by("lon", 1))
        right = lax.ppermute(first, "lon", shift_by("lon", -1))
        return left, right

    left, right = halo(static_first, static_last)
    static = filtered(stat_matrix, left, static_first, static_last, right, [wide_sdev[None]], None)
    total = None
    ready = None
    after = static_first
    for xs in received:
        first, last = product(wide_field, xs, after)
        if ready is not None:
            total = filtered(loc_matrix, *ready, total)
            after = total
        else:
            after = static
        left, right = halo(first, last)
        ready = left, first, last, right, xs
    total = filtered(loc_matrix, *ready, total)

    blocks = fold(total, static, parts)

    nblk = columns // block_lon * lat_blocks
    ids = jnp.where(obs_block >= 0, obs_block - lax.axis_index("lon") * nblk, -1)
    backs = observe(
        me, blocks, vert_all, horiz, ids[None], obs_value[None], obs_rinv[None],
        parts, halves, lat_blocks,
    )
    backs = exchange(backs, "lev", -1)
    shares = sum(x[-8:] for x in backs)
    reach = 1
    while reach < lax.axis_size("lon"):
        pairs = [(i, i ^ reach) for i in range(lax.axis_size("lon"))]
        shares = shares + lax.ppermute(shares, "lon", pairs)
        reach *= 2
    obs_cost = jnp.sum(shares)

    increment, adjoint_field = unpack(index, backs, levels, columns, lanes)
    return (increment, adjoint_field, obs_cost)


def solution(mesh):
    return jax.shard_map(
        body,
        mesh=mesh,
        in_specs=(
            P("lev", "lon", None),
            P(None, "lev", "lon", None),
            P("lev", "lon", None),
            P(),
            P(),
            P("lev", None),
            P("lev", None),
            P("lon"),
            P("lon"),
            P("lon"),
            P("lon", None),
            P("lon", "lev"),
        ),
        out_specs=(P("lev", "lon", None), P("lev", "lon", None), P()),
        check_vma=False,
    )
```

time: 398 us -> 229 us (0.58)
  blocking collectives: 171 us -> 0 us
  Pallas kernels: 0 us -> 68.3 us
  waiting for transfers between devices: 117 us -> 53.3 us
  starting transfers between devices: 31.1 us -> 76.4 us
  matrix products: 23.3 us -> 2.56 us
  local copies, waits for them, and re-layouts: 41.5 us -> 24.9 us
  other arithmetic: 11.6 us -> 1.33 us
    all_gather x2 -> x0, blocking collectives: 148 us -> none  [the longest x1 135 us: body(): lax.all_gather(loc_vert, 'lev', axis=0, tiled=True)]
    ppermute x4 -> x41, starting transfers between devices: 6.12 us -> 76.4 us  [the longest x24 56.3 us: exchange(): lax.ppermute(blocks[s], axis, shift_by(axis, sign * s))]
    pallas_call x0 -> x25, Pallas kernels: none -> 68.3 us  [the longest x7 30.5 us: filtered(): pl.pallas_call(functools.partial(filter_kernel, pair, total is not None),...]
    all_to_all x5 -> x0, waiting for transfers between devices: 52.4 us -> none  [the longest x1 46.5 us: body(): lax.all_to_all(ens, 'lev', split_axis=2, concat_axis=1, tiled=True)]
    all_to_all x5 -> x0, starting transfers between devices: 25 us -> none  [the longest x1 5.57 us: body(): lax.all_to_all(ssmooth, 'lev', split_axis=2, concat_axis=1, tiled=True)]
    psum x2 -> x0, blocking collectives: 22.3 us -> none  [the longest x1 12.3 us: body(): obs_cost = lax.psum(0.5 * jnp.sum(dep * miss), 'lon')]
    dot_general x8 -> x2, matrix products: 23.3 us -> 2.56 us  [operator(): tall = jnp.dot(grow, wide, preferred_element_type=f32)]
    convert_element_type x3 -> x0, local copies, waits for them, and re-layouts: 15.6 us -> none  [the longest x1 10.2 us: body(): ens_cols = jnp.sum(ecols.astype(jnp.float32) * zvert, axis=0)[None]]
  transfers between devices with their start and end apart: 9 -> 41, of which waited for: 5 -> 14; matrix products, arithmetic and copies ran while one was open for 16% -> 4% of each run, Pallas kernels for 0% -> 27%
where the time goes in v1:
time: 229 us; the launch traced here: 228 us
  starting transfers between devices  76.4 us (33%)
  Pallas kernels  68.3 us (30%)
  waiting for transfers between devices  53.3 us (23%)
  local copies, waits for them, and re-layouts  24.9 us (11%)
  matrix products  2.56 us (1%)
    ppermute x24, starting transfers between devices, exchange(): lax.ppermute(blocks[s], axis, shift_by(axis, sign * s))  56.3 us
    ppermute x24, waiting for transfers between devices, exchange(): lax.ppermute(blocks[s], axis, shift_by(axis, sign * s))  49.6 us
    pallas_call x7, Pallas kernels, filtered(): pl.pallas_call(functools.partial(filter_kernel, pair, total is not None),...  30.5 us
    pallas_call x6, Pallas kernels, pack(): pl.pallas_call(functools.partial(pack_kernel, parts, halves), grid=(count...  21.1 us
    unnamed x130, local copies, waits for them, and re-layouts  18.6 us
    ppermute x7, starting transfers between devices, halo(): right = lax.ppermute(first, 'lon', shift_by('lon', -1))  18.5 us
    pallas_call x6, Pallas kernels, product(): pl.pallas_call(functools.partial(product_kernel, parts), grid=(count // s...  11.2 us
  transfers between devices with their start and end apart: 41, of which 14 were waited for; matrix products, arithmetic and copies ran while one was open for 4% of the time, Pallas kernels for 27%

profile of v1, /device:TPU:0, one launch (start us, length us, event | category | flops | bytes accessed | tf_op | source)
XLA Modules:
  0.0 228.1 jit_solution(1941000742984430987)
XLA Ops:
  7.5 3.1 %collective-permute-start = (bf16[496,128]{1,0:T(8,128)(2,1)S(1)}, bf16[496,128]{1,0:T(8,128)(2,1)S(1)}, u32[]{:S(2)}, u32[]{:S(2)}) collective-permute-start(bf16[496,128]{1,0:T(8,128)(2,1)S(1)} %get-tuple-element.67), channel_id=1, source_target_pairs={{0,1},{1,2},{2,3},{3,0},{4,5},{5,6},{6,7},{7,4},{8,9},{9,10},{10,1... | collective-permute-start | bytes 380936 | tf_op jit(solution)/shard_map/ppermute | solution.py:426
  15.5 4.0 %pack.7 = (bf16[4,2,144,128]{3,2,1,0:T(8,128)(2,1)}, bf16[4,2,144,128]{3,2,1,0:T(8,128)(2,1)}, bf16[4,2,144,128]{3,2,1,0:T(8,128)(2,1)}, bf16[4,2,144,128]{3,2,1,0:T(8,128)(2,1)}) custom-call(s32[2]{0:T(128)} %pad_add_fusion.me_ref.after, bf16[80,18,16,128]{3,2,1,0:T(8,128)(2,1)} %ens_ref.11, bf16[496,128]{1,0:T(8,128)(2,1)} %copy-done.16), custom_call_target="tpu_custom_call" | custom-call | flops 16000000 | bytes 2359296 | tf_op jit(solution)/shard_map/pack/pallas_call | solution.py:75
  19.5 4.0 %pack.8 = (bf16[4,2,144,128]{3,2,1,0:T(8,128)(2,1)}, bf16[4,2,144,128]{3,2,1,0:T(8,128)(2,1)}, bf16[4,2,144,128]{3,2,1,0:T(8,128)(2,1)}, bf16[4,2,144,128]{3,2,1,0:T(8,128)(2,1)}) custom-call(s32[2]{0:T(128)} %pad_add_fusion.me_ref.after, bf16[80,18,16,128]{3,2,1,0:T(8,128)(2,1)} %ens_ref.11, bf16[4,2,144,128]{3,2,1,0:T(8,128)(2,1)} %get-tuple-element.62.after.refs_0_), custom_call_target="tpu_custom_call" | custom-call | flops 16000000 | bytes 2359296 | tf_op jit(solution)/shard_map/pack/pallas_call | solution.py:75
  23.6 4.0 %pack.9 = (bf16[4,2,144,128]{3,2,1,0:T(8,128)(2,1)}, bf16[4,2,144,128]{3,2,1,0:T(8,128)(2,1)}, bf16[4,2,144,128]{3,2,1,0:T(8,128)(2,1)}, bf16[4,2,144,128]{3,2,1,0:T(8,128)(2,1)}) custom-call(s32[2]{0:T(128)} %pad_add_fusion.me_ref.after, bf16[80,18,16,128]{3,2,1,0:T(8,128)(2,1)} %ens_ref.11, bf16[4,2,144,128]{3,2,1,0:T(8,128)(2,1)} %get-tuple-element.63.after.refs_0_), custom_call_target="tpu_custom_call" | custom-call | flops 16000000 | bytes 2359296 | tf_op jit(solution)/shard_map/pack/pallas_call | solution.py:75
  27.6 4.0 %pack.10 = (bf16[4,2,144,128]{3,2,1,0:T(8,128)(2,1)}, bf16[4,2,144,128]{3,2,1,0:T(8,128)(2,1)}, bf16[4,2,144,128]{3,2,1,0:T(8,128)(2,1)}, bf16[4,2,144,128]{3,2,1,0:T(8,128)(2,1)}) custom-call(s32[2]{0:T(128)} %pad_add_fusion.me_ref.after, bf16[80,18,16,128]{3,2,1,0:T(8,128)(2,1)} %ens_ref.11, bf16[4,2,144,128]{3,2,1,0:T(8,128)(2,1)} %get-tuple-element.64.after.refs_0_), custom_call_target="tpu_custom_call" | custom-call | flops 16000000 | bytes 2359296 | tf_op jit(solution)/shard_map/pack/pallas_call | solution.py:75
  34.2 2.9 %collective-permute-start.12 = (bf16[2,2,144,128]{3,2,1,0:T(8,128)(2,1)S(1)}, bf16[2,2,144,128]{3,2,1,0:T(8,128)(2,1)S(1)}, u32[]{:S(2)}, u32[]{:S(2)}) collective-permute-start(bf16[2,2,144,128]{3,2,1,0:T(8,128)(2,1)S(1)} %copy-done.58), channel_id=1, source_target_pairs={{0,3},{1,0},{2,1},{3,2},{4,7},{5,4},{6,5},{7,6},{8,11},{9,8},{10,9... | collective-permute-start | bytes 442376 | tf_op jit(solution)/shard_map/ppermute | solution.py:426
  41.7 2.6 %collective-permute-start.4 = (bf16[1,576,128]{2,1,0:T(8,128)(2,1)S(1)}, bf16[1,576,128]{2,1,0:T(8,128)(2,1)S(1)}, u32[]{:S(2)}, u32[]{:S(2)}) collective-permute-start(bf16[1,576,128]{2,1,0:T(8,128)(2,1)S(1)} %get-tuple-element.76.first.after), channel_id=1, source_target_pairs={{0,28},{4,0},{8,4},{12,8},{16,12},{20,16},{24,20},{28,24},{1,29},{... | collective-permute-start | bytes 442376 | tf_op jit(solution)/shard_map/ppermute | solution.py:525
  48.0 2.8 %collective-permute-start.7 = (bf16[4,2,144,128]{3,2,1,0:T(8,128)(2,1)}, bf16[4,2,144,128]{3,2,1,0:T(8,128)(2,1)}, u32[]{:S(2)}, u32[]{:S(2)}) collective-permute-start(bf16[4,2,144,128]{3,2,1,0:T(8,128)(2,1)} %get-tuple-element.80), channel_id=1, source_target_pairs={{0,3},{1,0},{2,1},{3,2},{4,7},{5,4},{6,5},{7,6},{8,11},{9,8},{10,9... | collective-permute-start | bytes 884744 | tf_op jit(solution)/shard_map/ppermute | solution.py:426
  53.0 2.6 %collective-permute-start.14 = (bf16[2,576,128]{2,1,0:T(8,128)(2,1)}, bf16[2,576,128]{2,1,0:T(8,128)(2,1)}, u32[]{:S(2)}, u32[]{:S(2)}) collective-permute-start(bf16[2,576,128]{2,1,0:T(8,128)(2,1)} %get-tuple-element.87.first), channel_id=1, source_target_pairs={{0,28},{4,0},{8,4},{12,8},{16,12},{20,16},{24,20},{28,24},{1,29},{... | collective-permute-start | bytes 884744 | tf_op jit(solution)/shard_map/ppermute | solution.py:525
  62.4 6.3 %collective-permute-done.6.refs_2_ = bf16[4,2,144,128]{3,2,1,0:T(8,128)(2,1)} collective-permute-done((bf16[4,2,144,128]{3,2,1,0:T(8,128)(2,1)}, bf16[4,2,144,128]{3,2,1,0:T(8,128)(2,1)}, u32[]{:S(2)}, u32[]{:S(2)}) %collective-permute-start.6) | collective-permute-done | bytes 294944 | tf_op jit(solution)/shard_map/ppermute | solution.py:426
  73.8 6.2 %collective-permute-start.20 = (bf16[4,2,144,128]{3,2,1,0:T(8,128)(2,1)}, bf16[4,2,144,128]{3,2,1,0:T(8,128)(2,1)}, u32[]{:S(2)}, u32[]{:S(2)}) collective-permute-start(bf16[4,2,144,128]{3,2,1,0:T(8,128)(2,1)} %get-tuple-element.93), channel_id=1, source_target_pairs={{0,1},{1,2},{2,3},{3,0},{4,5},{5,6},{6,7},{7,4},{8,9},{9,10},{10,1... | collective-permute-start | bytes 884744 | tf_op jit(solution)/shard_map/ppermute | solution.py:426
  83.3 3.3 %filtered.8.refs_4_.after = f32[2,576,128]{2,1,0:T(8,128)S(1)} custom-call(bf16[576,1728]{1,0:T(8,128)(2,1)S(1)} %fusion.1.matrix_ref, bf16[2,576,128]{2,1,0:T(8,128)(2,1)} %collective-permute-done.13.left, bf16[2,576,128]{2,1,0:T(8,128)(2,1)} %get-tuple-element.87.first, bf16[2,576,128]{2,1,0:T(8,128)(2,1)} %get-tuple-element.86.last, ...), custom_call_target="tpu_custom_call" | custom-call | flops 1019215872 | bytes 1769472 | tf_op jit(solution)/shard_map/filtered/pallas_call | solution.py:262
  89.4 10.9 %collective-permute-done.21.refs_2_ = bf16[4,2,144,128]{3,2,1,0:T(8,128)(2,1)} collective-permute-done((bf16[4,2,144,128]{3,2,1,0:T(8,128)(2,1)}, bf16[4,2,144,128]{3,2,1,0:T(8,128)(2,1)}, u32[]{:S(2)}, u32[]{:S(2)}) %collective-permute-start.21) | collective-permute-done | bytes 294944 | tf_op jit(solution)/shard_map/ppermute | solution.py:426
  105.6 6.8 %collective-permute-start.15 = (bf16[4,2,144,128]{3,2,1,0:T(8,128)(2,1)S(1)}, bf16[4,2,144,128]{3,2,1,0:T(8,128)(2,1)S(1)}, u32[]{:S(2)}, u32[]{:S(2)}) collective-permute-start(bf16[4,2,144,128]{3,2,1,0:T(8,128)(2,1)S(1)} %copy-done.54), channel_id=1, source_target_pairs={{0,1},{1,2},{2,3},{3,0},{4,5},{5,6},{6,7},{7,4},{8,9},{9,10},{10,1... | collective-permute-start | bytes 884744 | tf_op jit(solution)/shard_map/ppermute | solution.py:426
  114.8 6.1 %filtered.9.after.refs_4_ = f32[2,576,128]{2,1,0:T(8,128)} custom-call(bf16[576,1728]{1,0:T(8,128)(2,1)} %copy-done.2, bf16[4,576,128]{2,1,0:T(8,128)(2,1)} %collective-permute-done.8.left, bf16[4,576,128]{2,1,0:T(8,128)(2,1)} %get-tuple-element.82.first, bf16[4,576,128]{2,1,0:T(8,128)(2,1)} %get-tuple-element.81.last, ...), custom_call_target="tpu_custom_call" | custom-call | flops 2038431744 | bytes 3538944 | tf_op jit(solution)/shard_map/filtered/pallas_call | solution.py:262
  121.0 10.9 %collective-permute-done.16.refs_2_ = bf16[4,2,144,128]{3,2,1,0:T(8,128)(2,1)S(1)} collective-permute-done((bf16[4,2,144,128]{3,2,1,0:T(8,128)(2,1)S(1)}, bf16[4,2,144,128]{3,2,1,0:T(8,128)(2,1)S(1)}, u32[]{:S(2)}, u32[]{:S(2)}) %collective-permute-start.16) | collective-permute-done | bytes 294944 | tf_op jit(solution)/shard_map/ppermute | solution.py:426
  138.6 6.1 %collective-permute-start.30 = (bf16[4,2,144,128]{3,2,1,0:T(8,128)(2,1)S(1)}, bf16[4,2,144,128]{3,2,1,0:T(8,128)(2,1)S(1)}, u32[]{:S(2)}, u32[]{:S(2)}) collective-permute-start(bf16[4,2,144,128]{3,2,1,0:T(8,128)(2,1)S(1)} %copy-done.51), channel_id=1, source_target_pairs={{0,1},{1,2},{2,3},{3,0},{4,5},{5,6},{6,7},{7,4},{8,9},{9,10},{10,1... | collective-permute-start | bytes 884744 | tf_op jit(solution)/shard_map/ppermute | solution.py:426
  147.9 6.1 %filtered.10.refs_4_.after = f32[2,576,128]{2,1,0:T(8,128)} custom-call(bf16[576,1728]{1,0:T(8,128)(2,1)} %copy-done.2, bf16[4,576,128]{2,1,0:T(8,128)(2,1)} %copy-done.46, bf16[4,576,128]{2,1,0:T(8,128)(2,1)} %get-tuple-element.97.first, bf16[4,576,128]{2,1,0:T(8,128)(2,1)} %get-tuple-element.96.last, bf16[4,576,128]{2,1,0:T(8,128)(2,1)} %copy-done.48, ...), custom_call_target="tpu_custom_call" | custom-call | flops 2038431744 | bytes 3538944 | tf_op jit(solution)/shard_map/filtered/pallas_call | solution.py:262
  154.4 9.9 %collective-permute-done.31.refs_2_ = bf16[4,2,144,128]{3,2,1,0:T(8,128)(2,1)S(1)} collective-permute-done((bf16[4,2,144,128]{3,2,1,0:T(8,128)(2,1)S(1)}, bf16[4,2,144,128]{3,2,1,0:T(8,128)(2,1)S(1)}, u32[]{:S(2)}, u32[]{:S(2)}) %collective-permute-start.31) | collective-permute-done | bytes 294944 | tf_op jit(solution)/shard_map/ppermute | solution.py:426
  171.0 6.1 %collective-permute-start.25 = (bf16[2,2,144,128]{3,2,1,0:T(8,128)(2,1)S(1)}, bf16[2,2,144,128]{3,2,1,0:T(8,128)(2,1)S(1)}, u32[]{:S(2)}, u32[]{:S(2)}) collective-permute-start(bf16[2,2,144,128]{3,2,1,0:T(8,128)(2,1)S(1)} %copy-done.57), channel_id=1, source_target_pairs={{0,1},{1,2},{2,3},{3,0},{4,5},{5,6},{6,7},{7,4},{8,9},{9,10},{10,1... | collective-permute-start | bytes 442376 | tf_op jit(solution)/shard_map/ppermute | solution.py:426
  179.6 6.1 %filtered.11.after.refs_4_ = f32[2,576,128]{2,1,0:T(8,128)} custom-call(bf16[576,1728]{1,0:T(8,128)(2,1)} %copy-done.2, bf16[4,576,128]{2,1,0:T(8,128)(2,1)} %copy-done.45, bf16[4,576,128]{2,1,0:T(8,128)(2,1)} %get-tuple-element.92.first, bf16[4,576,128]{2,1,0:T(8,128)(2,1)} %get-tuple-element.91.last, bf16[4,576,128]{2,1,0:T(8,128)(2,1)} %copy-done.47, ...), custom_call_target="tpu_custom_call" | custom-call | flops 2038431744 | bytes 3538944 | tf_op jit(solution)/shard_map/filtered/pallas_call | solution.py:262
  191.5 6.2 %filtered.12.refs_4_ = f32[2,576,128]{2,1,0:T(8,128)} custom-call(bf16[576,1728]{1,0:T(8,128)(2,1)} %copy-done.2, bf16[4,576,128]{2,1,0:T(8,128)(2,1)} %collective-permute-done.33.left, bf16[4,576,128]{2,1,0:T(8,128)(2,1)} %get-tuple-element.107.first, bf16[4,576,128]{2,1,0:T(8,128)(2,1)} %get-tuple-element.106.last, ...), custom_call_target="tpu_custom_call" | custom-call | flops 2038431744 | bytes 3538944 | tf_op jit(solution)/shard_map/filtered/pallas_call | solution.py:262
  203.0 4.7 %collective-permute-start.35 = (f32[152,128]{1,0:T(8,128)S(1)}, f32[152,128]{1,0:T(8,128)S(1)}, u32[]{:S(2)}, u32[]{:S(2)}) collective-permute-start(f32[152,128]{1,0:T(8,128)S(1)} %get-tuple-element.114), channel_id=1, source_target_pairs={{0,3},{1,0},{2,1},{3,2},{4,7},{5,4},{6,5},{7,6},{8,11},{9,8},{10,9... | collective-permute-start | bytes 233480 | tf_op jit(solution)/shard_map/ppermute | solution.py:426
  210.5 5.4 %collective-permute-done.36 = f32[152,128]{1,0:T(8,128)S(1)} collective-permute-done((f32[152,128]{1,0:T(8,128)S(1)}, f32[152,128]{1,0:T(8,128)S(1)}, u32[]{:S(2)}, u32[]{:S(2)}) %collective-permute-start.36) | collective-permute-done | bytes 77856 | tf_op jit(solution)/shard_map/ppermute | solution.py:426
  (233 shorter events, 95.6 us)
Async XLA Ops:
  7.5 26.7 %collective-permute-start = (bf16[496,128]{1,0:T(8,128)(2,1)S(1)}, bf16[496,128]{1,0:T(8,128)(2,1)S(1)}, u32[]{:S(2)}, u32[]{:S(2)}) collective-permute-start(bf16[496,128]{1,0:T(8,128)(2,1)S(1)} %get-tuple-element.67), channel_id=1, source_target_pairs={{0,1},{1,2},{2,3},{3,0},{4,5},{5,6},{6,7},{7,4},{8,9},{9,10},{10,1... | collective-permute-start | bytes 380936 | tf_op jit(solution)/shard_map/ppermute | solution.py:426
  10.6 26.5 %collective-permute-start.1 = (bf16[496,128]{1,0:T(8,128)(2,1)S(1)}, bf16[496,128]{1,0:T(8,128)(2,1)S(1)}, u32[]{:S(2)}, u32[]{:S(2)}) collective-permute-start(bf16[496,128]{1,0:T(8,128)(2,1)S(1)} %get-tuple-element.68), channel_id=1, source_target_pairs={{0,2},{1,3},{2,0},{3,1},{4,6},{5,7},{6,4},{7,5},{8,10},{9,11},{10,... | collective-permute-start | bytes 380936 | tf_op jit(solution)/shard_map/ppermute | solution.py:426
  13.2 23.9 %collective-permute-start.2 = (bf16[496,128]{1,0:T(8,128)(2,1)S(1)}, bf16[496,128]{1,0:T(8,128)(2,1)S(1)}, u32[]{:S(2)}, u32[]{:S(2)}) collective-permute-start(bf16[496,128]{1,0:T(8,128)(2,1)S(1)} %get-tuple-element.69), channel_id=1, source_target_pairs={{0,3},{1,0},{2,1},{3,2},{4,7},{5,4},{6,5},{7,6},{8,11},{9,8},{10,9... | collective-permute-start | bytes 380936 | tf_op jit(solution)/shard_map/ppermute | solution.py:426
  14.5 31.3 %collective-permute-start.10 = (bf16[2,2,144,128]{3,2,1,0:T(8,128)(2,1)}, bf16[2,2,144,128]{3,2,1,0:T(8,128)(2,1)S(1)}, u32[]{:S(2)}, u32[]{:S(2)}) collective-permute-start(bf16[2,2,144,128]{3,2,1,0:T(8,128)(2,1)} %get-tuple-element.83), channel_id=1, source_target_pairs={{0,1},{1,2},{2,3},{3,0},{4,5},{5,6},{6,7},{7,4},{8,9},{9,10},{10,1... | collective-permute-start | bytes 442376 | tf_op jit(solution)/shard_map/ppermute | solution.py:426
  15.2 31.2 %collective-permute-start.11 = (bf16[2,2,144,128]{3,2,1,0:T(8,128)(2,1)}, bf16[2,2,144,128]{3,2,1,0:T(8,128)(2,1)S(1)}, u32[]{:S(2)}, u32[]{:S(2)}) collective-permute-start(bf16[2,2,144,128]{3,2,1,0:T(8,128)(2,1)} %get-tuple-element.84), channel_id=1, source_target_pairs={{0,2},{1,3},{2,0},{3,1},{4,6},{5,7},{6,4},{7,5},{8,10},{9,11},{10,... | collective-permute-start | bytes 442376 | tf_op jit(solution)/shard_map/ppermute | solution.py:426
  45.8 16.6 %collective-permute-start.5 = (bf16[4,2,144,128]{3,2,1,0:T(8,128)(2,1)}, bf16[4,2,144,128]{3,2,1,0:T(8,128)(2,1)}, u32[]{:S(2)}, u32[]{:S(2)}) collective-permute-start(bf16[4,2,144,128]{3,2,1,0:T(8,128)(2,1)} %get-tuple-element.78), channel_id=1, source_target_pairs={{0,1},{1,2},{2,3},{3,0},{4,5},{5,6},{6,7},{7,4},{8,9},{9,10},{10,1... | collective-permute-start | bytes 884744 | tf_op jit(solution)/shard_map/ppermute | solution.py:426
  46.4 22.2 %collective-permute-start.6 = (bf16[4,2,144,128]{3,2,1,0:T(8,128)(2,1)}, bf16[4,2,144,128]{3,2,1,0:T(8,128)(2,1)}, u32[]{:S(2)}, u32[]{:S(2)}) collective-permute-start(bf16[4,2,144,128]{3,2,1,0:T(8,128)(2,1)} %get-tuple-element.79), channel_id=1, source_target_pairs={{0,2},{1,3},{2,0},{3,1},{4,6},{5,7},{6,4},{7,5},{8,10},{9,11},{10,... | collective-permute-start | bytes 884744 | tf_op jit(solution)/shard_map/ppermute | solution.py:426
  48.0 20.7 %collective-permute-start.7 = (bf16[4,2,144,128]{3,2,1,0:T(8,128)(2,1)}, bf16[4,2,144,128]{3,2,1,0:T(8,128)(2,1)}, u32[]{:S(2)}, u32[]{:S(2)}) collective-permute-start(bf16[4,2,144,128]{3,2,1,0:T(8,128)(2,1)} %get-tuple-element.80), channel_id=1, source_target_pairs={{0,3},{1,0},{2,1},{3,2},{4,7},{5,4},{6,5},{7,6},{8,11},{9,8},{10,9... | collective-permute-start | bytes 884744 | tf_op jit(solution)/shard_map/ppermute | solution.py:426
  52.3 27.7 %collective-permute-start.13 = (bf16[2,576,128]{2,1,0:T(8,128)(2,1)}, bf16[2,576,128]{2,1,0:T(8,128)(2,1)}, u32[]{:S(2)}, u32[]{:S(2)}) collective-permute-start(bf16[2,576,128]{2,1,0:T(8,128)(2,1)} %get-tuple-element.86.last), channel_id=1, source_target_pairs={{0,4},{4,8},{8,12},{12,16},{16,20},{20,24},{24,28},{28,0},{1,5},{5... | collective-permute-start | bytes 884744 | tf_op jit(solution)/shard_map/ppermute | solution.py:524
  53.0 28.7 %collective-permute-start.14 = (bf16[2,576,128]{2,1,0:T(8,128)(2,1)}, bf16[2,576,128]{2,1,0:T(8,128)(2,1)}, u32[]{:S(2)}, u32[]{:S(2)}) collective-permute-start(bf16[2,576,128]{2,1,0:T(8,128)(2,1)} %get-tuple-element.87.first), channel_id=1, source_target_pairs={{0,28},{4,0},{8,4},{12,8},{16,12},{20,16},{24,20},{28,24},{1,29},{... | collective-permute-start | bytes 884744 | tf_op jit(solution)/shard_map/ppermute | solution.py:525
  71.2 41.2 %collective-permute-start.8 = (bf16[4,576,128]{2,1,0:T(8,128)(2,1)}, bf16[4,576,128]{2,1,0:T(8,128)(2,1)}, u32[]{:S(2)}, u32[]{:S(2)}) collective-permute-start(bf16[4,576,128]{2,1,0:T(8,128)(2,1)} %get-tuple-element.81.last), channel_id=1, source_target_pairs={{0,4},{4,8},{8,12},{12,16},{16,20},{20,24},{24,28},{28,0},{1,5},{5... | collective-permute-start | bytes 1769480 | tf_op jit(solution)/shard_map/ppermute | solution.py:524
  71.2 42.4 %collective-permute-start.9 = (bf16[4,576,128]{2,1,0:T(8,128)(2,1)}, bf16[4,576,128]{2,1,0:T(8,128)(2,1)}, u32[]{:S(2)}, u32[]{:S(2)}) collective-permute-start(bf16[4,576,128]{2,1,0:T(8,128)(2,1)} %get-tuple-element.82.first), channel_id=1, source_target_pairs={{0,28},{4,0},{8,4},{12,8},{16,12},{20,16},{24,20},{28,24},{1,29},{... | collective-permute-start | bytes 1769480 | tf_op jit(solution)/shard_map/ppermute | solution.py:525
  80.0 20.3 %collective-permute-start.21 = (bf16[4,2,144,128]{3,2,1,0:T(8,128)(2,1)}, bf16[4,2,144,128]{3,2,1,0:T(8,128)(2,1)}, u32[]{:S(2)}, u32[]{:S(2)}) collective-permute-start(bf16[4,2,144,128]{3,2,1,0:T(8,128)(2,1)} %get-tuple-element.94), channel_id=1, source_target_pairs={{0,2},{1,3},{2,0},{3,1},{4,6},{5,7},{6,4},{7,5},{8,10},{9,11},{10,... | collective-permute-start | bytes 884744 | tf_op jit(solution)/shard_map/ppermute | solution.py:426
  81.7 18.7 %collective-permute-start.22 = (bf16[4,2,144,128]{3,2,1,0:T(8,128)(2,1)}, bf16[4,2,144,128]{3,2,1,0:T(8,128)(2,1)}, u32[]{:S(2)}, u32[]{:S(2)}) collective-permute-start(bf16[4,2,144,128]{3,2,1,0:T(8,128)(2,1)} %get-tuple-element.95), channel_id=1, source_target_pairs={{0,3},{1,0},{2,1},{3,2},{4,7},{5,4},{6,5},{7,6},{8,11},{9,8},{10,9... | collective-permute-start | bytes 884744 | tf_op jit(solution)/shard_map/ppermute | solution.py:426
  102.9 41.7 %collective-permute-start.23 = (bf16[4,576,128]{2,1,0:T(8,128)(2,1)}, bf16[4,576,128]{2,1,0:T(8,128)(2,1)S(1)}, u32[]{:S(2)}, u32[]{:S(2)}) collective-permute-start(bf16[4,576,128]{2,1,0:T(8,128)(2,1)} %get-tuple-element.96.last), channel_id=1, source_target_pairs={{0,4},{4,8},{8,12},{12,16},{16,20},{20,24},{24,28},{28,0},{1,5},{5... | collective-permute-start | bytes 1769480 | tf_op jit(solution)/shard_map/ppermute | solution.py:524
  102.9 44.2 %collective-permute-start.24 = (bf16[4,576,128]{2,1,0:T(8,128)(2,1)}, bf16[4,576,128]{2,1,0:T(8,128)(2,1)S(1)}, u32[]{:S(2)}, u32[]{:S(2)}) collective-permute-start(bf16[4,576,128]{2,1,0:T(8,128)(2,1)} %get-tuple-element.97.first), channel_id=1, source_target_pairs={{0,28},{4,0},{8,4},{12,8},{16,12},{20,16},{24,20},{28,24},{1,29},{... | collective-permute-start | bytes 1769480 | tf_op jit(solution)/shard_map/ppermute | solution.py:525
  112.3 19.6 %collective-permute-start.16 = (bf16[4,2,144,128]{3,2,1,0:T(8,128)(2,1)S(1)}, bf16[4,2,144,128]{3,2,1,0:T(8,128)(2,1)S(1)}, u32[]{:S(2)}, u32[]{:S(2)}) collective-permute-start(bf16[4,2,144,128]{3,2,1,0:T(8,128)(2,1)S(1)} %copy-done.53), channel_id=1, source_target_pairs={{0,2},{1,3},{2,0},{3,1},{4,6},{5,7},{6,4},{7,5},{8,10},{9,11},{10,... | collective-permute-start | bytes 884744 | tf_op jit(solution)/shard_map/ppermute | solution.py:426
  113.6 18.3 %collective-permute-start.17 = (bf16[4,2,144,128]{3,2,1,0:T(8,128)(2,1)S(1)}, bf16[4,2,144,128]{3,2,1,0:T(8,128)(2,1)S(1)}, u32[]{:S(2)}, u32[]{:S(2)}) collective-permute-start(bf16[4,2,144,128]{3,2,1,0:T(8,128)(2,1)S(1)} %copy-done.52), channel_id=1, source_target_pairs={{0,3},{1,0},{2,1},{3,2},{4,7},{5,4},{6,5},{7,6},{8,11},{9,8},{10,9... | collective-permute-start | bytes 884744 | tf_op jit(solution)/shard_map/ppermute | solution.py:426
  135.9 41.1 %collective-permute-start.18 = (bf16[4,576,128]{2,1,0:T(8,128)(2,1)}, bf16[4,576,128]{2,1,0:T(8,128)(2,1)S(1)}, u32[]{:S(2)}, u32[]{:S(2)}) collective-permute-start(bf16[4,576,128]{2,1,0:T(8,128)(2,1)} %get-tuple-element.91.last), channel_id=1, source_target_pairs={{0,4},{4,8},{8,12},{12,16},{16,20},{20,24},{24,28},{28,0},{1,5},{5... | collective-permute-start | bytes 1769480 | tf_op jit(solution)/shard_map/ppermute | solution.py:524
  135.9 42.5 %collective-permute-start.19 = (bf16[4,576,128]{2,1,0:T(8,128)(2,1)}, bf16[4,576,128]{2,1,0:T(8,128)(2,1)S(1)}, u32[]{:S(2)}, u32[]{:S(2)}) collective-permute-start(bf16[4,576,128]{2,1,0:T(8,128)(2,1)} %get-tuple-element.92.first), channel_id=1, source_target_pairs={{0,28},{4,0},{8,4},{12,8},{16,12},{20,16},{24,20},{28,24},{1,29},{... | collective-permute-start | bytes 1769480 | tf_op jit(solution)/shard_map/ppermute | solution.py:525
  144.6 19.7 %collective-permute-start.31 = (bf16[4,2,144,128]{3,2,1,0:T(8,128)(2,1)S(1)}, bf16[4,2,144,128]{3,2,1,0:T(8,128)(2,1)S(1)}, u32[]{:S(2)}, u32[]{:S(2)}) collective-permute-start(bf16[4,2,144,128]{3,2,1,0:T(8,128)(2,1)S(1)} %copy-done.50), channel_id=1, source_target_pairs={{0,2},{1,3},{2,0},{3,1},{4,6},{5,7},{6,4},{7,5},{8,10},{9,11},{10,... | collective-permute-start | bytes 884744 | tf_op jit(solution)/shard_map/ppermute | solution.py:426
  147.1 17.2 %collective-permute-start.32 = (bf16[4,2,144,128]{3,2,1,0:T(8,128)(2,1)S(1)}, bf16[4,2,144,128]{3,2,1,0:T(8,128)(2,1)S(1)}, u32[]{:S(2)}, u32[]{:S(2)}) collective-permute-start(bf16[4,2,144,128]{3,2,1,0:T(8,128)(2,1)S(1)} %copy-done.49), channel_id=1, source_target_pairs={{0,3},{1,0},{2,1},{3,2},{4,7},{5,4},{6,5},{7,6},{8,11},{9,8},{10,9... | collective-permute-start | bytes 884744 | tf_op jit(solution)/shard_map/ppermute | solution.py:426
  168.3 23.1 %collective-permute-start.33 = (bf16[4,576,128]{2,1,0:T(8,128)(2,1)}, bf16[4,576,128]{2,1,0:T(8,128)(2,1)}, u32[]{:S(2)}, u32[]{:S(2)}) collective-permute-start(bf16[4,576,128]{2,1,0:T(8,128)(2,1)} %get-tuple-element.106.last), channel_id=1, source_target_pairs={{0,4},{4,8},{8,12},{12,16},{16,20},{20,24},{24,28},{28,0},{1,5},{5... | collective-permute-start | bytes 1769480 | tf_op jit(solution)/shard_map/ppermute | solution.py:524
  168.3 23.1 %collective-permute-start.34 = (bf16[4,576,128]{2,1,0:T(8,128)(2,1)}, bf16[4,576,128]{2,1,0:T(8,128)(2,1)}, u32[]{:S(2)}, u32[]{:S(2)}) collective-permute-start(bf16[4,576,128]{2,1,0:T(8,128)(2,1)} %get-tuple-element.107.first), channel_id=1, source_target_pairs={{0,28},{4,0},{8,4},{12,8},{16,12},{20,16},{24,20},{28,24},{1,29},{... | collective-permute-start | bytes 1769480 | tf_op jit(solution)/shard_map/ppermute | solution.py:525
  (78 other events, 643.2 us)

commit v2 on v1

--- a/solution.py
+++ b/solution.py
@@ -12,8 +12,14 @@
 static_weight = 0.5
 block_lon = 8
 block_lat = 16
+LIMIT = 44
+plan = (2, 4, 4, 4, 2, 2, 2)
 f32 = jnp.float32
 bf16 = jnp.bfloat16
+
+
+def my_partner(place):
+    return lax.axis_index("lev") ^ place
 
 
 def shift_by(axis, amount):
@@ -30,7 +36,7 @@
 
 
 def params(count=0):
-    return pltpu.CompilerParams(vmem_limit_bytes=(24 if count <= 2 else 58) * 2**20)
+    return pltpu.CompilerParams(vmem_limit_bytes=(58 if count > 20 else LIMIT) * 2**20)
 
 
 def smem():
@@ -55,20 +61,19 @@
     return out
 
 
-def pack_kernel(parts, halves, me_ref, ens_ref, after, *outs):
+def pack_kernel(parts, halves, ens_ref, after, *outs):
     levels, columns, lanes = ens_ref.shape[1:]
     width = lanes // parts
     rows = columns // halves
-    me = me_ref[0]
     sources = [ens_ref[p].astype(f32).reshape(levels * columns, lanes) for p in range(parts)]
     for s, out in enumerate(outs):
-        packed = regroup(sources, lax.rem(me + s, parts), parts, width)
+        packed = regroup(sources, my_partner(s), parts, width)
         packed = packed.reshape(levels, halves, rows, lanes)
         for h in range(halves):
             out[0, h] = packed[:, h].reshape(levels * rows, lanes).astype(bf16)
 
 
-def pack(me, ens, start, count, parts, halves, after):
+def pack(ens, start, count, parts, halves, after):
     _, levels, columns, lanes = ens.shape
     rows = levels * columns // halves
     shape = jax.ShapeDtypeStruct((count, halves, rows, lanes), bf16)
@@ -76,16 +81,15 @@
         functools.partial(pack_kernel, parts, halves),
         grid=(count,),
         in_specs=[
-            smem(),
             pl.BlockSpec((parts, levels, columns, lanes), lambda i: (start + i, 0, 0, 0)),
             anywhere(),
         ],
         out_specs=[pl.BlockSpec((1, halves, rows, lanes), lambda i: (i, 0, 0, 0))] * parts,
         out_shape=[shape] * parts,
         cost_estimate=cost(count * 4e6, count * parts * halves * rows * lanes * 4),
-        compiler_params=params(8),
+        compiler_params=params(99),
         name="pack",
-    )(me, ens, after)
+    )(ens, after)
 
 
 def ceil_to(x, unit):
@@ -93,55 +97,54 @@
 
 
 def message_rows(levels, half_rows, slots, lanes):
-    vert = 2 * half_rows
-    loc = vert + ceil_to(levels * slots // lanes, 16)
+    loc = 2 * half_rows
     stat = loc + ceil_to(levels, 16)
-    return 0, half_rows, vert, loc, stat, stat + ceil_to(levels, 16)
+    return 0, half_rows, loc, stat, stat + ceil_to(levels, 16), levels * slots // lanes
 
 
 def pack_small_kernel(
-    parts, halves, first, me_ref, field_ref, sdev_ref, vert_ref, loc_ref, stat_ref, after, *outs
+    parts, halves, first, field_ref, sdev_ref, vert_ref, loc_ref, stat_ref, after, *outs
 ):
+    *outs, flat_ref = outs
     levels, columns, lanes = field_ref.shape
     width = lanes // parts
     rows = columns // halves
     slots = vert_ref.shape[0]
-    me = me_ref[0]
     sources = []
     for h in range(halves):
         for ref in (field_ref, sdev_ref):
             sources.append(ref[:, h * rows : (h + 1) * rows, :].reshape(levels * rows, lanes))
     flat = vert_ref[...].T
-    flat = jnp.concatenate(
+    flat_ref[...] = jnp.concatenate(
         [flat[:, t : t + lanes] for t in range(0, slots, lanes)], axis=0
     ).astype(bf16)
     for s, out in enumerate(outs):
-        high, low = split(regroup(sources, lax.rem(me + s, parts), parts, width))
+        high, low = split(regroup(sources, my_partner(s), parts, width))
         out[first[0] : first[1], :] = high
         out[first[1] : first[2], :] = low
-        out[first[2] : first[2] + flat.shape[0], :] = flat
-        for begin, ref in ((first[3], loc_ref), (first[4], stat_ref)):
+        for begin, ref in ((first[2], loc_ref), (first[3], stat_ref)):
             out[begin : begin + ceil_to(levels, 16), :] = jnp.zeros(
                 (ceil_to(levels, 16), lanes), bf16
             )
             out[begin : begin + levels, : ref.shape[1]] = ref[...]
 
 
-def pack_small(me, field, sdev, vert, loc, stat, parts, halves, after):
+def pack_small(field, sdev, vert, loc, stat, parts, halves, after):
     levels, columns, lanes = field.shape
     first = message_rows(levels, levels * columns // halves, vert.shape[0], lanes)
     return pl.pallas_call(
         functools.partial(pack_small_kernel, parts, halves, first),
-        in_specs=[smem()] + [vmem()] * 5 + [anywhere()],
-        out_specs=[vmem()] * parts,
-        out_shape=[jax.ShapeDtypeStruct((first[-1], lanes), bf16)] * parts,
+        in_specs=[vmem()] * 5 + [anywhere()],
+        out_specs=[vmem()] * (parts + 1),
+        out_shape=[jax.ShapeDtypeStruct((first[-2], lanes), bf16)] * parts
+        + [jax.ShapeDtypeStruct((first[-1], lanes), bf16)],
         compiler_params=params(),
         name="pack_small",
-    )(me, field, sdev, vert, loc, stat, after)
+    )(field, sdev, vert, loc, stat, after)
 
 
 def spread_kernel(parts, halves, levels, first, after, *refs):
-    messages, (wide_field, wide_sdev, left_end, right_end, vert, loc, stat) = (
+    messages, (wide_field, wide_sdev, left_end, right_end, loc, stat) = (
         refs[:parts],
         refs[parts:],
     )
@@ -163,12 +166,7 @@
             wide_field[h, s * rows : (s + 1) * rows, :] = wide[0]
             wide_sdev[h, s * rows : (s + 1) * rows, :] = wide[1]
             ends[h][0, s * rows : (s + 1) * rows, :] = (wide[0] * wide[1]).astype(bf16)
-        here = slice(s * levels, (s + 1) * levels)
-        count = vert.shape[1] // lanes
-        x = message[first[2] : first[2] + count * levels, :].astype(f32)
-        for t in range(count):
-            vert[here, t * lanes : (t + 1) * lanes] = x[t * levels : (t + 1) * levels]
-    for begin, out in ((first[3], loc), (first[4], stat)):
+    for begin, out in ((first[2], loc), (first[3], stat)):
         out[...] = jnp.concatenate(
             [m[begin : begin + ceil_to(levels, 16), :].astype(f32)[:levels] for m in messages],
             axis=0,
@@ -181,19 +179,18 @@
     wide = jax.ShapeDtypeStruct((halves, parts * rows, lanes), f32)
     end = jax.ShapeDtypeStruct((1, parts * rows, lanes), bf16)
     matrix = jax.ShapeDtypeStruct((parts * levels, lanes), bf16)
-    vert = jax.ShapeDtypeStruct((parts * levels, slots), f32)
     return pl.pallas_call(
         functools.partial(spread_kernel, parts, halves, levels, first),
         in_specs=[anywhere()] + [vmem()] * parts,
-        out_specs=[vmem()] * 7,
-        out_shape=[wide, wide, end, end, vert, matrix, matrix],
+        out_specs=[vmem()] * 6,
+        out_shape=[wide, wide, end, end, matrix, matrix],
         compiler_params=params(),
         name="spread",
     )(after, *messages)
 
 
-def product_kernel(parts, field_ref, after, *refs):
-    xs, ends = refs[:parts], refs[parts:]
+def product_kernel(parts, field_ref, *refs):
+    xs, ends = refs[:parts], refs[-2:]
     count, _, rows, _ = xs[0].shape
     for s, x in enumerate(xs):
         here = slice(s * rows, (s + 1) * rows)
@@ -211,14 +208,15 @@
     return pl.pallas_call(
         functools.partial(product_kernel, parts),
         grid=(count // step,),
-        in_specs=[pl.BlockSpec(wide_field.shape, lambda i: (0, 0, 0)), anywhere()]
-        + [pl.BlockSpec((step, halves, rows, lanes), lambda i: (i, 0, 0, 0))] * parts,
+        in_specs=[pl.BlockSpec(wide_field.shape, lambda i: (0, 0, 0))]
+        + [pl.BlockSpec((step, halves, rows, lanes), lambda i: (i, 0, 0, 0))] * parts
+        + [anywhere()] * len(after),
         out_specs=[pl.BlockSpec((step, parts * rows, lanes), lambda i: (i, 0, 0))] * halves,
         out_shape=[end] * halves,
         cost_estimate=cost(count * 1e6, count * halves * parts * rows * lanes * 4),
         compiler_params=params(count),
         name="product",
-    )(wide_field, after, *xs)
+    )(wide_field, *xs, *after)
 
 
 def filter_kernel(pair, has_total, matrix_ref, left, first, last, right, *refs):
@@ -350,14 +348,22 @@
 
 
 def observe_kernel(
-    parts, halves, lat_blocks, me_ref, blocks_ref, vert_ref, high, low, high_t, low_t,
-    ids_ref, value_ref, rinv_ref, *outs
+    parts, halves, lat_blocks, blocks_ref, *refs
 ):
+    verts, (
+        high, low, high_t, low_t, ids_ref, value_ref, rinv_ref, share_ref, *outs, vert_ref
+    ) = refs[:parts], refs[parts:]
     block_rows, stacked, cells = blocks_ref.shape
     levels = stacked // halves
     piece = levels // parts
-    base = me_ref[0] * block_rows
+    base = lax.axis_index("lev") * block_rows
     ids = ids_ref[...]
+    for s, ref in enumerate(verts):
+        rows = ref[...].astype(f32)
+        for t in range(rows.shape[0] // piece):
+            vert_ref[s * piece : (s + 1) * piece, t * cells : (t + 1) * cells] = rows[
+                t * piece : (t + 1) * piece
+            ]
     vert = vert_ref[...]
     picks = [
         [ids == h * lat_blocks + base + b for b in range(block_rows)] for h in range(halves)
@@ -373,57 +379,94 @@
     miss = hx - value_ref[...]
     dep = jnp.where(mine, rinv_ref[...] * miss, 0.0)
     total = 0.5 * jnp.sum(dep * miss, axis=1, keepdims=True)
-    tile = (8, cells)
-    spot = lax.broadcasted_iota(jnp.int32, tile, 0) * cells
-    spot = spot + lax.broadcasted_iota(jnp.int32, tile, 1)
-    share = jnp.where(spot == me_ref[1], jnp.broadcast_to(total, tile), 0.0)
-    for ref in outs:
-        ref[ref.shape[0] - 8 :, :] = share
+    slot = lax.axis_index("lon") * parts + lax.axis_index("lev")
+    spot = lax.broadcasted_iota(jnp.int32, share_ref.shape, 0) * cells
+    spot = spot + lax.broadcasted_iota(jnp.int32, share_ref.shape, 1)
+    share_ref[...] = jnp.where(spot == slot, jnp.broadcast_to(total, share_ref.shape), 0.0)
+    both = [[], []]
     for b in range(block_rows):
         weights = jnp.concatenate(
             [vert * jnp.where(picks[h][b], dep, 0.0) for h in range(halves)], axis=0
         )
         adjoint = product3(weights, high[...], low[...])
-        for h in range(halves):
-            block = h * block_rows + b
-            for s, ref in enumerate(outs):
-                first = h * levels + s * piece
-                count = piece * halves * block_rows
-                where = pl.ds(block, piece, stride=halves * block_rows)
-                ref[where, :] = blocks_ref[b, first : first + piece, :]
-                where = pl.ds(count + block, piece, stride=halves * block_rows)
-                ref[where, :] = adjoint[first : first + piece]
-
-
-def observe(me, blocks, vert, horiz, ids, value, rinv, parts, halves, lat_blocks):
+        both[0].append(blocks_ref[b])
+        both[1].append(adjoint)
+    for s, ref in enumerate(outs):
+        pieces = [
+            x[h * levels + s * piece : h * levels + (s + 1) * piece]
+            for b in range(block_rows)
+            for x in (both[0][b], both[1][b])
+            for h in range(halves)
+        ]
+        ref[...] = jnp.concatenate(pieces, axis=0).astype(bf16)
+
+
+def observe(blocks, verts, horiz, ids, value, rinv, parts, halves, lat_blocks):
     block_rows, stacked, cells = blocks.shape
-    back = jax.ShapeDtypeStruct((2 * block_rows * stacked // parts + 8, cells), f32)
+    back = jax.ShapeDtypeStruct((2 * block_rows * stacked // parts, cells), bf16)
+    share = jax.ShapeDtypeStruct((8, 128), f32)
     return pl.pallas_call(
         functools.partial(observe_kernel, parts, halves, lat_blocks),
-        in_specs=[smem()] + [vmem()] * 9,
-        out_specs=[vmem()] * parts,
-        out_shape=[back] * parts,
+        in_specs=[vmem()] * (8 + len(verts)),
+        scratch_shapes=[pltpu.VMEM((stacked // halves, ids.shape[1]), f32)],
+        out_specs=[vmem()] * (parts + 1),
+        out_shape=[share] + [back] * parts,
         cost_estimate=cost(1e9, 4e6),
         compiler_params=params(),
         name="observe",
-    )(me, blocks, vert, *horiz, ids, value, rinv)
-
-
-def unpack(index, backs, levels, columns, lanes):
-    parts = len(backs)
+    )(blocks, *verts, *horiz, ids, value, rinv)
+
+
+def unpack_kernel(halves, levels, *refs):
+    *backs, increment_ref, adjoint_ref, strips = refs
+    rows, lanes = backs[0].shape
+    width = lanes // len(backs)
+    block_rows = width // block_lat
+    count = rows // block_rows
+    group = lane_groups((count, lanes), block_lat)
+    pieces = []
+    for s, ref in enumerate(backs):
+        x = ref[...].astype(f32)
+        for b in range(block_rows):
+            place = my_partner(s) * width + b * block_lat
+            pieces.append((place, x[b * count : (b + 1) * count]))
+    for i in range(block_lon):
+        strip = None
+        for place, x in pieces:
+            x = jnp.where(group == i, x, 0.0)
+            x = pltpu.roll(x, lax.rem(place + lanes - i * block_lat, lanes), 1)
+            strip = x if strip is None else strip + x
+        strips[i * count : (i + 1) * count, :] = strip
+    for n, out_ref in enumerate((increment_ref, adjoint_ref)):
+        for h in range(halves):
+            for l in range(levels):
+                row = (n * halves + h) * levels + l
+                first = (l * halves + h) * block_lon
+                out_ref[first : first + block_lon, :] = strips[
+                    pl.ds(row, block_lon, stride=count), :
+                ]
+
+
+def unpack(backs, levels, columns, lanes):
     halves = columns // block_lon
-    block_rows = lanes // parts // block_lat
-    used = 2 * levels * halves * block_rows
-    twice = jnp.concatenate([x[None, :used] for x in backs + backs], axis=0)
-    ordered = lax.dynamic_slice_in_dim(twice, (parts - index) % parts, parts, axis=0)
-    ordered = ordered.reshape(parts, 2, levels, halves, block_rows, block_lon, block_lat)
-    both = ordered.transpose(1, 2, 3, 5, 0, 4, 6).reshape(2, levels, columns, lanes)
-    return both[0], both[1]
-
-
-def exchange(blocks, axis, sign):
+    outs = pl.pallas_call(
+        functools.partial(unpack_kernel, halves, levels),
+        in_specs=[vmem()] * len(backs),
+        out_specs=[vmem()] * 2,
+        out_shape=[jax.ShapeDtypeStruct((levels * columns, lanes), f32)] * 2,
+        scratch_shapes=[pltpu.VMEM((2 * levels * columns, lanes), f32)],
+        cost_estimate=cost(1e7, 1e6),
+        compiler_params=params(),
+        name="unpack",
+    )(*backs)
+    return [x.reshape(levels, columns, lanes) for x in outs]
+
+
+def exchange(blocks):
+    count = lax.axis_size("lev")
     return [blocks[0]] + [
-        lax.ppermute(blocks[s], axis, shift_by(axis, sign * s)) for s in range(1, len(blocks))
+        lax.ppermute(blocks[place], "lev", [(i, i ^ place) for i in range(count)])
+        for place in range(1, count)
     ]
 
 
@@ -450,12 +493,21 @@
     )(lon_taper.astype(f32), static_taper.astype(f32))
 
 
-def operator(vert_rows, band, me, parts, levels, rows):
+def total_of(x, axis):
+    reach = 1
+    while reach < lax.axis_size(axis):
+        pairs = [(i, i ^ reach) for i in range(lax.axis_size(axis))]
+        x = x + lax.ppermute(x, axis, pairs)
+        reach *= 2
+    return x
+
+
+def operator(vert_rows, band, parts, levels, rows):
     total = parts * levels
     span = total * rows
     column = jnp.arange(3 * span)
     source = column % span // rows
-    owner = (me - source // levels) % parts
+    owner = my_partner(source // levels)
     pick = (jnp.arange(vert_rows.shape[1])[:, None] == (owner * levels + source % levels)[None, :])
     wide = jnp.dot(vert_rows, pick.astype(bf16), preferred_element_type=f32).astype(bf16)
     grow = (jnp.arange(span)[:, None] // rows == jnp.arange(total)[None, :]).astype(bf16)
@@ -463,15 +515,16 @@
     return (tall.reshape(total, rows, 3 * span) * band[None]).astype(bf16).reshape(span, 3 * span)
 
 
-def sent(packed):
-    return exchange(packed, "lev", 1)
+def filters_after(chunk, chunks):
+    held = 2 if chunk >= chunks - 3 else 1
+    last = chunks - 1 if chunk == chunks - 1 else chunk - held
+    held = 2 if chunk - 1 >= chunks - 3 else 1
+    return range(max(chunk - 1 - held + 1, 0), last + 1)
 
 
 def chunk_sizes(groups):
-    sizes = [2, 4, 4, 4, 4, 2]
-    if sum(sizes) == groups:
-        return sizes
-    return [groups - groups // 2, groups // 2] if groups > 1 else [groups]
+    ends = [groups * sum(plan[: n + 1]) // sum(plan) for n in range(len(plan))]
+    return [end - begin for begin, end in zip([0] + ends, ends)]
 
 
 def body(
@@ -494,30 +547,29 @@
     halves = columns // rows
     lat_blocks = lanes // block_lat
     slots = obs_block.shape[0]
-    index = lax.axis_index("lev")
-    me = jnp.stack([index, lax.axis_index("lon") * parts + index]).astype(jnp.int32)
 
     sizes = chunk_sizes(members // parts)
     starts = [sum(sizes[:n]) for n in range(len(sizes))]
-    first_pack = pack(me, ens, starts[0], sizes[0], parts, halves, me)
-    messages = pack_small(
-        me, field, sdev, obs_vert, loc_vert, static_vert, parts, halves, first_pack[0]
+    first_pack = pack(ens, starts[0], sizes[0], parts, halves, lon_taper)
+    *messages, vert_rows = pack_small(
+        field, sdev, obs_vert, loc_vert, static_vert, parts, halves, first_pack[0]
     )
     half_rows = levels * rows
-    received = [sent(first_pack)]
+    received = [exchange(first_pack)]
     after = messages[0]
-    messages = exchange(messages, "lev", 1)
+    messages = exchange(messages)
     for n in range(1, len(sizes)):
-        packed = pack(me, ens, starts[n], sizes[n], parts, halves, after)
+        packed = pack(ens, starts[n], sizes[n], parts, halves, after)
         after = packed[0]
-        received.append(sent(packed))
-
-    wide_field, wide_sdev, static_first, static_last, vert_all, loc_all, stat_all = spread(
+        received.append(exchange(packed))
+
+    verts = exchange([vert_rows] * parts)
+    wide_field, wide_sdev, static_first, static_last, loc_all, stat_all = spread(
         messages, levels, half_rows, slots, parts, halves, after
     )
     lon_band, static_band = bands(lon_taper, static_taper, rows, parts * half_rows)
-    loc_matrix = operator(loc_all, lon_band, index, parts, levels, rows)
-    stat_matrix = operator(stat_all, static_band, index, parts, levels, rows)
+    loc_matrix = operator(loc_all, lon_band, parts, levels, rows)
+    stat_matrix = operator(stat_all, static_band, parts, levels, rows)
     horiz = horiz_parts(obs_horiz)
 
     def halo(first, last):
@@ -528,37 +580,30 @@
     left, right = halo(static_first, static_last)
     static = filtered(stat_matrix, left, static_first, static_last, right, [wide_sdev[None]], None)
     total = None
-    ready = None
-    after = static_first
-    for xs in received:
+    ready = []
+    after = [static_first]
+    for n, xs in enumerate(received):
         first, last = product(wide_field, xs, after)
-        if ready is not None:
-            total = filtered(loc_matrix, *ready, total)
-            after = total
-        else:
-            after = static
         left, right = halo(first, last)
-        ready = left, first, last, right, xs
-    total = filtered(loc_matrix, *ready, total)
+        ready.append((left, first, last, right, xs))
+        after = [first] if n else [first, static]
+        for m in filters_after(n, len(received)):
+            total = filtered(loc_matrix, *ready[m], total)
+            after = [total]
 
     blocks = fold(total, static, parts)
 
     nblk = columns // block_lon * lat_blocks
     ids = jnp.where(obs_block >= 0, obs_block - lax.axis_index("lon") * nblk, -1)
-    backs = observe(
-        me, blocks, vert_all, horiz, ids[None], obs_value[None], obs_rinv[None],
+    share, *backs = observe(
+        blocks, verts, horiz, ids[None], obs_value[None], obs_rinv[None],
         parts, halves, lat_blocks,
     )
-    backs = exchange(backs, "lev", -1)
-    shares = sum(x[-8:] for x in backs)
-    reach = 1
-    while reach < lax.axis_size("lon"):
-        pairs = [(i, i ^ reach) for i in range(lax.axis_size("lon"))]
-        shares = shares + lax.ppermute(shares, "lon", pairs)
-        reach *= 2
+    backs = exchange(backs)
+    shares = total_of(total_of(share, "lon"), "lev")
     obs_cost = jnp.sum(shares)
 
-    increment, adjoint_field = unpack(index, backs, levels, columns, lanes)
+    increment, adjoint_field = unpack(backs, levels, columns, lanes)
     return (increment, adjoint_field, obs_cost)
 
 

time: 229 us -> 227 us (level)
  Pallas kernels: 68.3 us -> 58.4 us
  starting transfers between devices: 76.4 us -> 82.3 us
  waiting for transfers between devices: 53.3 us -> 59.1 us
  local copies, waits for them, and re-layouts: 24.9 us -> 20.6 us
    pallas_call x7 -> x8, Pallas kernels: 30.5 us -> 22.2 us  [filtered(): pl.pallas_call(functools.partial(filter_kernel, pair, total is not None),...]
    ppermute x7 -> x8, waiting for transfers between devices: 0.13 us -> 7.13 us  [halo(): left = lax.ppermute(last, 'lon', shift_by('lon', 1))]
    ppermute x27 -> x35, starting transfers between devices: 57.9 us -> 64.6 us  [the longest x30 64.4 us: exchange(): lax.ppermute(blocks[place], 'lev', [(i, i ^ place) for i in range(count)])]
    squeeze x2 -> x0, local copies, waits for them, and re-layouts: 4.22 us -> none  [unpack(): return (both[0], both[1])]
    pallas_call x6 -> x7, Pallas kernels: 11.2 us -> 8.83 us  [product(): pl.pallas_call(functools.partial(product_kernel, parts), grid=(count // s...]
    unnamed x130 -> x137, local copies, waits for them, and re-layouts: 18.6 us -> 20.6 us
    ppermute x7 -> x8, starting transfers between devices: 18.5 us -> 17 us  [halo(): right = lax.ppermute(first, 'lon', shift_by('lon', -1))]
    ppermute x27 -> x35, waiting for transfers between devices: 53.1 us -> 51.9 us  [the longest x30 40 us: exchange(): lax.ppermute(blocks[place], 'lev', [(i, i ^ place) for i in range(count)])]
  transfers between devices with their start and end apart: 41 -> 51, of which waited for: 14 -> 17; matrix products, arithmetic and copies ran while one was open for 4% -> 2% of each run, Pallas kernels for 27% -> 24%
where the time goes in v2:
time: 227 us; the launch traced here: 226 us
  starting transfers between devices  82.3 us (36%)
  waiting for transfers between devices  59.1 us (26%)
  Pallas kernels  58.4 us (26%)
  local copies, waits for them, and re-layouts  20.6 us (9%)
  matrix products  3.39 us (1%)
    ppermute x30, starting transfers between devices, exchange(): lax.ppermute(blocks[place], 'lev', [(i, i ^ place) for i in range(count)])  64.4 us
    ppermute x30, waiting for transfers between devices, exchange(): lax.ppermute(blocks[place], 'lev', [(i, i ^ place) for i in range(count)])  40 us
    pallas_call x8, Pallas kernels, filtered(): pl.pallas_call(functools.partial(filter_kernel, pair, total is not None),...  22.2 us
    pallas_call x7, Pallas kernels, pack(): pl.pallas_call(functools.partial(pack_kernel, parts, halves), grid=(count...  21.8 us
    unnamed x137, local copies, waits for them, and re-layouts  20.6 us
    ppermute x8, starting transfers between devices, halo(): right = lax.ppermute(first, 'lon', shift_by('lon', -1))  17 us
    ppermute x5, waiting for transfers between devices, total_of(): x = x + lax.ppermute(x, axis, pairs)  11.9 us
    pallas_call x7, Pallas kernels, product(): pl.pallas_call(functools.partial(product_kernel, parts), grid=(count // s...  8.83 us
  transfers between devices with their start and end apart: 51, of which 17 were waited for; matrix products, arithmetic and copies ran while one was open for 2% of the time, Pallas kernels for 24%

profile of v2, /device:TPU:0, one launch (start us, length us, event | category | flops | bytes accessed | tf_op | source)
XLA Modules:
  0.0 225.8 jit_solution(8851297568626965023)
XLA Ops:
  3.2 3.1 %collective-permute-start.12 = (bf16[2,2,144,128]{3,2,1,0:T(8,128)(2,1)}, bf16[2,2,144,128]{3,2,1,0:T(8,128)(2,1)S(1)}, u32[]{:S(2)}, u32[]{:S(2)}) collective-permute-start(bf16[2,2,144,128]{3,2,1,0:T(8,128)(2,1)} %get-tuple-element.92), channel_id=1, source_target_pairs={{0,1},{1,0},{2,3},{3,2},{4,5},{5,4},{6,7},{7,6},{8,9},{9,8},{10,11... | collective-permute-start | bytes 442376 | tf_op jit(solution)/shard_map/ppermute | solution.py:468
  8.5 3.0 %collective-permute-start.1 = (bf16[352,128]{1,0:T(8,128)(2,1)S(1)}, bf16[352,128]{1,0:T(8,128)(2,1)S(1)}, u32[]{:S(2)}, u32[]{:S(2)}) collective-permute-start(bf16[352,128]{1,0:T(8,128)(2,1)S(1)} %get-tuple-element.78), channel_id=1, source_target_pairs={{0,2},{1,3},{2,0},{3,1},{4,6},{5,7},{6,4},{7,5},{8,10},{9,11},{10,... | collective-permute-start | bytes 270344 | tf_op jit(solution)/shard_map/ppermute | solution.py:468
  12.9 4.0 %pack.8 = (bf16[4,2,144,128]{3,2,1,0:T(8,128)(2,1)}, bf16[4,2,144,128]{3,2,1,0:T(8,128)(2,1)}, bf16[4,2,144,128]{3,2,1,0:T(8,128)(2,1)}, bf16[4,2,144,128]{3,2,1,0:T(8,128)(2,1)}) custom-call(bf16[80,18,16,128]{3,2,1,0:T(8,128)(2,1)} %ens_ref.13, bf16[352,128]{1,0:T(8,128)(2,1)} %copy-done.31), custom_call_target="tpu_custom_call" | custom-call | flops 16000000 | bytes 2359296 | tf_op jit(solution)/shard_map/pack/pallas_call | solution.py:80
  17.1 4.0 %pack.9 = (bf16[4,2,144,128]{3,2,1,0:T(8,128)(2,1)}, bf16[4,2,144,128]{3,2,1,0:T(8,128)(2,1)}, bf16[4,2,144,128]{3,2,1,0:T(8,128)(2,1)}, bf16[4,2,144,128]{3,2,1,0:T(8,128)(2,1)}) custom-call(bf16[80,18,16,128]{3,2,1,0:T(8,128)(2,1)} %ens_ref.13, bf16[4,2,144,128]{3,2,1,0:T(8,128)(2,1)} %get-tuple-element.71.after.refs_0_), custom_call_target="tpu_custom_call" | custom-call | flops 16000000 | bytes 2359296 | tf_op jit(solution)/shard_map/pack/pallas_call | solution.py:80
  21.1 4.0 %pack.10 = (bf16[4,2,144,128]{3,2,1,0:T(8,128)(2,1)}, bf16[4,2,144,128]{3,2,1,0:T(8,128)(2,1)}, bf16[4,2,144,128]{3,2,1,0:T(8,128)(2,1)}, bf16[4,2,144,128]{3,2,1,0:T(8,128)(2,1)}) custom-call(bf16[80,18,16,128]{3,2,1,0:T(8,128)(2,1)} %ens_ref.13, bf16[4,2,144,128]{3,2,1,0:T(8,128)(2,1)} %get-tuple-element.72.after.refs_0_), custom_call_target="tpu_custom_call" | custom-call | flops 16000000 | bytes 2359296 | tf_op jit(solution)/shard_map/pack/pallas_call | solution.py:80
  32.5 2.9 %collective-permute-start.13 = (bf16[2,2,144,128]{3,2,1,0:T(8,128)(2,1)S(1)}, bf16[2,2,144,128]{3,2,1,0:T(8,128)(2,1)S(1)}, u32[]{:S(2)}, u32[]{:S(2)}) collective-permute-start(bf16[2,2,144,128]{3,2,1,0:T(8,128)(2,1)S(1)} %copy-done.66), channel_id=1, source_target_pairs={{0,2},{1,3},{2,0},{3,1},{4,6},{5,7},{6,4},{7,5},{8,10},{9,11},{10,... | collective-permute-start | bytes 442376 | tf_op jit(solution)/shard_map/ppermute | solution.py:468
  48.5 14.8 %collective-permute-start.23 = (bf16[4,2,144,128]{3,2,1,0:T(8,128)(2,1)}, bf16[4,2,144,128]{3,2,1,0:T(8,128)(2,1)}, u32[]{:S(2)}, u32[]{:S(2)}) collective-permute-start(bf16[4,2,144,128]{3,2,1,0:T(8,128)(2,1)} %get-tuple-element.106), channel_id=1, source_target_pairs={{0,1},{1,0},{2,3},{3,2},{4,5},{5,4},{6,7},{7,6},{8,9},{9,8},{10,11... | collective-permute-start | bytes 884744 | tf_op jit(solution)/shard_map/ppermute | solution.py:468
  75.8 3.4 %collective-permute-done.10.refs_2_ = bf16[4,2,144,128]{3,2,1,0:T(8,128)(2,1)} collective-permute-done((bf16[4,2,144,128]{3,2,1,0:T(8,128)(2,1)}, bf16[4,2,144,128]{3,2,1,0:T(8,128)(2,1)}, u32[]{:S(2)}, u32[]{:S(2)}) %collective-permute-start.10) | collective-permute-done | bytes 294944 | tf_op jit(solution)/shard_map/ppermute | solution.py:468
  84.9 6.9 %collective-permute-done.24.refs_2_ = bf16[4,2,144,128]{3,2,1,0:T(8,128)(2,1)} collective-permute-done((bf16[4,2,144,128]{3,2,1,0:T(8,128)(2,1)}, bf16[4,2,144,128]{3,2,1,0:T(8,128)(2,1)}, u32[]{:S(2)}, u32[]{:S(2)}) %collective-permute-start.24) | collective-permute-done | bytes 294944 | tf_op jit(solution)/shard_map/ppermute | solution.py:468
  93.5 5.1 %collective-permute-start.6 = (bf16[4,2,144,128]{3,2,1,0:T(8,128)(2,1)}, bf16[4,2,144,128]{3,2,1,0:T(8,128)(2,1)}, u32[]{:S(2)}, u32[]{:S(2)}) collective-permute-start(bf16[4,2,144,128]{3,2,1,0:T(8,128)(2,1)} %get-tuple-element.86), channel_id=1, source_target_pairs={{0,1},{1,0},{2,3},{3,2},{4,5},{5,4},{6,7},{7,6},{8,9},{9,8},{10,11... | collective-permute-start | bytes 884744 | tf_op jit(solution)/shard_map/ppermute | solution.py:468
  100.4 4.1 %collective-permute-done.19.left = bf16[2,576,128]{2,1,0:T(8,128)(2,1)} collective-permute-done((bf16[2,576,128]{2,1,0:T(8,128)(2,1)}, bf16[2,576,128]{2,1,0:T(8,128)(2,1)}, u32[]{:S(2)}, u32[]{:S(2)}) %collective-permute-start.19) | collective-permute-done | bytes 294944 | tf_op jit(solution)/shard_map/ppermute | solution.py:576
  104.4 7.7 %collective-permute-start.7 = (bf16[4,2,144,128]{3,2,1,0:T(8,128)(2,1)}, bf16[4,2,144,128]{3,2,1,0:T(8,128)(2,1)S(1)}, u32[]{:S(2)}, u32[]{:S(2)}) collective-permute-start(bf16[4,2,144,128]{3,2,1,0:T(8,128)(2,1)} %get-tuple-element.87), channel_id=1, source_target_pairs={{0,2},{1,3},{2,0},{3,1},{4,6},{5,7},{6,4},{7,5},{8,10},{9,11},{10,... | collective-permute-start | bytes 884744 | tf_op jit(solution)/shard_map/ppermute | solution.py:468
  121.5 4.1 %filtered.10.refs_4_ = f32[2,576,128]{2,1,0:T(8,128)S(1)} custom-call(bf16[576,1728]{1,0:T(8,128)(2,1)S(1)} %fusion.1.matrix_ref, bf16[4,576,128]{2,1,0:T(8,128)(2,1)} %collective-permute-done.17.left, bf16[4,576,128]{2,1,0:T(8,128)(2,1)} %get-tuple-element.102.first, bf16[4,576,128]{2,1,0:T(8,128)(2,1)} %get-tuple-element.101.last, ...), custom_call_target="tpu_custom_call" | custom-call | flops 2038431744 | bytes 3538944 | tf_op jit(solution)/shard_map/filtered/pallas_call | solution.py:260
  125.6 7.0 %collective-permute-done.7.refs_2_ = bf16[4,2,144,128]{3,2,1,0:T(8,128)(2,1)S(1)} collective-permute-done((bf16[4,2,144,128]{3,2,1,0:T(8,128)(2,1)}, bf16[4,2,144,128]{3,2,1,0:T(8,128)(2,1)S(1)}, u32[]{:S(2)}, u32[]{:S(2)}) %collective-permute-start.7) | collective-permute-done | bytes 294944 | tf_op jit(solution)/shard_map/ppermute | solution.py:468
  137.6 5.8 %collective-permute-done.34.refs_2_ = bf16[2,2,144,128]{3,2,1,0:T(8,128)(2,1)S(1)} collective-permute-done((bf16[2,2,144,128]{3,2,1,0:T(8,128)(2,1)S(1)}, bf16[2,2,144,128]{3,2,1,0:T(8,128)(2,1)S(1)}, u32[]{:S(2)}, u32[]{:S(2)}) %collective-permute-start.34) | collective-permute-done | bytes 147488 | tf_op jit(solution)/shard_map/ppermute | solution.py:468
  143.9 7.1 %collective-permute-done.35.refs_3_ = bf16[2,2,144,128]{3,2,1,0:T(8,128)(2,1)S(1)} collective-permute-done((bf16[2,2,144,128]{3,2,1,0:T(8,128)(2,1)S(1)}, bf16[2,2,144,128]{3,2,1,0:T(8,128)(2,1)S(1)}, u32[]{:S(2)}, u32[]{:S(2)}) %collective-permute-start.35) | collective-permute-done | bytes 147488 | tf_op jit(solution)/shard_map/ppermute | solution.py:468
  150.9 3.6 %collective-permute-start.30 = (bf16[2,2,144,128]{3,2,1,0:T(8,128)(2,1)S(1)}, bf16[2,2,144,128]{3,2,1,0:T(8,128)(2,1)S(1)}, u32[]{:S(2)}, u32[]{:S(2)}) collective-permute-start(bf16[2,2,144,128]{3,2,1,0:T(8,128)(2,1)S(1)} %copy-done.61), channel_id=1, source_target_pairs={{0,1},{1,0},{2,3},{3,2},{4,5},{5,4},{6,7},{7,6},{8,9},{9,8},{10,11... | collective-permute-start | bytes 442376 | tf_op jit(solution)/shard_map/ppermute | solution.py:468
  157.1 3.8 %filtered.11.refs_4_ = f32[2,576,128]{2,1,0:T(8,128)S(1)} custom-call(bf16[576,1728]{1,0:T(8,128)(2,1)S(1)} %fusion.1.matrix_ref, bf16[4,576,128]{2,1,0:T(8,128)(2,1)S(1)} %collective-permute-done.26.left, bf16[4,576,128]{2,1,0:T(8,128)(2,1)S(1)} %get-tuple-element.110.first, bf16[4,576,128]{2,1,0:T(8,128)(2,1)S(1)} %get-tuple-element.109.last, ...), custom_call_target="tpu_custom_call" | custom-call | flops 2038431744 | bytes 3538944 | tf_op jit(solution)/shard_map/filtered/pallas_call | solution.py:260
  162.7 5.5 %collective-permute-done.31.refs_2_ = bf16[2,2,144,128]{3,2,1,0:T(8,128)(2,1)} collective-permute-done((bf16[2,2,144,128]{3,2,1,0:T(8,128)(2,1)}, bf16[2,2,144,128]{3,2,1,0:T(8,128)(2,1)}, u32[]{:S(2)}, u32[]{:S(2)}) %collective-permute-start.31) | collective-permute-done | bytes 147488 | tf_op jit(solution)/shard_map/ppermute | solution.py:468
  172.4 3.4 %collective-permute-start.5 = (bf16[2,2,144,128]{3,2,1,0:T(8,128)(2,1)}, bf16[2,2,144,128]{3,2,1,0:T(8,128)(2,1)S(1)}, u32[]{:S(2)}, u32[]{:S(2)}) collective-permute-start(bf16[2,2,144,128]{3,2,1,0:T(8,128)(2,1)} %get-tuple-element.85), channel_id=1, source_target_pairs={{0,3},{1,2},{2,1},{3,0},{4,7},{5,6},{6,5},{7,4},{8,11},{9,10},{10,... | collective-permute-start | bytes 442376 | tf_op jit(solution)/shard_map/ppermute | solution.py:468
  179.7 4.2 %filtered.12.refs_4_ = f32[2,576,128]{2,1,0:T(8,128)S(1)} custom-call(bf16[576,1728]{1,0:T(8,128)(2,1)S(1)} %fusion.1.matrix_ref, bf16[4,576,128]{2,1,0:T(8,128)(2,1)} %collective-permute-done.21.left, bf16[4,576,128]{2,1,0:T(8,128)(2,1)} %get-tuple-element.105.first, bf16[4,576,128]{2,1,0:T(8,128)(2,1)} %get-tuple-element.104.last, ...), custom_call_target="tpu_custom_call" | custom-call | flops 2038431744 | bytes 3538944 | tf_op jit(solution)/shard_map/filtered/pallas_call | solution.py:260
  205.1 3.6 %collective-permute-done.47 = f32[8,128]{1,0:T(8,128)S(1)} collective-permute-done((f32[8,128]{1,0:T(8,128)S(1)}, f32[8,128]{1,0:T(8,128)S(1)}, u32[]{:S(2)}, u32[]{:S(2)}) %collective-permute-start.47) | collective-permute-done | bytes 4128 | tf_op jit(solution)/shard_map/ppermute | solution.py:500
  208.8 3.4 %collective-permute-done.48 = f32[8,128]{1,0:T(8,128)S(1)} collective-permute-done((f32[8,128]{1,0:T(8,128)S(1)}, f32[8,128]{1,0:T(8,128)S(1)}, u32[]{:S(2)}, u32[]{:S(2)}) %collective-permute-start.48) | collective-permute-done | bytes 4128 | tf_op jit(solution)/shard_map/ppermute | solution.py:500
  212.3 3.6 %collective-permute-done.49 = f32[8,128]{1,0:T(8,128)S(1)} collective-permute-done((f32[8,128]{1,0:T(8,128)S(1)}, f32[8,128]{1,0:T(8,128)S(1)}, u32[]{:S(2)}, u32[]{:S(2)}) %collective-permute-start.49) | collective-permute-done | bytes 4128 | tf_op jit(solution)/shard_map/ppermute | solution.py:500
  (256 shorter events, 106.2 us)
Async XLA Ops:
  3.2 38.2 %collective-permute-start.12 = (bf16[2,2,144,128]{3,2,1,0:T(8,128)(2,1)}, bf16[2,2,144,128]{3,2,1,0:T(8,128)(2,1)S(1)}, u32[]{:S(2)}, u32[]{:S(2)}) collective-permute-start(bf16[2,2,144,128]{3,2,1,0:T(8,128)(2,1)} %get-tuple-element.92), channel_id=1, source_target_pairs={{0,1},{1,0},{2,3},{3,2},{4,5},{5,4},{6,7},{7,6},{8,9},{9,8},{10,11... | collective-permute-start | bytes 442376 | tf_op jit(solution)/shard_map/ppermute | solution.py:468
  8.5 24.0 %collective-permute-start = (bf16[352,128]{1,0:T(8,128)(2,1)S(1)}, bf16[352,128]{1,0:T(8,128)(2,1)S(1)}, u32[]{:S(2)}, u32[]{:S(2)}) collective-permute-start(bf16[352,128]{1,0:T(8,128)(2,1)S(1)} %get-tuple-element.77), channel_id=1, source_target_pairs={{0,1},{1,0},{2,3},{3,2},{4,5},{5,4},{6,7},{7,6},{8,9},{9,8},{10,11... | collective-permute-start | bytes 270344 | tf_op jit(solution)/shard_map/ppermute | solution.py:468
  8.5 26.8 %collective-permute-start.1 = (bf16[352,128]{1,0:T(8,128)(2,1)S(1)}, bf16[352,128]{1,0:T(8,128)(2,1)S(1)}, u32[]{:S(2)}, u32[]{:S(2)}) collective-permute-start(bf16[352,128]{1,0:T(8,128)(2,1)S(1)} %get-tuple-element.78), channel_id=1, source_target_pairs={{0,2},{1,3},{2,0},{3,1},{4,6},{5,7},{6,4},{7,5},{8,10},{9,11},{10,... | collective-permute-start | bytes 270344 | tf_op jit(solution)/shard_map/ppermute | solution.py:468
  11.6 25.2 %collective-permute-start.2 = (bf16[352,128]{1,0:T(8,128)(2,1)S(1)}, bf16[352,128]{1,0:T(8,128)(2,1)S(1)}, u32[]{:S(2)}, u32[]{:S(2)}) collective-permute-start(bf16[352,128]{1,0:T(8,128)(2,1)S(1)} %get-tuple-element.79), channel_id=1, source_target_pairs={{0,3},{1,2},{2,1},{3,0},{4,7},{5,6},{6,5},{7,4},{8,11},{9,10},{10,... | collective-permute-start | bytes 270344 | tf_op jit(solution)/shard_map/ppermute | solution.py:468
  16.9 47.1 %collective-permute-start.9 = (bf16[4,2,144,128]{3,2,1,0:T(8,128)(2,1)}, bf16[4,2,144,128]{3,2,1,0:T(8,128)(2,1)S(1)}, u32[]{:S(2)}, u32[]{:S(2)}) collective-permute-start(bf16[4,2,144,128]{3,2,1,0:T(8,128)(2,1)} %get-tuple-element.89), channel_id=1, source_target_pairs={{0,1},{1,0},{2,3},{3,2},{4,5},{5,4},{6,7},{7,6},{8,9},{9,8},{10,11... | collective-permute-start | bytes 884744 | tf_op jit(solution)/shard_map/ppermute | solution.py:468
  41.4 21.9 %collective-permute-start.16 = (bf16[1,576,128]{2,1,0:T(8,128)(2,1)S(1)}, bf16[1,576,128]{2,1,0:T(8,128)(2,1)S(1)}, u32[]{:S(2)}, u32[]{:S(2)}) collective-permute-start(bf16[1,576,128]{2,1,0:T(8,128)(2,1)S(1)} %get-tuple-element.95.refs_4_.first), channel_id=1, source_target_pairs={{0,28},{4,0},{8,4},{12,8},{16,12},{20,16},{24,20},{28,24},{1,29},{... | collective-permute-start | bytes 442376 | tf_op jit(solution)/shard_map/ppermute | solution.py:577
  45.3 33.9 %collective-permute-start.10 = (bf16[4,2,144,128]{3,2,1,0:T(8,128)(2,1)}, bf16[4,2,144,128]{3,2,1,0:T(8,128)(2,1)}, u32[]{:S(2)}, u32[]{:S(2)}) collective-permute-start(bf16[4,2,144,128]{3,2,1,0:T(8,128)(2,1)} %get-tuple-element.90), channel_id=1, source_target_pairs={{0,2},{1,3},{2,0},{3,1},{4,6},{5,7},{6,4},{7,5},{8,10},{9,11},{10,... | collective-permute-start | bytes 884744 | tf_op jit(solution)/shard_map/ppermute | solution.py:468
  45.6 33.6 %collective-permute-start.11 = (bf16[4,2,144,128]{3,2,1,0:T(8,128)(2,1)}, bf16[4,2,144,128]{3,2,1,0:T(8,128)(2,1)}, u32[]{:S(2)}, u32[]{:S(2)}) collective-permute-start(bf16[4,2,144,128]{3,2,1,0:T(8,128)(2,1)} %get-tuple-element.91), channel_id=1, source_target_pairs={{0,3},{1,2},{2,1},{3,0},{4,7},{5,6},{6,5},{7,4},{8,11},{9,10},{10,... | collective-permute-start | bytes 884744 | tf_op jit(solution)/shard_map/ppermute | solution.py:468
  48.5 36.4 %collective-permute-start.23 = (bf16[4,2,144,128]{3,2,1,0:T(8,128)(2,1)}, bf16[4,2,144,128]{3,2,1,0:T(8,128)(2,1)}, u32[]{:S(2)}, u32[]{:S(2)}) collective-permute-start(bf16[4,2,144,128]{3,2,1,0:T(8,128)(2,1)} %get-tuple-element.106), channel_id=1, source_target_pairs={{0,1},{1,0},{2,3},{3,2},{4,5},{5,4},{6,7},{7,6},{8,9},{9,8},{10,11... | collective-permute-start | bytes 884744 | tf_op jit(solution)/shard_map/ppermute | solution.py:468
  64.0 27.9 %collective-permute-start.24 = (bf16[4,2,144,128]{3,2,1,0:T(8,128)(2,1)}, bf16[4,2,144,128]{3,2,1,0:T(8,128)(2,1)}, u32[]{:S(2)}, u32[]{:S(2)}) collective-permute-start(bf16[4,2,144,128]{3,2,1,0:T(8,128)(2,1)} %get-tuple-element.107), channel_id=1, source_target_pairs={{0,2},{1,3},{2,0},{3,1},{4,6},{5,7},{6,4},{7,5},{8,10},{9,11},{10,... | collective-permute-start | bytes 884744 | tf_op jit(solution)/shard_map/ppermute | solution.py:468
  64.7 28.8 %collective-permute-start.25 = (bf16[4,2,144,128]{3,2,1,0:T(8,128)(2,1)}, bf16[4,2,144,128]{3,2,1,0:T(8,128)(2,1)}, u32[]{:S(2)}, u32[]{:S(2)}) collective-permute-start(bf16[4,2,144,128]{3,2,1,0:T(8,128)(2,1)} %get-tuple-element.108), channel_id=1, source_target_pairs={{0,3},{1,2},{2,1},{3,0},{4,7},{5,6},{6,5},{7,4},{8,11},{9,10},{10,... | collective-permute-start | bytes 884744 | tf_op jit(solution)/shard_map/ppermute | solution.py:468
  82.3 36.2 %collective-permute-start.17 = (bf16[4,576,128]{2,1,0:T(8,128)(2,1)}, bf16[4,576,128]{2,1,0:T(8,128)(2,1)}, u32[]{:S(2)}, u32[]{:S(2)}) collective-permute-start(bf16[4,576,128]{2,1,0:T(8,128)(2,1)} %get-tuple-element.101.last), channel_id=1, source_target_pairs={{0,4},{4,8},{8,12},{12,16},{16,20},{20,24},{24,28},{28,0},{1,5},{5... | collective-permute-start | bytes 1769480 | tf_op jit(solution)/shard_map/ppermute | solution.py:576
  82.3 38.8 %collective-permute-start.18 = (bf16[4,576,128]{2,1,0:T(8,128)(2,1)}, bf16[4,576,128]{2,1,0:T(8,128)(2,1)}, u32[]{:S(2)}, u32[]{:S(2)}) collective-permute-start(bf16[4,576,128]{2,1,0:T(8,128)(2,1)} %get-tuple-element.102.first), channel_id=1, source_target_pairs={{0,28},{4,0},{8,4},{12,8},{16,12},{20,16},{24,20},{28,24},{1,29},{... | collective-permute-start | bytes 1769480 | tf_op jit(solution)/shard_map/ppermute | solution.py:577
  84.9 19.5 %collective-permute-start.19 = (bf16[2,576,128]{2,1,0:T(8,128)(2,1)}, bf16[2,576,128]{2,1,0:T(8,128)(2,1)}, u32[]{:S(2)}, u32[]{:S(2)}) collective-permute-start(bf16[2,576,128]{2,1,0:T(8,128)(2,1)} %get-tuple-element.103.last), channel_id=1, source_target_pairs={{0,4},{4,8},{8,12},{12,16},{16,20},{20,24},{24,28},{28,0},{1,5},{5... | collective-permute-start | bytes 884744 | tf_op jit(solution)/shard_map/ppermute | solution.py:576
  91.8 20.3 %collective-permute-start.20 = (bf16[2,576,128]{2,1,0:T(8,128)(2,1)}, bf16[2,576,128]{2,1,0:T(8,128)(2,1)}, u32[]{:S(2)}, u32[]{:S(2)}) collective-permute-start(bf16[2,576,128]{2,1,0:T(8,128)(2,1)} %get-tuple-element.96.refs_4_.first), channel_id=1, source_target_pairs={{0,28},{4,0},{8,4},{12,8},{16,12},{20,16},{24,20},{28,24},{1,29},{... | collective-permute-start | bytes 884744 | tf_op jit(solution)/shard_map/ppermute | solution.py:577
  93.5 24.8 %collective-permute-start.6 = (bf16[4,2,144,128]{3,2,1,0:T(8,128)(2,1)}, bf16[4,2,144,128]{3,2,1,0:T(8,128)(2,1)}, u32[]{:S(2)}, u32[]{:S(2)}) collective-permute-start(bf16[4,2,144,128]{3,2,1,0:T(8,128)(2,1)} %get-tuple-element.86), channel_id=1, source_target_pairs={{0,1},{1,0},{2,3},{3,2},{4,5},{5,4},{6,7},{7,6},{8,9},{9,8},{10,11... | collective-permute-start | bytes 884744 | tf_op jit(solution)/shard_map/ppermute | solution.py:468
  104.4 28.2 %collective-permute-start.7 = (bf16[4,2,144,128]{3,2,1,0:T(8,128)(2,1)}, bf16[4,2,144,128]{3,2,1,0:T(8,128)(2,1)S(1)}, u32[]{:S(2)}, u32[]{:S(2)}) collective-permute-start(bf16[4,2,144,128]{3,2,1,0:T(8,128)(2,1)} %get-tuple-element.87), channel_id=1, source_target_pairs={{0,2},{1,3},{2,0},{3,1},{4,6},{5,7},{6,4},{7,5},{8,10},{9,11},{10,... | collective-permute-start | bytes 884744 | tf_op jit(solution)/shard_map/ppermute | solution.py:468
  112.1 20.5 %collective-permute-start.8 = (bf16[4,2,144,128]{3,2,1,0:T(8,128)(2,1)}, bf16[4,2,144,128]{3,2,1,0:T(8,128)(2,1)S(1)}, u32[]{:S(2)}, u32[]{:S(2)}) collective-permute-start(bf16[4,2,144,128]{3,2,1,0:T(8,128)(2,1)} %get-tuple-element.88), channel_id=1, source_target_pairs={{0,3},{1,2},{2,1},{3,0},{4,7},{5,6},{6,5},{7,4},{8,11},{9,10},{10,... | collective-permute-start | bytes 884744 | tf_op jit(solution)/shard_map/ppermute | solution.py:468
  118.4 36.2 %collective-permute-start.26 = (bf16[4,576,128]{2,1,0:T(8,128)(2,1)S(1)}, bf16[4,576,128]{2,1,0:T(8,128)(2,1)S(1)}, u32[]{:S(2)}, u32[]{:S(2)}) collective-permute-start(bf16[4,576,128]{2,1,0:T(8,128)(2,1)S(1)} %get-tuple-element.109.last), channel_id=1, source_target_pairs={{0,4},{4,8},{8,12},{12,16},{16,20},{20,24},{24,28},{28,0},{1,5},{5... | collective-permute-start | bytes 1769480 | tf_op jit(solution)/shard_map/ppermute | solution.py:576
  118.5 36.1 %collective-permute-start.27 = (bf16[4,576,128]{2,1,0:T(8,128)(2,1)S(1)}, bf16[4,576,128]{2,1,0:T(8,128)(2,1)S(1)}, u32[]{:S(2)}, u32[]{:S(2)}) collective-permute-start(bf16[4,576,128]{2,1,0:T(8,128)(2,1)S(1)} %get-tuple-element.110.first), channel_id=1, source_target_pairs={{0,28},{4,0},{8,4},{12,8},{16,12},{20,16},{24,20},{28,24},{1,29},{... | collective-permute-start | bytes 1769480 | tf_op jit(solution)/shard_map/ppermute | solution.py:577
  134.9 37.4 %collective-permute-start.21 = (bf16[4,576,128]{2,1,0:T(8,128)(2,1)}, bf16[4,576,128]{2,1,0:T(8,128)(2,1)}, u32[]{:S(2)}, u32[]{:S(2)}) collective-permute-start(bf16[4,576,128]{2,1,0:T(8,128)(2,1)} %get-tuple-element.104.last), channel_id=1, source_target_pairs={{0,4},{4,8},{8,12},{12,16},{16,20},{20,24},{24,28},{28,0},{1,5},{5... | collective-permute-start | bytes 1769480 | tf_op jit(solution)/shard_map/ppermute | solution.py:576
  134.9 40.8 %collective-permute-start.22 = (bf16[4,576,128]{2,1,0:T(8,128)(2,1)}, bf16[4,576,128]{2,1,0:T(8,128)(2,1)}, u32[]{:S(2)}, u32[]{:S(2)}) collective-permute-start(bf16[4,576,128]{2,1,0:T(8,128)(2,1)} %get-tuple-element.105.first), channel_id=1, source_target_pairs={{0,28},{4,0},{8,4},{12,8},{16,12},{20,16},{24,20},{28,24},{1,29},{... | collective-permute-start | bytes 1769480 | tf_op jit(solution)/shard_map/ppermute | solution.py:577
  162.7 24.2 %collective-permute-start.38 = (bf16[2,576,128]{2,1,0:T(8,128)(2,1)}, bf16[2,576,128]{2,1,0:T(8,128)(2,1)}, u32[]{:S(2)}, u32[]{:S(2)}) collective-permute-start(bf16[2,576,128]{2,1,0:T(8,128)(2,1)} %get-tuple-element.122.last), channel_id=1, source_target_pairs={{0,4},{4,8},{8,12},{12,16},{16,20},{20,24},{24,28},{28,0},{1,5},{5... | collective-permute-start | bytes 884744 | tf_op jit(solution)/shard_map/ppermute | solution.py:576
  168.2 16.3 %collective-permute-start.4 = (bf16[2,2,144,128]{3,2,1,0:T(8,128)(2,1)}, bf16[2,2,144,128]{3,2,1,0:T(8,128)(2,1)S(1)}, u32[]{:S(2)}, u32[]{:S(2)}) collective-permute-start(bf16[2,2,144,128]{3,2,1,0:T(8,128)(2,1)} %get-tuple-element.84), channel_id=1, source_target_pairs={{0,2},{1,3},{2,0},{3,1},{4,6},{5,7},{6,4},{7,5},{8,10},{9,11},{10,... | collective-permute-start | bytes 442376 | tf_op jit(solution)/shard_map/ppermute | solution.py:468
  (95 other events, 899.4 us)

commit v3 on v2

--- a/solution.py
+++ b/solution.py
@@ -347,29 +347,44 @@
     return dot(a_high, high) + (dot(a_low, high) + dot(a_high, low))
 
 
-def observe_kernel(
-    parts, halves, lat_blocks, blocks_ref, *refs
+def vert_kernel(*refs):
+    *verts, out = refs
+    lanes = verts[0].shape[1]
+    piece = out.shape[0] // len(verts)
+    for s, ref in enumerate(verts):
+        rows = ref[...].astype(f32)
+        for t in range(out.shape[1] // lanes):
+            here = slice(t * piece, (t + 1) * piece)
+            out[s * piece : (s + 1) * piece, t * lanes : (t + 1) * lanes] = rows[here]
+
+
+def join_vert(verts, levels, slots):
+    return pl.pallas_call(
+        vert_kernel,
+        in_specs=[vmem()] * len(verts),
+        out_specs=vmem(),
+        out_shape=jax.ShapeDtypeStruct((len(verts) * levels, slots), f32),
+        cost_estimate=cost(1e6, 1e6),
+        compiler_params=params(),
+        name="join_vert",
+    )(*verts)
+
+
+def block_picks(ids, halves, block_rows, lat_blocks):
+    base = lax.axis_index("lev") * block_rows
+    return [[ids == h * lat_blocks + base + b for b in range(block_rows)] for h in range(halves)]
+
+
+def depart_kernel(
+    halves, lat_blocks, blocks_ref, vert_ref, high_t, low_t, ids_ref, value_ref, rinv_ref,
+    dep_ref, share_ref
 ):
-    verts, (
-        high, low, high_t, low_t, ids_ref, value_ref, rinv_ref, share_ref, *outs, vert_ref
-    ) = refs[:parts], refs[parts:]
     block_rows, stacked, cells = blocks_ref.shape
     levels = stacked // halves
-    piece = levels // parts
-    base = lax.axis_index("lev") * block_rows
-    ids = ids_ref[...]
-    for s, ref in enumerate(verts):
-        rows = ref[...].astype(f32)
-        for t in range(rows.shape[0] // piece):
-            vert_ref[s * piece : (s + 1) * piece, t * cells : (t + 1) * cells] = rows[
-                t * piece : (t + 1) * piece
-            ]
     vert = vert_ref[...]
-    picks = [
-        [ids == h * lat_blocks + base + b for b in range(block_rows)] for h in range(halves)
-    ]
+    picks = block_picks(ids_ref[...], halves, block_rows, lat_blocks)
     mine = None
-    hx = jnp.zeros(ids.shape, f32)
+    hx = jnp.zeros(ids_ref.shape, f32)
     for b in range(block_rows):
         projected = product3(blocks_ref[b], high_t[...], low_t[...])
         for h in range(halves):
@@ -378,19 +393,30 @@
             mine = picks[h][b] if mine is None else mine | picks[h][b]
     miss = hx - value_ref[...]
     dep = jnp.where(mine, rinv_ref[...] * miss, 0.0)
+    dep_ref[...] = dep
     total = 0.5 * jnp.sum(dep * miss, axis=1, keepdims=True)
-    slot = lax.axis_index("lon") * parts + lax.axis_index("lev")
+    slot = lax.axis_index("lon") * lax.axis_size("lev") + lax.axis_index("lev")
     spot = lax.broadcasted_iota(jnp.int32, share_ref.shape, 0) * cells
     spot = spot + lax.broadcasted_iota(jnp.int32, share_ref.shape, 1)
     share_ref[...] = jnp.where(spot == slot, jnp.broadcast_to(total, share_ref.shape), 0.0)
+
+
+def adjoint_kernel(
+    parts, halves, lat_blocks, blocks_ref, vert_ref, high, low, ids_ref, dep_ref, *outs
+):
+    block_rows, stacked, _ = blocks_ref.shape
+    levels = stacked // halves
+    piece = levels // parts
+    vert = vert_ref[...]
+    dep = dep_ref[...]
+    picks = block_picks(ids_ref[...], halves, block_rows, lat_blocks)
     both = [[], []]
     for b in range(block_rows):
         weights = jnp.concatenate(
             [vert * jnp.where(picks[h][b], dep, 0.0) for h in range(halves)], axis=0
         )
-        adjoint = product3(weights, high[...], low[...])
         both[0].append(blocks_ref[b])
-        both[1].append(adjoint)
+        both[1].append(product3(weights, high[...], low[...]))
     for s, ref in enumerate(outs):
         pieces = [
             x[h * levels + s * piece : h * levels + (s + 1) * piece]
@@ -401,20 +427,32 @@
         ref[...] = jnp.concatenate(pieces, axis=0).astype(bf16)
 
 
-def observe(blocks, verts, horiz, ids, value, rinv, parts, halves, lat_blocks):
+def observe(blocks, vert, horiz, ids, value, rinv, parts, halves, lat_blocks):
+    high, low, high_t, low_t = horiz
     block_rows, stacked, cells = blocks.shape
+    dep, share = pl.pallas_call(
+        functools.partial(depart_kernel, halves, lat_blocks),
+        in_specs=[vmem()] * 7,
+        out_specs=[vmem()] * 2,
+        out_shape=[
+            jax.ShapeDtypeStruct(ids.shape, f32),
+            jax.ShapeDtypeStruct((8, cells), f32),
+        ],
+        cost_estimate=cost(1e9, 4e6),
+        compiler_params=params(),
+        name="depart",
+    )(blocks, vert, high_t, low_t, ids, value, rinv)
     back = jax.ShapeDtypeStruct((2 * block_rows * stacked // parts, cells), bf16)
-    share = jax.ShapeDtypeStruct((8, 128), f32)
-    return pl.pallas_call(
-        functools.partial(observe_kernel, parts, halves, lat_blocks),
-        in_specs=[vmem()] * (8 + len(verts)),
-        scratch_shapes=[pltpu.VMEM((stacked // halves, ids.shape[1]), f32)],
-        out_specs=[vmem()] * (parts + 1),
-        out_shape=[share] + [back] * parts,
+    backs = pl.pallas_call(
+        functools.partial(adjoint_kernel, parts, halves, lat_blocks),
+        in_specs=[vmem()] * 6,
+        out_specs=[vmem()] * parts,
+        out_shape=[back] * parts,
         cost_estimate=cost(1e9, 4e6),
         compiler_params=params(),
-        name="observe",
-    )(blocks, *verts, *horiz, ids, value, rinv)
+        name="adjoint",
+    )(blocks, vert, high, low, ids, dep)
+    return share, backs
 
 
 def unpack_kernel(halves, levels, *refs):
@@ -595,8 +633,8 @@
 
     nblk = columns // block_lon * lat_blocks
     ids = jnp.where(obs_block >= 0, obs_block - lax.axis_index("lon") * nblk, -1)
-    share, *backs = observe(
-        blocks, verts, horiz, ids[None], obs_value[None], obs_rinv[None],
+    share, backs = observe(
+        blocks, join_vert(verts, levels, slots), horiz, ids[None], obs_value[None], obs_rinv[None],
         parts, halves, lat_blocks,
     )
     backs = exchange(backs)

time: 227 us -> 240 us (1.057)
  waiting for transfers between devices: 59.1 us -> 73 us
  local copies, waits for them, and re-layouts: 20.6 us -> 25.2 us
  starting transfers between devices: 82.3 us -> 78.1 us
    ppermute x30, waiting for transfers between devices: 40 us -> 56 us  [exchange(): lax.ppermute(blocks[place], 'lev', [(i, i ^ place) for i in range(count)])]
    ppermute x30, starting transfers between devices: 64.4 us -> 58.3 us  [exchange(): lax.ppermute(blocks[place], 'lev', [(i, i ^ place) for i in range(count)])]
    unnamed x137 -> x159, local copies, waits for them, and re-layouts: 20.6 us -> 25.2 us
    ppermute x5, starting transfers between devices: 0.24 us -> 4.44 us  [total_of(): x = x + lax.ppermute(x, axis, pairs)]
    ppermute x5, waiting for transfers between devices: 11.9 us -> 9.23 us  [total_of(): x = x + lax.ppermute(x, axis, pairs)]
  transfers between devices with their start and end apart: 51 -> 51, of which waited for: 17 -> 17; matrix products, arithmetic and copies ran while one was open for 2% -> 2% of each run, Pallas kernels for 24% -> 21%
where the time goes in v3:
time: 240 us; the launch traced here: 239 us
  starting transfers between devices  78.1 us (33%)
  waiting for transfers between devices  73 us (30%)
  Pallas kernels  57.5 us (24%)
  local copies, waits for them, and re-layouts  25.2 us (10%)
  matrix products  3.28 us (1%)
    ppermute x30, starting transfers between devices, exchange(): lax.ppermute(blocks[place], 'lev', [(i, i ^ place) for i in range(count)])  58.3 us
    ppermute x30, waiting for transfers between devices, exchange(): lax.ppermute(blocks[place], 'lev', [(i, i ^ place) for i in range(count)])  56 us
    unnamed x159, local copies, waits for them, and re-layouts  25.2 us
    pallas_call x8, Pallas kernels, filtered(): pl.pallas_call(functools.partial(filter_kernel, pair, total is not None),...  22.2 us
    pallas_call x7, Pallas kernels, pack(): pl.pallas_call(functools.partial(pack_kernel, parts, halves), grid=(count...  21.7 us
    ppermute x8, starting transfers between devices, halo(): right = lax.ppermute(first, 'lon', shift_by('lon', -1))  15.2 us
    ppermute x5, waiting for transfers between devices, total_of(): x = x + lax.ppermute(x, axis, pairs)  9.23 us
    pallas_call x7, Pallas kernels, product(): pl.pallas_call(functools.partial(product_kernel, parts), grid=(count // s...  7.88 us
  transfers between devices with their start and end apart: 51, of which 17 were waited for; matrix products, arithmetic and copies ran while one was open for 2% of the time, Pallas kernels for 21%

profile of v3, /device:TPU:0, one launch (start us, length us, event | category | flops | bytes accessed | tf_op | source)
XLA Modules:
  0.0 239.2 jit_solution(12531631089841561561)
XLA Ops:
  6.3 3.1 %collective-permute-start = (bf16[352,128]{1,0:T(8,128)(2,1)S(1)}, bf16[352,128]{1,0:T(8,128)(2,1)S(1)}, u32[]{:S(2)}, u32[]{:S(2)}) collective-permute-start(bf16[352,128]{1,0:T(8,128)(2,1)S(1)} %get-tuple-element.78), channel_id=1, source_target_pairs={{0,1},{1,0},{2,3},{3,2},{4,5},{5,4},{6,7},{7,6},{8,9},{9,8},{10,11... | collective-permute-start | bytes 270344 | tf_op jit(solution)/shard_map/ppermute | solution.py:506
  11.9 4.0 %pack.8 = (bf16[4,2,144,128]{3,2,1,0:T(8,128)(2,1)}, bf16[4,2,144,128]{3,2,1,0:T(8,128)(2,1)}, bf16[4,2,144,128]{3,2,1,0:T(8,128)(2,1)}, bf16[4,2,144,128]{3,2,1,0:T(8,128)(2,1)}) custom-call(bf16[80,18,16,128]{3,2,1,0:T(8,128)(2,1)} %ens_ref.13, bf16[352,128]{1,0:T(8,128)(2,1)} %copy-done.39), custom_call_target="tpu_custom_call" | custom-call | flops 16000000 | bytes 2359296 | tf_op jit(solution)/shard_map/pack/pallas_call | solution.py:80
  15.9 4.0 %pack.9 = (bf16[4,2,144,128]{3,2,1,0:T(8,128)(2,1)}, bf16[4,2,144,128]{3,2,1,0:T(8,128)(2,1)}, bf16[4,2,144,128]{3,2,1,0:T(8,128)(2,1)}, bf16[4,2,144,128]{3,2,1,0:T(8,128)(2,1)}) custom-call(bf16[80,18,16,128]{3,2,1,0:T(8,128)(2,1)} %ens_ref.13, bf16[4,2,144,128]{3,2,1,0:T(8,128)(2,1)} %get-tuple-element.72.after.refs_0_), custom_call_target="tpu_custom_call" | custom-call | flops 16000000 | bytes 2359296 | tf_op jit(solution)/shard_map/pack/pallas_call | solution.py:80
  19.9 4.0 %pack.10 = (bf16[4,2,144,128]{3,2,1,0:T(8,128)(2,1)}, bf16[4,2,144,128]{3,2,1,0:T(8,128)(2,1)}, bf16[4,2,144,128]{3,2,1,0:T(8,128)(2,1)}, bf16[4,2,144,128]{3,2,1,0:T(8,128)(2,1)}) custom-call(bf16[80,18,16,128]{3,2,1,0:T(8,128)(2,1)} %ens_ref.13, bf16[4,2,144,128]{3,2,1,0:T(8,128)(2,1)} %get-tuple-element.73.after.refs_0_), custom_call_target="tpu_custom_call" | custom-call | flops 16000000 | bytes 2359296 | tf_op jit(solution)/shard_map/pack/pallas_call | solution.py:80
  37.2 5.9 %collective-permute-done.2.refs_3_ = bf16[352,128]{1,0:T(8,128)(2,1)S(1)} collective-permute-done((bf16[352,128]{1,0:T(8,128)(2,1)S(1)}, bf16[352,128]{1,0:T(8,128)(2,1)S(1)}, u32[]{:S(2)}, u32[]{:S(2)}) %collective-permute-start.2) | collective-permute-done | bytes 90144 | tf_op jit(solution)/shard_map/ppermute | solution.py:506
  43.9 3.0 %collective-permute-start.10 = (bf16[4,2,144,128]{3,2,1,0:T(8,128)(2,1)}, bf16[4,2,144,128]{3,2,1,0:T(8,128)(2,1)S(1)}, u32[]{:S(2)}, u32[]{:S(2)}) collective-permute-start(bf16[4,2,144,128]{3,2,1,0:T(8,128)(2,1)} %get-tuple-element.91), channel_id=1, source_target_pairs={{0,2},{1,3},{2,0},{3,1},{4,6},{5,7},{6,4},{7,5},{8,10},{9,11},{10,... | collective-permute-start | bytes 884744 | tf_op jit(solution)/shard_map/ppermute | solution.py:506
  57.8 3.0 %collective-permute-start.24 = (bf16[4,2,144,128]{3,2,1,0:T(8,128)(2,1)}, bf16[4,2,144,128]{3,2,1,0:T(8,128)(2,1)}, u32[]{:S(2)}, u32[]{:S(2)}) collective-permute-start(bf16[4,2,144,128]{3,2,1,0:T(8,128)(2,1)} %get-tuple-element.108), channel_id=1, source_target_pairs={{0,2},{1,3},{2,0},{3,1},{4,6},{5,7},{6,4},{7,5},{8,10},{9,11},{10,... | collective-permute-start | bytes 884744 | tf_op jit(solution)/shard_map/ppermute | solution.py:506
  63.0 9.8 %collective-permute-done.10.refs_2_ = bf16[4,2,144,128]{3,2,1,0:T(8,128)(2,1)S(1)} collective-permute-done((bf16[4,2,144,128]{3,2,1,0:T(8,128)(2,1)}, bf16[4,2,144,128]{3,2,1,0:T(8,128)(2,1)S(1)}, u32[]{:S(2)}, u32[]{:S(2)}) %collective-permute-start.10) | collective-permute-done | bytes 294944 | tf_op jit(solution)/shard_map/ppermute | solution.py:506
  89.5 8.0 %collective-permute-done.24.refs_2_ = bf16[4,2,144,128]{3,2,1,0:T(8,128)(2,1)} collective-permute-done((bf16[4,2,144,128]{3,2,1,0:T(8,128)(2,1)}, bf16[4,2,144,128]{3,2,1,0:T(8,128)(2,1)}, u32[]{:S(2)}, u32[]{:S(2)}) %collective-permute-start.24) | collective-permute-done | bytes 294944 | tf_op jit(solution)/shard_map/ppermute | solution.py:506
  97.5 10.1 %collective-permute-start.6 = (bf16[4,2,144,128]{3,2,1,0:T(8,128)(2,1)}, bf16[4,2,144,128]{3,2,1,0:T(8,128)(2,1)}, u32[]{:S(2)}, u32[]{:S(2)}) collective-permute-start(bf16[4,2,144,128]{3,2,1,0:T(8,128)(2,1)} %get-tuple-element.87), channel_id=1, source_target_pairs={{0,1},{1,0},{2,3},{3,2},{4,5},{5,4},{6,7},{7,6},{8,9},{9,8},{10,11... | collective-permute-start | bytes 884744 | tf_op jit(solution)/shard_map/ppermute | solution.py:506
  113.7 2.7 %filtered.9.refs_4_ = f32[2,576,128]{2,1,0:T(8,128)S(1)} custom-call(bf16[576,1728]{1,0:T(8,128)(2,1)S(1)} %fusion.1.matrix_ref, bf16[2,576,128]{2,1,0:T(8,128)(2,1)} %collective-permute-done.19.left, bf16[2,576,128]{2,1,0:T(8,128)(2,1)} %get-tuple-element.97.refs_4_.first, bf16[2,576,128]{2,1,0:T(8,128)(2,1)} %get-tuple-element.104.last, ...), custom_call_target="tpu_custom_call" | custom-call | flops 1019215872 | bytes 1769472 | tf_op jit(solution)/shard_map/filtered/pallas_call | solution.py:260
  119.3 12.1 %collective-permute-done.7.refs_2_ = bf16[4,2,144,128]{3,2,1,0:T(8,128)(2,1)} collective-permute-done((bf16[4,2,144,128]{3,2,1,0:T(8,128)(2,1)}, bf16[4,2,144,128]{3,2,1,0:T(8,128)(2,1)}, u32[]{:S(2)}, u32[]{:S(2)}) %collective-permute-start.7) | collective-permute-done | bytes 294944 | tf_op jit(solution)/shard_map/ppermute | solution.py:506
  131.4 4.7 %collective-permute-start.30 = (bf16[2,2,144,128]{3,2,1,0:T(8,128)(2,1)S(1)}, bf16[2,2,144,128]{3,2,1,0:T(8,128)(2,1)S(1)}, u32[]{:S(2)}, u32[]{:S(2)}) collective-permute-start(bf16[2,2,144,128]{3,2,1,0:T(8,128)(2,1)S(1)} %copy-done.74), channel_id=1, source_target_pairs={{0,1},{1,0},{2,3},{3,2},{4,5},{5,4},{6,7},{7,6},{8,9},{9,8},{10,11... | collective-permute-start | bytes 442376 | tf_op jit(solution)/shard_map/ppermute | solution.py:506
  139.1 4.0 %filtered.10.refs_4_ = f32[2,576,128]{2,1,0:T(8,128)S(1)} custom-call(bf16[576,1728]{1,0:T(8,128)(2,1)S(1)} %fusion.1.matrix_ref, bf16[4,576,128]{2,1,0:T(8,128)(2,1)} %collective-permute-done.17.left, bf16[4,576,128]{2,1,0:T(8,128)(2,1)} %get-tuple-element.103.first, bf16[4,576,128]{2,1,0:T(8,128)(2,1)} %get-tuple-element.102.last, ...), custom_call_target="tpu_custom_call" | custom-call | flops 2038431744 | bytes 3538944 | tf_op jit(solution)/shard_map/filtered/pallas_call | solution.py:260
  148.8 7.4 %collective-permute-done.34.refs_2_ = bf16[2,2,144,128]{3,2,1,0:T(8,128)(2,1)S(1)} collective-permute-done((bf16[2,2,144,128]{3,2,1,0:T(8,128)(2,1)S(1)}, bf16[2,2,144,128]{3,2,1,0:T(8,128)(2,1)S(1)}, u32[]{:S(2)}, u32[]{:S(2)}) %collective-permute-start.34) | collective-permute-done | bytes 147488 | tf_op jit(solution)/shard_map/ppermute | solution.py:506
  156.2 8.6 %collective-permute-done.35.refs_3_ = bf16[2,2,144,128]{3,2,1,0:T(8,128)(2,1)S(1)} collective-permute-done((bf16[2,2,144,128]{3,2,1,0:T(8,128)(2,1)S(1)}, bf16[2,2,144,128]{3,2,1,0:T(8,128)(2,1)S(1)}, u32[]{:S(2)}, u32[]{:S(2)}) %collective-permute-start.35) | collective-permute-done | bytes 147488 | tf_op jit(solution)/shard_map/ppermute | solution.py:506
  164.8 3.3 %collective-permute-start.4 = (bf16[2,2,144,128]{3,2,1,0:T(8,128)(2,1)}, bf16[2,2,144,128]{3,2,1,0:T(8,128)(2,1)}, u32[]{:S(2)}, u32[]{:S(2)}) collective-permute-start(bf16[2,2,144,128]{3,2,1,0:T(8,128)(2,1)} %get-tuple-element.85), channel_id=1, source_target_pairs={{0,2},{1,3},{2,0},{3,1},{4,6},{5,7},{6,4},{7,5},{8,10},{9,11},{10,... | collective-permute-start | bytes 442376 | tf_op jit(solution)/shard_map/ppermute | solution.py:506
  168.6 3.4 %collective-permute-start.32 = (bf16[2,2,144,128]{3,2,1,0:T(8,128)(2,1)S(1)}, bf16[2,2,144,128]{3,2,1,0:T(8,128)(2,1)S(1)}, u32[]{:S(2)}, u32[]{:S(2)}) collective-permute-start(bf16[2,2,144,128]{3,2,1,0:T(8,128)(2,1)S(1)} %copy-done.69), channel_id=1, source_target_pairs={{0,3},{1,2},{2,1},{3,0},{4,7},{5,6},{6,5},{7,4},{8,11},{9,10},{10,... | collective-permute-start | bytes 442376 | tf_op jit(solution)/shard_map/ppermute | solution.py:506
  172.0 3.8 %filtered.11.refs_4_ = f32[2,576,128]{2,1,0:T(8,128)S(1)} custom-call(bf16[576,1728]{1,0:T(8,128)(2,1)S(1)} %fusion.1.matrix_ref, bf16[4,576,128]{2,1,0:T(8,128)(2,1)S(1)} %collective-permute-done.26.left, bf16[4,576,128]{2,1,0:T(8,128)(2,1)S(1)} %get-tuple-element.111.first, bf16[4,576,128]{2,1,0:T(8,128)(2,1)S(1)} %get-tuple-element.110.last, ...), custom_call_target="tpu_custom_call" | custom-call | flops 2038431744 | bytes 3538944 | tf_op jit(solution)/shard_map/filtered/pallas_call | solution.py:260
  180.5 3.3 %collective-permute-start.40 = (bf16[144,128]{1,0:T(8,128)(2,1)}, bf16[144,128]{1,0:T(8,128)(2,1)S(1)}, u32[]{:S(2)}, u32[]{:S(2)}) collective-permute-start(bf16[144,128]{1,0:T(8,128)(2,1)} %copy-done.59), channel_id=1, source_target_pairs={{0,1},{1,0},{2,3},{3,2},{4,5},{5,4},{6,7},{7,6},{8,9},{9,8},{10,11... | collective-permute-start | bytes 110600 | tf_op jit(solution)/shard_map/ppermute | solution.py:506
  190.6 4.2 %filtered.12.refs_4_ = f32[2,576,128]{2,1,0:T(8,128)S(1)} custom-call(bf16[576,1728]{1,0:T(8,128)(2,1)S(1)} %fusion.1.matrix_ref, bf16[4,576,128]{2,1,0:T(8,128)(2,1)} %collective-permute-done.21.left, bf16[4,576,128]{2,1,0:T(8,128)(2,1)} %get-tuple-element.106.first, bf16[4,576,128]{2,1,0:T(8,128)(2,1)} %get-tuple-element.105.last, ...), custom_call_target="tpu_custom_call" | custom-call | flops 2038431744 | bytes 3538944 | tf_op jit(solution)/shard_map/filtered/pallas_call | solution.py:260
  207.4 4.7 %collective-permute-done.28.left = bf16[2,576,128]{2,1,0:T(8,128)(2,1)S(1)} collective-permute-done((bf16[2,576,128]{2,1,0:T(8,128)(2,1)S(1)}, bf16[2,576,128]{2,1,0:T(8,128)(2,1)S(1)}, u32[]{:S(2)}, u32[]{:S(2)}) %collective-permute-start.28) | collective-permute-done | bytes 294944 | tf_op jit(solution)/shard_map/ppermute | solution.py:614
  217.3 3.5 %collective-permute-done.47 = f32[8,128]{1,0:T(8,128)S(1)} collective-permute-done((f32[8,128]{1,0:T(8,128)S(1)}, f32[8,128]{1,0:T(8,128)S(1)}, u32[]{:S(2)}, u32[]{:S(2)}) %collective-permute-start.47) | collective-permute-done | bytes 4128 | tf_op jit(solution)/shard_map/ppermute | solution.py:538
  225.0 3.1 %collective-permute-done.49 = f32[8,128]{1,0:T(8,128)S(1)} collective-permute-done((f32[8,128]{1,0:T(8,128)S(1)}, f32[8,128]{1,0:T(8,128)S(1)}, u32[]{:S(2)}, u32[]{:S(2)}) %collective-permute-start.49) | collective-permute-done | bytes 4128 | tf_op jit(solution)/shard_map/ppermute | solution.py:538
  (280 shorter events, 113.9 us)
Async XLA Ops:
  6.3 27.0 %collective-permute-start = (bf16[352,128]{1,0:T(8,128)(2,1)S(1)}, bf16[352,128]{1,0:T(8,128)(2,1)S(1)}, u32[]{:S(2)}, u32[]{:S(2)}) collective-permute-start(bf16[352,128]{1,0:T(8,128)(2,1)S(1)} %get-tuple-element.78), channel_id=1, source_target_pairs={{0,1},{1,0},{2,3},{3,2},{4,5},{5,4},{6,7},{7,6},{8,9},{9,8},{10,11... | collective-permute-start | bytes 270344 | tf_op jit(solution)/shard_map/ppermute | solution.py:506
  9.3 25.9 %collective-permute-start.1 = (bf16[352,128]{1,0:T(8,128)(2,1)S(1)}, bf16[352,128]{1,0:T(8,128)(2,1)S(1)}, u32[]{:S(2)}, u32[]{:S(2)}) collective-permute-start(bf16[352,128]{1,0:T(8,128)(2,1)S(1)} %get-tuple-element.79), channel_id=1, source_target_pairs={{0,2},{1,3},{2,0},{3,1},{4,6},{5,7},{6,4},{7,5},{8,10},{9,11},{10,... | collective-permute-start | bytes 270344 | tf_op jit(solution)/shard_map/ppermute | solution.py:506
  33.3 17.7 %collective-permute-start.13 = (bf16[2,2,144,128]{3,2,1,0:T(8,128)(2,1)S(1)}, bf16[2,2,144,128]{3,2,1,0:T(8,128)(2,1)S(1)}, u32[]{:S(2)}, u32[]{:S(2)}) collective-permute-start(bf16[2,2,144,128]{3,2,1,0:T(8,128)(2,1)S(1)} %copy-done.76), channel_id=1, source_target_pairs={{0,2},{1,3},{2,0},{3,1},{4,6},{5,7},{6,4},{7,5},{8,10},{9,11},{10,... | collective-permute-start | bytes 442376 | tf_op jit(solution)/shard_map/ppermute | solution.py:506
  35.2 15.8 %collective-permute-start.14 = (bf16[2,2,144,128]{3,2,1,0:T(8,128)(2,1)S(1)}, bf16[2,2,144,128]{3,2,1,0:T(8,128)(2,1)S(1)}, u32[]{:S(2)}, u32[]{:S(2)}) collective-permute-start(bf16[2,2,144,128]{3,2,1,0:T(8,128)(2,1)S(1)} %copy-done.75), channel_id=1, source_target_pairs={{0,3},{1,2},{2,1},{3,0},{4,7},{5,6},{6,5},{7,4},{8,11},{9,10},{10,... | collective-permute-start | bytes 442376 | tf_op jit(solution)/shard_map/ppermute | solution.py:506
  43.2 17.7 %collective-permute-start.9 = (bf16[4,2,144,128]{3,2,1,0:T(8,128)(2,1)}, bf16[4,2,144,128]{3,2,1,0:T(8,128)(2,1)S(1)}, u32[]{:S(2)}, u32[]{:S(2)}) collective-permute-start(bf16[4,2,144,128]{3,2,1,0:T(8,128)(2,1)} %get-tuple-element.90), channel_id=1, source_target_pairs={{0,1},{1,0},{2,3},{3,2},{4,5},{5,4},{6,7},{7,6},{8,9},{9,8},{10,11... | collective-permute-start | bytes 884744 | tf_op jit(solution)/shard_map/ppermute | solution.py:506
  43.9 29.0 %collective-permute-start.10 = (bf16[4,2,144,128]{3,2,1,0:T(8,128)(2,1)}, bf16[4,2,144,128]{3,2,1,0:T(8,128)(2,1)S(1)}, u32[]{:S(2)}, u32[]{:S(2)}) collective-permute-start(bf16[4,2,144,128]{3,2,1,0:T(8,128)(2,1)} %get-tuple-element.91), channel_id=1, source_target_pairs={{0,2},{1,3},{2,0},{3,1},{4,6},{5,7},{6,4},{7,5},{8,10},{9,11},{10,... | collective-permute-start | bytes 884744 | tf_op jit(solution)/shard_map/ppermute | solution.py:506
  46.9 26.7 %collective-permute-start.11 = (bf16[4,2,144,128]{3,2,1,0:T(8,128)(2,1)}, bf16[4,2,144,128]{3,2,1,0:T(8,128)(2,1)S(1)}, u32[]{:S(2)}, u32[]{:S(2)}) collective-permute-start(bf16[4,2,144,128]{3,2,1,0:T(8,128)(2,1)} %get-tuple-element.92), channel_id=1, source_target_pairs={{0,3},{1,2},{2,1},{3,0},{4,7},{5,6},{6,5},{7,4},{8,11},{9,10},{10,... | collective-permute-start | bytes 884744 | tf_op jit(solution)/shard_map/ppermute | solution.py:506
  57.2 32.4 %collective-permute-start.23 = (bf16[4,2,144,128]{3,2,1,0:T(8,128)(2,1)}, bf16[4,2,144,128]{3,2,1,0:T(8,128)(2,1)}, u32[]{:S(2)}, u32[]{:S(2)}) collective-permute-start(bf16[4,2,144,128]{3,2,1,0:T(8,128)(2,1)} %get-tuple-element.107), channel_id=1, source_target_pairs={{0,1},{1,0},{2,3},{3,2},{4,5},{5,4},{6,7},{7,6},{8,9},{9,8},{10,11... | collective-permute-start | bytes 884744 | tf_op jit(solution)/shard_map/ppermute | solution.py:506
  57.8 39.7 %collective-permute-start.24 = (bf16[4,2,144,128]{3,2,1,0:T(8,128)(2,1)}, bf16[4,2,144,128]{3,2,1,0:T(8,128)(2,1)}, u32[]{:S(2)}, u32[]{:S(2)}) collective-permute-start(bf16[4,2,144,128]{3,2,1,0:T(8,128)(2,1)} %get-tuple-element.108), channel_id=1, source_target_pairs={{0,2},{1,3},{2,0},{3,1},{4,6},{5,7},{6,4},{7,5},{8,10},{9,11},{10,... | collective-permute-start | bytes 884744 | tf_op jit(solution)/shard_map/ppermute | solution.py:506
  61.6 35.9 %collective-permute-start.25 = (bf16[4,2,144,128]{3,2,1,0:T(8,128)(2,1)}, bf16[4,2,144,128]{3,2,1,0:T(8,128)(2,1)}, u32[]{:S(2)}, u32[]{:S(2)}) collective-permute-start(bf16[4,2,144,128]{3,2,1,0:T(8,128)(2,1)} %get-tuple-element.109), channel_id=1, source_target_pairs={{0,3},{1,2},{2,1},{3,0},{4,7},{5,6},{6,5},{7,4},{8,11},{9,10},{10,... | collective-permute-start | bytes 884744 | tf_op jit(solution)/shard_map/ppermute | solution.py:506
  73.5 34.1 %collective-permute-start.19 = (bf16[2,576,128]{2,1,0:T(8,128)(2,1)}, bf16[2,576,128]{2,1,0:T(8,128)(2,1)}, u32[]{:S(2)}, u32[]{:S(2)}) collective-permute-start(bf16[2,576,128]{2,1,0:T(8,128)(2,1)} %get-tuple-element.104.last), channel_id=1, source_target_pairs={{0,4},{4,8},{8,12},{12,16},{16,20},{20,24},{24,28},{28,0},{1,5},{5... | collective-permute-start | bytes 884744 | tf_op jit(solution)/shard_map/ppermute | solution.py:614
  74.3 34.3 %collective-permute-start.20 = (bf16[2,576,128]{2,1,0:T(8,128)(2,1)}, bf16[2,576,128]{2,1,0:T(8,128)(2,1)}, u32[]{:S(2)}, u32[]{:S(2)}) collective-permute-start(bf16[2,576,128]{2,1,0:T(8,128)(2,1)} %get-tuple-element.97.refs_4_.first), channel_id=1, source_target_pairs={{0,28},{4,0},{8,4},{12,8},{16,12},{20,16},{24,20},{28,24},{1,29},{... | collective-permute-start | bytes 884744 | tf_op jit(solution)/shard_map/ppermute | solution.py:615
  89.5 46.6 %collective-permute-start.17 = (bf16[4,576,128]{2,1,0:T(8,128)(2,1)}, bf16[4,576,128]{2,1,0:T(8,128)(2,1)}, u32[]{:S(2)}, u32[]{:S(2)}) collective-permute-start(bf16[4,576,128]{2,1,0:T(8,128)(2,1)} %get-tuple-element.102.last), channel_id=1, source_target_pairs={{0,4},{4,8},{8,12},{12,16},{16,20},{20,24},{24,28},{28,0},{1,5},{5... | collective-permute-start | bytes 1769480 | tf_op jit(solution)/shard_map/ppermute | solution.py:614
  97.5 39.6 %collective-permute-start.18 = (bf16[4,576,128]{2,1,0:T(8,128)(2,1)}, bf16[4,576,128]{2,1,0:T(8,128)(2,1)}, u32[]{:S(2)}, u32[]{:S(2)}) collective-permute-start(bf16[4,576,128]{2,1,0:T(8,128)(2,1)} %get-tuple-element.103.first), channel_id=1, source_target_pairs={{0,28},{4,0},{8,4},{12,8},{16,12},{20,16},{24,20},{28,24},{1,29},{... | collective-permute-start | bytes 1769480 | tf_op jit(solution)/shard_map/ppermute | solution.py:615
  97.5 21.8 %collective-permute-start.6 = (bf16[4,2,144,128]{3,2,1,0:T(8,128)(2,1)}, bf16[4,2,144,128]{3,2,1,0:T(8,128)(2,1)}, u32[]{:S(2)}, u32[]{:S(2)}) collective-permute-start(bf16[4,2,144,128]{3,2,1,0:T(8,128)(2,1)} %get-tuple-element.87), channel_id=1, source_target_pairs={{0,1},{1,0},{2,3},{3,2},{4,5},{5,4},{6,7},{7,6},{8,9},{9,8},{10,11... | collective-permute-start | bytes 884744 | tf_op jit(solution)/shard_map/ppermute | solution.py:506
  107.7 23.7 %collective-permute-start.7 = (bf16[4,2,144,128]{3,2,1,0:T(8,128)(2,1)}, bf16[4,2,144,128]{3,2,1,0:T(8,128)(2,1)}, u32[]{:S(2)}, u32[]{:S(2)}) collective-permute-start(bf16[4,2,144,128]{3,2,1,0:T(8,128)(2,1)} %get-tuple-element.88), channel_id=1, source_target_pairs={{0,2},{1,3},{2,0},{3,1},{4,6},{5,7},{6,4},{7,5},{8,10},{9,11},{10,... | collective-permute-start | bytes 884744 | tf_op jit(solution)/shard_map/ppermute | solution.py:506
  108.6 22.8 %collective-permute-start.8 = (bf16[4,2,144,128]{3,2,1,0:T(8,128)(2,1)}, bf16[4,2,144,128]{3,2,1,0:T(8,128)(2,1)}, u32[]{:S(2)}, u32[]{:S(2)}) collective-permute-start(bf16[4,2,144,128]{3,2,1,0:T(8,128)(2,1)} %get-tuple-element.89), channel_id=1, source_target_pairs={{0,3},{1,2},{2,1},{3,0},{4,7},{5,6},{6,5},{7,4},{8,11},{9,10},{10,... | collective-permute-start | bytes 884744 | tf_op jit(solution)/shard_map/ppermute | solution.py:506
  119.3 48.8 %collective-permute-start.26 = (bf16[4,576,128]{2,1,0:T(8,128)(2,1)S(1)}, bf16[4,576,128]{2,1,0:T(8,128)(2,1)S(1)}, u32[]{:S(2)}, u32[]{:S(2)}) collective-permute-start(bf16[4,576,128]{2,1,0:T(8,128)(2,1)S(1)} %get-tuple-element.110.last), channel_id=1, source_target_pairs={{0,4},{4,8},{8,12},{12,16},{16,20},{20,24},{24,28},{28,0},{1,5},{5... | collective-permute-start | bytes 1769480 | tf_op jit(solution)/shard_map/ppermute | solution.py:614
  131.4 37.2 %collective-permute-start.27 = (bf16[4,576,128]{2,1,0:T(8,128)(2,1)S(1)}, bf16[4,576,128]{2,1,0:T(8,128)(2,1)S(1)}, u32[]{:S(2)}, u32[]{:S(2)}) collective-permute-start(bf16[4,576,128]{2,1,0:T(8,128)(2,1)S(1)} %get-tuple-element.111.first), channel_id=1, source_target_pairs={{0,28},{4,0},{8,4},{12,8},{16,12},{20,16},{24,20},{28,24},{1,29},{... | collective-permute-start | bytes 1769480 | tf_op jit(solution)/shard_map/ppermute | solution.py:615
  146.2 38.9 %collective-permute-start.21 = (bf16[4,576,128]{2,1,0:T(8,128)(2,1)}, bf16[4,576,128]{2,1,0:T(8,128)(2,1)}, u32[]{:S(2)}, u32[]{:S(2)}) collective-permute-start(bf16[4,576,128]{2,1,0:T(8,128)(2,1)} %get-tuple-element.105.last), channel_id=1, source_target_pairs={{0,4},{4,8},{8,12},{12,16},{16,20},{20,24},{24,28},{28,0},{1,5},{5... | collective-permute-start | bytes 1769480 | tf_op jit(solution)/shard_map/ppermute | solution.py:614
  146.2 40.3 %collective-permute-start.22 = (bf16[4,576,128]{2,1,0:T(8,128)(2,1)}, bf16[4,576,128]{2,1,0:T(8,128)(2,1)}, u32[]{:S(2)}, u32[]{:S(2)}) collective-permute-start(bf16[4,576,128]{2,1,0:T(8,128)(2,1)} %get-tuple-element.106.first), channel_id=1, source_target_pairs={{0,28},{4,0},{8,4},{12,8},{16,12},{20,16},{24,20},{28,24},{1,29},{... | collective-permute-start | bytes 1769480 | tf_op jit(solution)/shard_map/ppermute | solution.py:615
  164.8 15.8 %collective-permute-start.4 = (bf16[2,2,144,128]{3,2,1,0:T(8,128)(2,1)}, bf16[2,2,144,128]{3,2,1,0:T(8,128)(2,1)}, u32[]{:S(2)}, u32[]{:S(2)}) collective-permute-start(bf16[2,2,144,128]{3,2,1,0:T(8,128)(2,1)} %get-tuple-element.85), channel_id=1, source_target_pairs={{0,2},{1,3},{2,0},{3,1},{4,6},{5,7},{6,4},{7,5},{8,10},{9,11},{10,... | collective-permute-start | bytes 442376 | tf_op jit(solution)/shard_map/ppermute | solution.py:506
  168.1 15.7 %collective-permute-start.5 = (bf16[2,2,144,128]{3,2,1,0:T(8,128)(2,1)}, bf16[2,2,144,128]{3,2,1,0:T(8,128)(2,1)}, u32[]{:S(2)}, u32[]{:S(2)}) collective-permute-start(bf16[2,2,144,128]{3,2,1,0:T(8,128)(2,1)} %get-tuple-element.86), channel_id=1, source_target_pairs={{0,3},{1,2},{2,1},{3,0},{4,7},{5,6},{6,5},{7,4},{8,11},{9,10},{10,... | collective-permute-start | bytes 442376 | tf_op jit(solution)/shard_map/ppermute | solution.py:506
  177.6 21.0 %collective-permute-start.38 = (bf16[2,576,128]{2,1,0:T(8,128)(2,1)}, bf16[2,576,128]{2,1,0:T(8,128)(2,1)}, u32[]{:S(2)}, u32[]{:S(2)}) collective-permute-start(bf16[2,576,128]{2,1,0:T(8,128)(2,1)} %get-tuple-element.123.last), channel_id=1, source_target_pairs={{0,4},{4,8},{8,12},{12,16},{16,20},{20,24},{24,28},{28,0},{1,5},{5... | collective-permute-start | bytes 884744 | tf_op jit(solution)/shard_map/ppermute | solution.py:614
  (106 other events, 1186.5 us)

commit v4 on v3

--- a/solution.py
+++ b/solution.py
@@ -554,10 +554,10 @@
 
 
 def filters_after(chunk, chunks):
-    held = 2 if chunk >= chunks - 3 else 1
-    last = chunks - 1 if chunk == chunks - 1 else chunk - held
-    held = 2 if chunk - 1 >= chunks - 3 else 1
-    return range(max(chunk - 1 - held + 1, 0), last + 1)
+    ahead = chunks - 4
+    if chunk == chunks - 1:
+        return range(ahead, chunks)
+    return range(chunk - 1, chunk) if 1 <= chunk <= ahead else range(0)
 
 
 def chunk_sizes(groups):

time: 240 us -> 225 us (0.938)
  waiting for transfers between devices: 73 us -> 40.6 us
  local copies, waits for them, and re-layouts: 25.2 us -> 34 us
  starting transfers between devices: 78.1 us -> 85.7 us
    ppermute x30, waiting for transfers between devices: 56 us -> 30.6 us  [exchange(): lax.ppermute(blocks[place], 'lev', [(i, i ^ place) for i in range(count)])]
    unnamed x159 -> x181, local copies, waits for them, and re-layouts: 25.2 us -> 34 us
    ppermute x8, waiting for transfers between devices: 7.5 us -> 0.02 us  [halo(): left = lax.ppermute(last, 'lon', shift_by('lon', 1))]
    ppermute x30, starting transfers between devices: 58.3 us -> 64.1 us  [exchange(): lax.ppermute(blocks[place], 'lev', [(i, i ^ place) for i in range(count)])]
    ppermute x8, starting transfers between devices: 0.13 us -> 2.84 us  [halo(): left = lax.ppermute(last, 'lon', shift_by('lon', 1))]
    ppermute x8, starting transfers between devices: 15.2 us -> 12.7 us  [halo(): right = lax.ppermute(first, 'lon', shift_by('lon', -1))]
  transfers between devices with their start and end apart: 51 -> 51, of which waited for: 17 -> 12; matrix products, arithmetic and copies ran while one was open for 2% -> 2% of each run, Pallas kernels for 21% -> 22%
where the time goes in v4:
time: 225 us; the launch traced here: 223 us
  starting transfers between devices  85.7 us (38%)
  Pallas kernels  57.4 us (26%)
  waiting for transfers between devices  40.6 us (18%)
  local copies, waits for them, and re-layouts  34 us (15%)
  matrix products  3.4 us (2%)
    ppermute x30, starting transfers between devices, exchange(): lax.ppermute(blocks[place], 'lev', [(i, i ^ place) for i in range(count)])  64.1 us
    unnamed x181, local copies, waits for them, and re-layouts  34 us
    ppermute x30, waiting for transfers between devices, exchange(): lax.ppermute(blocks[place], 'lev', [(i, i ^ place) for i in range(count)])  30.6 us
    pallas_call x8, Pallas kernels, filtered(): pl.pallas_call(functools.partial(filter_kernel, pair, total is not None),...  22.2 us
    pallas_call x7, Pallas kernels, pack(): pl.pallas_call(functools.partial(pack_kernel, parts, halves), grid=(count...  21.7 us
    ppermute x8, starting transfers between devices, halo(): right = lax.ppermute(first, 'lon', shift_by('lon', -1))  12.7 us
    ppermute x5, waiting for transfers between devices, total_of(): x = x + lax.ppermute(x, axis, pairs)  9.94 us
    pallas_call x7, Pallas kernels, product(): pl.pallas_call(functools.partial(product_kernel, parts), grid=(count // s...  7.71 us
  transfers between devices with their start and end apart: 51, of which 12 were waited for; matrix products, arithmetic and copies ran while one was open for 2% of the time, Pallas kernels for 22%

profile of v4, /device:TPU:0, one launch (start us, length us, event | category | flops | bytes accessed | tf_op | source)
XLA Modules:
  0.0 223.2 jit_solution(2424605326202317761)
XLA Ops:
  6.3 3.1 %collective-permute-start.40 = (bf16[144,128]{1,0:T(8,128)(2,1)S(1)}, bf16[144,128]{1,0:T(8,128)(2,1)S(1)}, u32[]{:S(2)}, u32[]{:S(2)}) collective-permute-start(bf16[144,128]{1,0:T(8,128)(2,1)S(1)} %get-tuple-element.124.refs_0_), channel_id=1, source_target_pairs={{0,1},{1,0},{2,3},{3,2},{4,5},{5,4},{6,7},{7,6},{8,9},{9,8},{10,11... | collective-permute-start | bytes 110600 | tf_op jit(solution)/shard_map/ppermute | solution.py:506
  9.4 3.0 %collective-permute-start.1 = (bf16[352,128]{1,0:T(8,128)(2,1)S(1)}, bf16[352,128]{1,0:T(8,128)(2,1)S(1)}, u32[]{:S(2)}, u32[]{:S(2)}) collective-permute-start(bf16[352,128]{1,0:T(8,128)(2,1)S(1)} %get-tuple-element.79), channel_id=1, source_target_pairs={{0,2},{1,3},{2,0},{3,1},{4,6},{5,7},{6,4},{7,5},{8,10},{9,11},{10,... | collective-permute-start | bytes 270344 | tf_op jit(solution)/shard_map/ppermute | solution.py:506
  16.8 4.0 %pack.8 = (bf16[4,2,144,128]{3,2,1,0:T(8,128)(2,1)}, bf16[4,2,144,128]{3,2,1,0:T(8,128)(2,1)}, bf16[4,2,144,128]{3,2,1,0:T(8,128)(2,1)}, bf16[4,2,144,128]{3,2,1,0:T(8,128)(2,1)}) custom-call(bf16[80,18,16,128]{3,2,1,0:T(8,128)(2,1)} %ens_ref.13, bf16[352,128]{1,0:T(8,128)(2,1)} %copy-done.40), custom_call_target="tpu_custom_call" | custom-call | flops 16000000 | bytes 2359296 | tf_op jit(solution)/shard_map/pack/pallas_call | solution.py:80
  22.7 4.4 %collective-permute-done.2.refs_3_ = bf16[352,128]{1,0:T(8,128)(2,1)S(1)} collective-permute-done((bf16[352,128]{1,0:T(8,128)(2,1)S(1)}, bf16[352,128]{1,0:T(8,128)(2,1)S(1)}, u32[]{:S(2)}, u32[]{:S(2)}) %collective-permute-start.2) | collective-permute-done | bytes 90144 | tf_op jit(solution)/shard_map/ppermute | solution.py:506
  28.0 4.0 %pack.9 = (bf16[4,2,144,128]{3,2,1,0:T(8,128)(2,1)}, bf16[4,2,144,128]{3,2,1,0:T(8,128)(2,1)}, bf16[4,2,144,128]{3,2,1,0:T(8,128)(2,1)}, bf16[4,2,144,128]{3,2,1,0:T(8,128)(2,1)}) custom-call(bf16[80,18,16,128]{3,2,1,0:T(8,128)(2,1)} %ens_ref.13, bf16[4,2,144,128]{3,2,1,0:T(8,128)(2,1)} %get-tuple-element.72.after.refs_0_), custom_call_target="tpu_custom_call" | custom-call | flops 16000000 | bytes 2359296 | tf_op jit(solution)/shard_map/pack/pallas_call | solution.py:80
  32.0 4.0 %pack.10 = (bf16[4,2,144,128]{3,2,1,0:T(8,128)(2,1)}, bf16[4,2,144,128]{3,2,1,0:T(8,128)(2,1)}, bf16[4,2,144,128]{3,2,1,0:T(8,128)(2,1)}, bf16[4,2,144,128]{3,2,1,0:T(8,128)(2,1)}) custom-call(bf16[80,18,16,128]{3,2,1,0:T(8,128)(2,1)} %ens_ref.13, bf16[4,2,144,128]{3,2,1,0:T(8,128)(2,1)} %get-tuple-element.73.after.refs_0_), custom_call_target="tpu_custom_call" | custom-call | flops 16000000 | bytes 2359296 | tf_op jit(solution)/shard_map/pack/pallas_call | solution.py:80
  47.3 3.0 %collective-permute-start.24 = (bf16[4,2,144,128]{3,2,1,0:T(8,128)(2,1)}, bf16[4,2,144,128]{3,2,1,0:T(8,128)(2,1)S(1)}, u32[]{:S(2)}, u32[]{:S(2)}) collective-permute-start(bf16[4,2,144,128]{3,2,1,0:T(8,128)(2,1)} %get-tuple-element.106), channel_id=1, source_target_pairs={{0,3},{1,2},{2,1},{3,0},{4,7},{5,6},{6,5},{7,4},{8,11},{9,10},{10,... | collective-permute-start | bytes 884744 | tf_op jit(solution)/shard_map/ppermute | solution.py:506
  54.8 2.7 %collective-permute-start.13 = (bf16[4,2,144,128]{3,2,1,0:T(8,128)(2,1)}, bf16[4,2,144,128]{3,2,1,0:T(8,128)(2,1)}, u32[]{:S(2)}, u32[]{:S(2)}) collective-permute-start(bf16[4,2,144,128]{3,2,1,0:T(8,128)(2,1)} %get-tuple-element.94), channel_id=1, source_target_pairs={{0,2},{1,3},{2,0},{3,1},{4,6},{5,7},{6,4},{7,5},{8,10},{9,11},{10,... | collective-permute-start | bytes 884744 | tf_op jit(solution)/shard_map/ppermute | solution.py:506
  75.0 3.3 %collective-permute-start.35 = (bf16[4,2,144,128]{3,2,1,0:T(8,128)(2,1)}, bf16[4,2,144,128]{3,2,1,0:T(8,128)(2,1)}, u32[]{:S(2)}, u32[]{:S(2)}) collective-permute-start(bf16[4,2,144,128]{3,2,1,0:T(8,128)(2,1)} %get-tuple-element.119), channel_id=1, source_target_pairs={{0,1},{1,0},{2,3},{3,2},{4,5},{5,4},{6,7},{7,6},{8,9},{9,8},{10,11... | collective-permute-start | bytes 884744 | tf_op jit(solution)/shard_map/ppermute | solution.py:506
  78.2 6.5 %collective-permute-done.13.refs_2_ = bf16[4,2,144,128]{3,2,1,0:T(8,128)(2,1)} collective-permute-done((bf16[4,2,144,128]{3,2,1,0:T(8,128)(2,1)}, bf16[4,2,144,128]{3,2,1,0:T(8,128)(2,1)}, u32[]{:S(2)}, u32[]{:S(2)}) %collective-permute-start.13) | collective-permute-done | bytes 294944 | tf_op jit(solution)/shard_map/ppermute | solution.py:506
  89.2 13.6 %collective-permute-start.41 = (bf16[144,128]{1,0:T(8,128)(2,1)}, bf16[144,128]{1,0:T(8,128)(2,1)S(1)}, u32[]{:S(2)}, u32[]{:S(2)}) collective-permute-start(bf16[144,128]{1,0:T(8,128)(2,1)} %copy-done.63), channel_id=1, source_target_pairs={{0,2},{1,3},{2,0},{3,1},{4,6},{5,7},{6,4},{7,5},{8,10},{9,11},{10,... | collective-permute-start | bytes 110600 | tf_op jit(solution)/shard_map/ppermute | solution.py:506
  104.6 2.7 %filtered.8.refs_4_ = f32[2,576,128]{2,1,0:T(8,128)S(1)} custom-call(bf16[576,1728]{1,0:T(8,128)(2,1)S(1)} %fusion.1.matrix_ref, bf16[2,576,128]{2,1,0:T(8,128)(2,1)} %collective-permute-done.18.left, bf16[2,576,128]{2,1,0:T(8,128)(2,1)} %get-tuple-element.101.first.refs_4_, bf16[2,576,128]{2,1,0:T(8,128)(2,1)} %get-tuple-element.100.last, ...), custom_call_target="tpu_custom_call" | custom-call | flops 1019215872 | bytes 1769472 | tf_op jit(solution)/shard_map/filtered/pallas_call | solution.py:260
  114.0 7.0 %collective-permute-done.37.refs_3_ = bf16[4,2,144,128]{3,2,1,0:T(8,128)(2,1)S(1)} collective-permute-done((bf16[4,2,144,128]{3,2,1,0:T(8,128)(2,1)S(1)}, bf16[4,2,144,128]{3,2,1,0:T(8,128)(2,1)S(1)}, u32[]{:S(2)}, u32[]{:S(2)}) %collective-permute-start.37) | collective-permute-done | bytes 294944 | tf_op jit(solution)/shard_map/ppermute | solution.py:506
  122.9 4.5 %collective-permute-start.10 = (bf16[2,2,144,128]{3,2,1,0:T(8,128)(2,1)S(1)}, bf16[2,2,144,128]{3,2,1,0:T(8,128)(2,1)S(1)}, u32[]{:S(2)}, u32[]{:S(2)}) collective-permute-start(bf16[2,2,144,128]{3,2,1,0:T(8,128)(2,1)S(1)} %copy-done.87), channel_id=1, source_target_pairs={{0,2},{1,3},{2,0},{3,1},{4,6},{5,7},{6,4},{7,5},{8,10},{9,11},{10,... | collective-permute-start | bytes 442376 | tf_op jit(solution)/shard_map/ppermute | solution.py:506
  129.4 4.0 %filtered.10.refs_4_ = f32[2,576,128]{2,1,0:T(8,128)S(1)} custom-call(bf16[576,1728]{1,0:T(8,128)(2,1)S(1)} %fusion.1.matrix_ref, bf16[4,576,128]{2,1,0:T(8,128)(2,1)} %collective-permute-done.27.left, bf16[4,576,128]{2,1,0:T(8,128)(2,1)} %get-tuple-element.112.first, bf16[4,576,128]{2,1,0:T(8,128)(2,1)} %get-tuple-element.111.last, ...), custom_call_target="tpu_custom_call" | custom-call | flops 2038431744 | bytes 3538944 | tf_op jit(solution)/shard_map/filtered/pallas_call | solution.py:260
  142.3 3.9 %filtered.11.refs_4_ = f32[2,576,128]{2,1,0:T(8,128)S(1)} custom-call(bf16[576,1728]{1,0:T(8,128)(2,1)S(1)} %fusion.1.matrix_ref, bf16[4,576,128]{2,1,0:T(8,128)(2,1)S(1)} %collective-permute-done.20.left, bf16[4,576,128]{2,1,0:T(8,128)(2,1)S(1)} %get-tuple-element.103.first, bf16[4,576,128]{2,1,0:T(8,128)(2,1)S(1)} %get-tuple-element.102.last, ...), custom_call_target="tpu_custom_call" | custom-call | flops 2038431744 | bytes 3538944 | tf_op jit(solution)/shard_map/filtered/pallas_call | solution.py:260
  151.4 2.9 %collective-permute-done.8.refs_3_ = bf16[2,2,144,128]{3,2,1,0:T(8,128)(2,1)S(1)} collective-permute-done((bf16[2,2,144,128]{3,2,1,0:T(8,128)(2,1)S(1)}, bf16[2,2,144,128]{3,2,1,0:T(8,128)(2,1)S(1)}, u32[]{:S(2)}, u32[]{:S(2)}) %collective-permute-start.8) | collective-permute-done | bytes 147488 | tf_op jit(solution)/shard_map/ppermute | solution.py:506
  154.9 2.8 %collective-permute-start.4 = (bf16[2,2,144,128]{3,2,1,0:T(8,128)(2,1)}, bf16[2,2,144,128]{3,2,1,0:T(8,128)(2,1)}, u32[]{:S(2)}, u32[]{:S(2)}) collective-permute-start(bf16[2,2,144,128]{3,2,1,0:T(8,128)(2,1)} %get-tuple-element.85), channel_id=1, source_target_pairs={{0,2},{1,3},{2,0},{3,1},{4,6},{5,7},{6,4},{7,5},{8,10},{9,11},{10,... | collective-permute-start | bytes 442376 | tf_op jit(solution)/shard_map/ppermute | solution.py:506
  163.5 5.5 %collective-permute-done.4.refs_2_ = bf16[2,2,144,128]{3,2,1,0:T(8,128)(2,1)} collective-permute-done((bf16[2,2,144,128]{3,2,1,0:T(8,128)(2,1)}, bf16[2,2,144,128]{3,2,1,0:T(8,128)(2,1)}, u32[]{:S(2)}, u32[]{:S(2)}) %collective-permute-start.4) | collective-permute-done | bytes 147488 | tf_op jit(solution)/shard_map/ppermute | solution.py:506
  184.8 4.1 %filtered.12.refs_4_ = f32[2,576,128]{2,1,0:T(8,128)S(1)} custom-call(bf16[576,1728]{1,0:T(8,128)(2,1)S(1)} %fusion.1.matrix_ref, bf16[4,576,128]{2,1,0:T(8,128)(2,1)} %collective-permute-done.38.left, bf16[4,576,128]{2,1,0:T(8,128)(2,1)} %get-tuple-element.123.first, bf16[4,576,128]{2,1,0:T(8,128)(2,1)} %get-tuple-element.122.last, ...), custom_call_target="tpu_custom_call" | custom-call | flops 2038431744 | bytes 3538944 | tf_op jit(solution)/shard_map/filtered/pallas_call | solution.py:260
  198.1 3.6 %collective-permute-done.47 = f32[8,128]{1,0:T(8,128)S(1)} collective-permute-done((f32[8,128]{1,0:T(8,128)S(1)}, f32[8,128]{1,0:T(8,128)S(1)}, u32[]{:S(2)}, u32[]{:S(2)}) %collective-permute-start.47) | collective-permute-done | bytes 4128 | tf_op jit(solution)/shard_map/ppermute | solution.py:538
  201.8 3.6 %collective-permute-done.48 = f32[8,128]{1,0:T(8,128)S(1)} collective-permute-done((f32[8,128]{1,0:T(8,128)S(1)}, f32[8,128]{1,0:T(8,128)S(1)}, u32[]{:S(2)}, u32[]{:S(2)}) %collective-permute-start.48) | collective-permute-done | bytes 4128 | tf_op jit(solution)/shard_map/ppermute | solution.py:538
  205.3 3.7 %collective-permute-start.49 = (f32[8,128]{1,0:T(8,128)S(1)}, f32[8,128]{1,0:T(8,128)S(1)}, u32[]{:S(2)}, u32[]{:S(2)}) collective-permute-start(f32[8,128]{1,0:T(8,128)S(1)} %add.68), channel_id=1, source_target_pairs={{0,1},{1,0},{2,3},{3,2},{4,5},{5,4},{6,7},{7,6},{8,9},{9,8},{10,11... | collective-permute-start | bytes 12296 | tf_op jit(solution)/shard_map/ppermute | solution.py:538
  218.7 3.4 %collective-permute-done.45.refs_3_ = bf16[144,128]{1,0:T(8,128)(2,1)S(1)} collective-permute-done((bf16[144,128]{1,0:T(8,128)(2,1)S(1)}, bf16[144,128]{1,0:T(8,128)(2,1)S(1)}, u32[]{:S(2)}, u32[]{:S(2)}) %collective-permute-start.45) | collective-permute-done | bytes 36896 | tf_op jit(solution)/shard_map/ppermute | solution.py:506
  (302 shorter events, 118.5 us)
Async XLA Ops:
  12.4 34.3 %collective-permute-start.15 = (bf16[2,2,144,128]{3,2,1,0:T(8,128)(2,1)}, bf16[2,2,144,128]{3,2,1,0:T(8,128)(2,1)S(1)}, u32[]{:S(2)}, u32[]{:S(2)}) collective-permute-start(bf16[2,2,144,128]{3,2,1,0:T(8,128)(2,1)} %get-tuple-element.96), channel_id=1, source_target_pairs={{0,1},{1,0},{2,3},{3,2},{4,5},{5,4},{6,7},{7,6},{8,9},{9,8},{10,11... | collective-permute-start | bytes 442376 | tf_op jit(solution)/shard_map/ppermute | solution.py:506
  14.0 32.8 %collective-permute-start.16 = (bf16[2,2,144,128]{3,2,1,0:T(8,128)(2,1)}, bf16[2,2,144,128]{3,2,1,0:T(8,128)(2,1)S(1)}, u32[]{:S(2)}, u32[]{:S(2)}) collective-permute-start(bf16[2,2,144,128]{3,2,1,0:T(8,128)(2,1)} %get-tuple-element.97), channel_id=1, source_target_pairs={{0,2},{1,3},{2,0},{3,1},{4,6},{5,7},{6,4},{7,5},{8,10},{9,11},{10,... | collective-permute-start | bytes 442376 | tf_op jit(solution)/shard_map/ppermute | solution.py:506
  20.8 36.7 %collective-permute-start.22 = (bf16[4,2,144,128]{3,2,1,0:T(8,128)(2,1)}, bf16[4,2,144,128]{3,2,1,0:T(8,128)(2,1)S(1)}, u32[]{:S(2)}, u32[]{:S(2)}) collective-permute-start(bf16[4,2,144,128]{3,2,1,0:T(8,128)(2,1)} %get-tuple-element.104), channel_id=1, source_target_pairs={{0,1},{1,0},{2,3},{3,2},{4,5},{5,4},{6,7},{7,6},{8,9},{9,8},{10,11... | collective-permute-start | bytes 884744 | tf_op jit(solution)/shard_map/ppermute | solution.py:506
  21.5 38.8 %collective-permute-start.23 = (bf16[4,2,144,128]{3,2,1,0:T(8,128)(2,1)}, bf16[4,2,144,128]{3,2,1,0:T(8,128)(2,1)S(1)}, u32[]{:S(2)}, u32[]{:S(2)}) collective-permute-start(bf16[4,2,144,128]{3,2,1,0:T(8,128)(2,1)} %get-tuple-element.105), channel_id=1, source_target_pairs={{0,2},{1,3},{2,0},{3,1},{4,6},{5,7},{6,4},{7,5},{8,10},{9,11},{10,... | collective-permute-start | bytes 884744 | tf_op jit(solution)/shard_map/ppermute | solution.py:506
  27.1 20.2 %collective-permute-start.17 = (bf16[2,2,144,128]{3,2,1,0:T(8,128)(2,1)S(1)}, bf16[2,2,144,128]{3,2,1,0:T(8,128)(2,1)S(1)}, u32[]{:S(2)}, u32[]{:S(2)}) collective-permute-start(bf16[2,2,144,128]{3,2,1,0:T(8,128)(2,1)S(1)} %copy-done.88), channel_id=1, source_target_pairs={{0,3},{1,2},{2,1},{3,0},{4,7},{5,6},{6,5},{7,4},{8,11},{9,10},{10,... | collective-permute-start | bytes 442376 | tf_op jit(solution)/shard_map/ppermute | solution.py:506
  47.3 15.5 %collective-permute-start.24 = (bf16[4,2,144,128]{3,2,1,0:T(8,128)(2,1)}, bf16[4,2,144,128]{3,2,1,0:T(8,128)(2,1)S(1)}, u32[]{:S(2)}, u32[]{:S(2)}) collective-permute-start(bf16[4,2,144,128]{3,2,1,0:T(8,128)(2,1)} %get-tuple-element.106), channel_id=1, source_target_pairs={{0,3},{1,2},{2,1},{3,0},{4,7},{5,6},{6,5},{7,4},{8,11},{9,10},{10,... | collective-permute-start | bytes 884744 | tf_op jit(solution)/shard_map/ppermute | solution.py:506
  52.7 22.3 %collective-permute-start.12 = (bf16[4,2,144,128]{3,2,1,0:T(8,128)(2,1)}, bf16[4,2,144,128]{3,2,1,0:T(8,128)(2,1)}, u32[]{:S(2)}, u32[]{:S(2)}) collective-permute-start(bf16[4,2,144,128]{3,2,1,0:T(8,128)(2,1)} %get-tuple-element.93), channel_id=1, source_target_pairs={{0,1},{1,0},{2,3},{3,2},{4,5},{5,4},{6,7},{7,6},{8,9},{9,8},{10,11... | collective-permute-start | bytes 884744 | tf_op jit(solution)/shard_map/ppermute | solution.py:506
  54.8 30.0 %collective-permute-start.13 = (bf16[4,2,144,128]{3,2,1,0:T(8,128)(2,1)}, bf16[4,2,144,128]{3,2,1,0:T(8,128)(2,1)}, u32[]{:S(2)}, u32[]{:S(2)}) collective-permute-start(bf16[4,2,144,128]{3,2,1,0:T(8,128)(2,1)} %get-tuple-element.94), channel_id=1, source_target_pairs={{0,2},{1,3},{2,0},{3,1},{4,6},{5,7},{6,4},{7,5},{8,10},{9,11},{10,... | collective-permute-start | bytes 884744 | tf_op jit(solution)/shard_map/ppermute | solution.py:506
  58.3 26.5 %collective-permute-start.14 = (bf16[4,2,144,128]{3,2,1,0:T(8,128)(2,1)}, bf16[4,2,144,128]{3,2,1,0:T(8,128)(2,1)}, u32[]{:S(2)}, u32[]{:S(2)}) collective-permute-start(bf16[4,2,144,128]{3,2,1,0:T(8,128)(2,1)} %get-tuple-element.95), channel_id=1, source_target_pairs={{0,3},{1,2},{2,1},{3,0},{4,7},{5,6},{6,5},{7,4},{8,11},{9,10},{10,... | collective-permute-start | bytes 884744 | tf_op jit(solution)/shard_map/ppermute | solution.py:506
  61.1 23.8 %collective-permute-start.19 = (bf16[2,576,128]{2,1,0:T(8,128)(2,1)}, bf16[2,576,128]{2,1,0:T(8,128)(2,1)}, u32[]{:S(2)}, u32[]{:S(2)}) collective-permute-start(bf16[2,576,128]{2,1,0:T(8,128)(2,1)} %get-tuple-element.101.first.refs_4_), channel_id=1, source_target_pairs={{0,28},{4,0},{8,4},{12,8},{16,12},{20,16},{24,20},{28,24},{1,29},{... | collective-permute-start | bytes 884744 | tf_op jit(solution)/shard_map/ppermute | solution.py:615
  63.5 25.6 %collective-permute-start.18 = (bf16[2,576,128]{2,1,0:T(8,128)(2,1)}, bf16[2,576,128]{2,1,0:T(8,128)(2,1)}, u32[]{:S(2)}, u32[]{:S(2)}) collective-permute-start(bf16[2,576,128]{2,1,0:T(8,128)(2,1)} %get-tuple-element.100.last), channel_id=1, source_target_pairs={{0,4},{4,8},{8,12},{12,16},{16,20},{20,24},{24,28},{28,0},{1,5},{5... | collective-permute-start | bytes 884744 | tf_op jit(solution)/shard_map/ppermute | solution.py:614
  75.0 34.4 %collective-permute-start.35 = (bf16[4,2,144,128]{3,2,1,0:T(8,128)(2,1)}, bf16[4,2,144,128]{3,2,1,0:T(8,128)(2,1)}, u32[]{:S(2)}, u32[]{:S(2)}) collective-permute-start(bf16[4,2,144,128]{3,2,1,0:T(8,128)(2,1)} %get-tuple-element.119), channel_id=1, source_target_pairs={{0,1},{1,0},{2,3},{3,2},{4,5},{5,4},{6,7},{7,6},{8,9},{9,8},{10,11... | collective-permute-start | bytes 884744 | tf_op jit(solution)/shard_map/ppermute | solution.py:506
  84.8 27.2 %collective-permute-start.36 = (bf16[4,2,144,128]{3,2,1,0:T(8,128)(2,1)}, bf16[4,2,144,128]{3,2,1,0:T(8,128)(2,1)}, u32[]{:S(2)}, u32[]{:S(2)}) collective-permute-start(bf16[4,2,144,128]{3,2,1,0:T(8,128)(2,1)} %get-tuple-element.120), channel_id=1, source_target_pairs={{0,2},{1,3},{2,0},{3,1},{4,6},{5,7},{6,4},{7,5},{8,10},{9,11},{10,... | collective-permute-start | bytes 884744 | tf_op jit(solution)/shard_map/ppermute | solution.py:506
  84.8 38.2 %collective-permute-start.27 = (bf16[4,576,128]{2,1,0:T(8,128)(2,1)}, bf16[4,576,128]{2,1,0:T(8,128)(2,1)}, u32[]{:S(2)}, u32[]{:S(2)}) collective-permute-start(bf16[4,576,128]{2,1,0:T(8,128)(2,1)} %get-tuple-element.111.last), channel_id=1, source_target_pairs={{0,4},{4,8},{8,12},{12,16},{16,20},{20,24},{24,28},{28,0},{1,5},{5... | collective-permute-start | bytes 1769480 | tf_op jit(solution)/shard_map/ppermute | solution.py:614
  84.8 42.6 %collective-permute-start.28 = (bf16[4,576,128]{2,1,0:T(8,128)(2,1)}, bf16[4,576,128]{2,1,0:T(8,128)(2,1)}, u32[]{:S(2)}, u32[]{:S(2)}) collective-permute-start(bf16[4,576,128]{2,1,0:T(8,128)(2,1)} %get-tuple-element.112.first), channel_id=1, source_target_pairs={{0,28},{4,0},{8,4},{12,8},{16,12},{20,16},{24,20},{28,24},{1,29},{... | collective-permute-start | bytes 1769480 | tf_op jit(solution)/shard_map/ppermute | solution.py:615
  89.2 19.6 %collective-permute-start.41 = (bf16[144,128]{1,0:T(8,128)(2,1)}, bf16[144,128]{1,0:T(8,128)(2,1)S(1)}, u32[]{:S(2)}, u32[]{:S(2)}) collective-permute-start(bf16[144,128]{1,0:T(8,128)(2,1)} %copy-done.63), channel_id=1, source_target_pairs={{0,2},{1,3},{2,0},{3,1},{4,6},{5,7},{6,4},{7,5},{8,10},{9,11},{10,... | collective-permute-start | bytes 110600 | tf_op jit(solution)/shard_map/ppermute | solution.py:506
  109.4 30.3 %collective-permute-start.20 = (bf16[4,576,128]{2,1,0:T(8,128)(2,1)S(1)}, bf16[4,576,128]{2,1,0:T(8,128)(2,1)S(1)}, u32[]{:S(2)}, u32[]{:S(2)}) collective-permute-start(bf16[4,576,128]{2,1,0:T(8,128)(2,1)S(1)} %get-tuple-element.102.last), channel_id=1, source_target_pairs={{0,4},{4,8},{8,12},{12,16},{16,20},{20,24},{24,28},{28,0},{1,5},{5... | collective-permute-start | bytes 1769480 | tf_op jit(solution)/shard_map/ppermute | solution.py:614
  109.4 30.3 %collective-permute-start.21 = (bf16[4,576,128]{2,1,0:T(8,128)(2,1)S(1)}, bf16[4,576,128]{2,1,0:T(8,128)(2,1)S(1)}, u32[]{:S(2)}, u32[]{:S(2)}) collective-permute-start(bf16[4,576,128]{2,1,0:T(8,128)(2,1)S(1)} %get-tuple-element.103.first), channel_id=1, source_target_pairs={{0,28},{4,0},{8,4},{12,8},{16,12},{20,16},{24,20},{28,24},{1,29},{... | collective-permute-start | bytes 1769480 | tf_op jit(solution)/shard_map/ppermute | solution.py:615
  139.7 39.4 %collective-permute-start.38 = (bf16[4,576,128]{2,1,0:T(8,128)(2,1)}, bf16[4,576,128]{2,1,0:T(8,128)(2,1)}, u32[]{:S(2)}, u32[]{:S(2)}) collective-permute-start(bf16[4,576,128]{2,1,0:T(8,128)(2,1)} %get-tuple-element.122.last), channel_id=1, source_target_pairs={{0,4},{4,8},{8,12},{12,16},{16,20},{20,24},{24,28},{28,0},{1,5},{5... | collective-permute-start | bytes 1769480 | tf_op jit(solution)/shard_map/ppermute | solution.py:614
  139.7 39.5 %collective-permute-start.39 = (bf16[4,576,128]{2,1,0:T(8,128)(2,1)}, bf16[4,576,128]{2,1,0:T(8,128)(2,1)}, u32[]{:S(2)}, u32[]{:S(2)}) collective-permute-start(bf16[4,576,128]{2,1,0:T(8,128)(2,1)} %get-tuple-element.123.first), channel_id=1, source_target_pairs={{0,28},{4,0},{8,4},{12,8},{16,12},{20,16},{24,20},{28,24},{1,29},{... | collective-permute-start | bytes 1769480 | tf_op jit(solution)/shard_map/ppermute | solution.py:615
  150.2 19.4 %collective-permute-start.33 = (bf16[2,576,128]{2,1,0:T(8,128)(2,1)}, bf16[2,576,128]{2,1,0:T(8,128)(2,1)}, u32[]{:S(2)}, u32[]{:S(2)}) collective-permute-start(bf16[2,576,128]{2,1,0:T(8,128)(2,1)} %get-tuple-element.118.last), channel_id=1, source_target_pairs={{0,4},{4,8},{8,12},{12,16},{16,20},{20,24},{24,28},{28,0},{1,5},{5... | collective-permute-start | bytes 884744 | tf_op jit(solution)/shard_map/ppermute | solution.py:614
  169.1 19.9 %collective-permute-start.34 = (bf16[2,576,128]{2,1,0:T(8,128)(2,1)}, bf16[2,576,128]{2,1,0:T(8,128)(2,1)S(1)}, u32[]{:S(2)}, u32[]{:S(2)}) collective-permute-start(bf16[2,576,128]{2,1,0:T(8,128)(2,1)} %get-tuple-element.113.refs_4_.first), channel_id=1, source_target_pairs={{0,28},{4,0},{8,4},{12,8},{16,12},{20,16},{24,20},{28,24},{1,29},{... | collective-permute-start | bytes 884744 | tf_op jit(solution)/shard_map/ppermute | solution.py:615
  169.1 22.6 %collective-permute-start.31 = (bf16[2,576,128]{2,1,0:T(8,128)(2,1)S(1)}, bf16[2,576,128]{2,1,0:T(8,128)(2,1)S(1)}, u32[]{:S(2)}, u32[]{:S(2)}) collective-permute-start(bf16[2,576,128]{2,1,0:T(8,128)(2,1)S(1)} %get-tuple-element.117.last), channel_id=1, source_target_pairs={{0,4},{4,8},{8,12},{12,16},{16,20},{20,24},{24,28},{28,0},{1,5},{5... | collective-permute-start | bytes 884744 | tf_op jit(solution)/shard_map/ppermute | solution.py:614
  169.6 22.1 %collective-permute-start.32 = (bf16[2,576,128]{2,1,0:T(8,128)(2,1)S(1)}, bf16[2,576,128]{2,1,0:T(8,128)(2,1)S(1)}, u32[]{:S(2)}, u32[]{:S(2)}) collective-permute-start(bf16[2,576,128]{2,1,0:T(8,128)(2,1)S(1)} %get-tuple-element.114.refs_4_.first), channel_id=1, source_target_pairs={{0,28},{4,0},{8,4},{12,8},{16,12},{20,16},{24,20},{28,24},{1,29},{... | collective-permute-start | bytes 884744 | tf_op jit(solution)/shard_map/ppermute | solution.py:615
  (117 other events, 927.1 us)
